TPU v7x, 32 devices: a whole 2x2x4 slice. The times are simulated.
32 devices in a mesh: row: 8 (over y, x, core), col: 4 (over z).
Axes of the slice: x: 2, y: 2, z: 4, core: 2. Of those that a mesh axis runs over, the one named last changes fastest.
Arguments:
- tensor: float32 [128, 128, 768], P('row', 'col'), may hold values from -6 to 6
- start_one: float32 [128, 64], P('row'), may hold values from -0.5 to 0.5
- start_two: float32 [128, 64], P('col'), may hold values from -0.5 to 0.5
- start_three: float32 [768, 64], replicated, may hold values from -0.21875 to 0.21875
Outputs:
- factor_one: float32 [128, 64], replicated
- factor_two: float32 [128, 64], replicated
- factor_three: float32 [768, 64], replicated
- core: float32 [64, 64, 64], P(None, 'row', 'col')
All inputs are finite; a program needn't handle non-finite values.
Results may differ from a plain program's by a relative error of at most 0.0003.
Values sent between devices are 32-bit elements; how exact they have to be, the bound alone decides.
No kernel may reach another device: no remote copies, remote signals or barrier semaphores. Data moves between devices by JAX's collectives and lax.ppermute only.
A program may use at most 64 MiB of HBM per device.

v0:
```python
import math

import jax
import jax.numpy as jnp
from jax import lax
from jax.sharding import PartitionSpec as P

STEPS = 4


HIGHEST = lax.Precision.HIGHEST


def product(left, right):
    return jnp.dot(left, right, precision=HIGHEST, preferred_element_type=jnp.float32)


def left_product(left, right):
    return lax.dot_general(
        left, right, (((0,), (0,)), ((), ())), precision=HIGHEST, preferred_element_type=jnp.float32
    )


def right_product(left, right):
    return lax.dot_general(
        left, right, (((1,), (1,)), ((), ())), precision=HIGHEST, preferred_element_type=jnp.float32
    )


def cross_product(left, right):
    return lax.dot_general(
        left, right, (((0,), (1,)), ((), ())), precision=HIGHEST, preferred_element_type=jnp.float32
    )


def orthonormal(matrix, inner):
    lower = jnp.linalg.cholesky(inner)
    return jax.scipy.linalg.solve_triangular(lower, matrix.T, lower=True).T


def pairing(local, block_rows):
    return right_product(local, block_rows)


def settle(gram_whole, basis):
    for iteration in range(STEPS):
        image = product(gram_whole, basis)
        basis = orthonormal(image, left_product(image, image))
    return basis


def on_device(tensor, start_one, start_two, start_three):
    rows_one, rows_two, depth = tensor.shape
    rank = start_three.shape[1]
    flat = tensor.reshape(rows_one * rows_two, depth)
    contracted = cross_product(start_three, flat).reshape(rank, rows_one, rows_two)
    part_one = jnp.einsum("cij,jb->ibc", contracted, start_two, precision=HIGHEST).reshape(
        rows_one, rank * rank
    )
    slab_one = lax.psum_scatter(part_one, "col", scatter_dimension=1, tiled=True)
    slab_rows_one = lax.all_gather(slab_one, "row", axis=0, tiled=True)
    gram_one = lax.psum(right_product(slab_rows_one, slab_rows_one), "col")
    basis_one = settle(gram_one, lax.all_gather(start_one, "row", axis=0, tiled=True))
    own_one = lax.dynamic_slice_in_dim(basis_one, lax.axis_index("row") * rows_one, rows_one, 0)
    part_two = jnp.einsum("cij,ia->jac", contracted, own_one, precision=HIGHEST).reshape(
        rows_two, rank * rank
    )
    slab_two = lax.psum_scatter(part_two, "row", scatter_dimension=1, tiled=True)
    slab_rows_two = lax.all_gather(slab_two, "col", axis=0, tiled=True)
    gram_two = lax.psum(right_product(slab_rows_two, slab_rows_two), "row")
    basis_two = settle(gram_two, lax.all_gather(start_two, "col", axis=0, tiled=True))
    own_two = lax.dynamic_slice_in_dim(basis_two, lax.axis_index("col") * rows_two, rows_two, 0)
    received = lax.all_to_all(tensor, "row", split_axis=2, concat_axis=0, tiled=True)
    count, items, cells = received.shape
    merged = left_product(basis_one, received.reshape(count, items * cells))
    mixed = merged.reshape(rank, items, cells)
    part_three = jnp.einsum("ajk,jb->kba", mixed, own_two, precision=HIGHEST)
    cells_here = part_three.shape[0]
    slab_three = lax.psum_scatter(
        part_three.reshape(cells_here, rank * rank), "col", scatter_dimension=1, tiled=True
    )
    gram_part_three = pairing(slab_three, lax.all_gather(slab_three, "row", axis=0, tiled=True))
    gram_three = lax.psum(gram_part_three, "col")
    basis_three = start_three
    own_three = start_three
    for iteration in range(STEPS):
        image = product(gram_three, basis_three)
        inner = lax.psum(left_product(image, image), "row")
        own_three = orthonormal(image, inner)
        basis_three = lax.all_gather(own_three, "row", axis=0, tiled=True)
    core_part = left_product(own_three, slab_three)
    core_part = core_part.reshape(rank, core_part.shape[1] // rank, rank)
    core = lax.psum_scatter(core_part, "row", scatter_dimension=2, tiled=True).transpose(0, 2, 1)
    factor_one = basis_one * math.sqrt(basis_one.shape[0])
    factor_two = basis_two * math.sqrt(basis_two.shape[0])
    factor_three = basis_three * math.sqrt(basis_three.shape[0])
    return (factor_one, factor_two, factor_three, core)


def solution(mesh):
    return jax.shard_map(
        on_device,
        mesh=mesh,
        in_specs=(P("row", "col", None), P("row", None), P("col", None), P()),
        out_specs=(P(), P(), P(), P(None, "row", "col")),
        check_vma=False,
    )
```

profile of v0, /device:TPU:0, one launch (start us, length us, event | category | flops | bytes accessed | tf_op | source)
XLA Modules:
  0.0 638.1 jit_solution(973068163309146630)
XLA Ops:
  13.1 22.8 %reduce-scatter.5.cloned.1.call-done = f32[16,1024]{1,0:T(8,128)} async-done(((f32[16,4096]{1,0:T(8,128)}), f32[16,1024]{1,0:T(8,128)}) %reduce-scatter.5.cloned.1.call-update) | async-done | bytes 65552 | tf_op jit(solution)/shard_map/reduce_scatter | solution.py:60
  35.9 10.1 %all_gather.27 = f32[128,1024]{1,0:T(8,128)S(1)} all-gather(f32[16,1024]{1,0:T(8,128)} %reduce-scatter.5.cloned.1.call-done), channel_id=1, replica_groups=mesh['row'=8,'col'=4] {'row'}, dimensions={0}, use_global_device_ids=true | all-gather | bytes 589824 | tf_op jit(solution)/shard_map/all_gather | solution.py:61
  47.2 5.0 copy.67
  52.3 7.6 %reshape.61 = f32[8,1,49152]{2,1,0:T(1,128)} reshape(f32[768,16,32]{2,1,0:T(8,128)} %bitcast.262) | data formatting | bytes 3145728
  63.7 24.3 %all_gather.28 = f32[128,64]{1,0:T(8,128)S(1)} all-gather(f32[16,64]{1,0:T(8,128)S(1)} %copy-done.7), channel_id=1, replica_groups=mesh['row'=8,'col'=4] {'row'}, dimensions={0}, use_global_device_ids=true | all-gather | bytes 36864 | tf_op jit(solution)/shard_map/all_gather | solution.py:63
  89.5 5.8 cholesky.194
  96.7 4.9 custom-call.18
  103.2 5.8 cholesky.205
  110.4 4.9 custom-call.19
  116.9 5.8 cholesky.216
  124.1 4.9 custom-call.20
  129.8 5.8 cholesky.227
  137.0 4.9 custom-call.21
  144.4 13.1 %all_gather.30 = f32[128,64]{1,0:T(8,128)S(1)} all-gather(f32[32,64]{1,0:T(8,128)S(1)} %copy-done.6), channel_id=1, replica_groups=mesh['row'=8,'col'=4] {'col'}, dimensions={0}, use_global_device_ids=true | all-gather | bytes 40960 | tf_op jit(solution)/shard_map/all_gather | solution.py:71
  157.6 18.4 %reduce-scatter.7.cloned.1.call-done = f32[32,512]{1,0:T(8,128)} async-done(((f32[32,4096]{1,0:T(8,128)}), f32[32,512]{1,0:T(8,128)}) %reduce-scatter.7.cloned.1.call-update) | async-done | bytes 65552 | tf_op jit(solution)/shard_map/reduce_scatter | solution.py:68
  176.0 14.0 %all_gather.29 = f32[128,512]{1,0:T(8,128)S(1)} all-gather(f32[32,512]{1,0:T(8,128)} %reduce-scatter.7.cloned.1.call-done), channel_id=1, replica_groups=mesh['row'=8,'col'=4] {'col'}, dimensions={0}, use_global_device_ids=true | all-gather | bytes 327680 | tf_op jit(solution)/shard_map/all_gather | solution.py:69
  196.2 4.7 reshape.62
  200.9 5.2 copy.68
  213.9 31.0 %all-reduce.6.cloned.1.call-done = f32[128,128]{1,0:T(8,128)} async-done(((f32[128,128]{1,0:T(8,128)}), f32[128,128]{1,0:T(8,128)}) %all-reduce.6.cloned.1.call-update) | async-done | bytes 65552 | tf_op jit(solution)/shard_map/psum | solution.py:70
  246.4 5.8 cholesky.238
  253.6 4.9 custom-call.22
  260.1 5.8 cholesky.249
  267.3 4.9 custom-call.23
  273.9 5.8 cholesky.260
  281.0 4.9 custom-call.24
  286.7 5.8 cholesky.271
  293.9 5.0 custom-call.25
  304.2 43.1 %reduce-scatter.9.cloned.1.call-done = f32[96,1024]{0,1:T(8,128)} async-done(((f32[96,4096]{0,1:T(8,128)}), f32[96,1024]{0,1:T(8,128)}) %reduce-scatter.9.cloned.1.call-update) | async-done | bytes 393232 | tf_op jit(solution)/shard_map/reduce_scatter | solution.py:79
  349.4 31.5 %all-gather.6.cloned.1.call-done = f32[768,1024]{1,0:T(8,128)} async-done(((f32[96,1024]{1,0:T(8,128)}), f32[768,1024]{1,0:T(8,128)}) %all-gather.6.cloned.1.call-update) | async-done | bytes 3145744 | tf_op jit(solution)/shard_map/all_gather | solution.py:82
  380.9 5.3 fusion.94
  386.9 35.4 %all-reduce.8.cloned.1.call-done = f32[96,768]{1,0:T(8,128)} async-done(((f32[96,768]{1,0:T(8,128)}), f32[96,768]{1,0:T(8,128)}) %all-reduce.8.cloned.1.call-update) | async-done | bytes 294928 | tf_op jit(solution)/shard_map/psum | solution.py:83
  424.0 22.4 %psum.52 = f32[64,64]{0,1:T(8,128)S(1)} all-reduce(f32[64,64]{0,1:T(8,128)S(1)} %fusion.96), channel_id=1, replica_groups=mesh['row'=8,'col'=4] {'row'}, use_global_device_ids=true, to_apply=%region_8.11 | all-reduce | flops 4096 | bytes 32768 | tf_op jit(solution)/shard_map/psum | solution.py:88
  446.4 5.8 cholesky.282
  453.6 4.9 custom-call.26
  458.8 9.3 %all-gather = f32[8,96,64]{1,2,0:T(8,128)S(1)} all-gather(f32[1,96,64]{1,2,0:T(8,128)S(1)} %convolution_bitcast_fusion.5), channel_id=1, replica_groups=mesh['row'=8,'col'=4] {'row'}, dimensions={0}, use_global_device_ids=true | all-gather | bytes 221184 | tf_op jit(solution)/shard_map/all_gather | solution.py:90
  469.0 23.9 %psum.53 = f32[64,64]{0,1:T(8,128)S(1)} all-reduce(f32[64,64]{0,1:T(8,128)S(1)} %fusion.98), channel_id=1, replica_groups=mesh['row'=8,'col'=4] {'row'}, use_global_device_ids=true, to_apply=%region_9.0 | all-reduce | flops 4096 | bytes 32768 | tf_op jit(solution)/shard_map/psum | solution.py:88
  493.0 5.8 cholesky.293
  500.2 4.9 custom-call.27
  505.3 8.3 %all-gather.1 = f32[8,96,64]{1,2,0:T(8,128)S(1)} all-gather(f32[1,96,64]{1,2,0:T(8,128)S(1)} %convolution_bitcast_fusion.4), channel_id=1, replica_groups=mesh['row'=8,'col'=4] {'row'}, dimensions={0}, use_global_device_ids=true | all-gather | bytes 221184 | tf_op jit(solution)/shard_map/all_gather | solution.py:90
  514.6 23.6 %psum.54 = f32[64,64]{0,1:T(8,128)S(1)} all-reduce(f32[64,64]{0,1:T(8,128)S(1)} %fusion.100), channel_id=1, replica_groups=mesh['row'=8,'col'=4] {'row'}, use_global_device_ids=true, to_apply=%region_10.0 | all-reduce | flops 4096 | bytes 32768 | tf_op jit(solution)/shard_map/psum | solution.py:88
  538.3 5.8 cholesky.304
  545.5 4.9 custom-call.28
  550.6 9.3 %all-gather.2 = f32[8,96,64]{1,2,0:T(8,128)S(1)} all-gather(f32[1,96,64]{1,2,0:T(8,128)S(1)} %convolution_bitcast_fusion.3), channel_id=1, replica_groups=mesh['row'=8,'col'=4] {'row'}, dimensions={0}, use_global_device_ids=true | all-gather | bytes 221184 | tf_op jit(solution)/shard_map/all_gather | solution.py:90
  560.8 23.6 %psum.55 = f32[64,64]{0,1:T(8,128)S(1)} all-reduce(f32[64,64]{0,1:T(8,128)S(1)} %fusion.102), channel_id=1, replica_groups=mesh['row'=8,'col'=4] {'row'}, use_global_device_ids=true, to_apply=%region_11.15 | all-reduce | flops 4096 | bytes 32768 | tf_op jit(solution)/shard_map/psum | solution.py:88
  584.5 5.8 cholesky.315
  591.7 4.9 custom-call.29
  599.4 8.3 %all-gather.3 = f32[8,96,64]{1,2,0:T(8,128)S(1)} all-gather(f32[1,96,64]{1,2,0:T(8,128)S(1)} %bitcast.267), channel_id=1, replica_groups=mesh['row'=8,'col'=4] {'row'}, dimensions={0}, use_global_device_ids=true | all-gather | bytes 221184 | tf_op jit(solution)/shard_map/all_gather | solution.py:90
  608.7 22.2 %reduce-scatter.11.cloned.1.call-done = f32[64,16,8]{0,1,2:T(8,128)} async-done(((f32[64,16,64]{0,1,2:T(8,128)}), f32[64,16,8]{0,1,2:T(8,128)}) %reduce-scatter.11.cloned.1.call-update) | async-done | bytes 32784 | tf_op jit(solution)/shard_map/reduce_scatter | solution.py:93
  (161 shorter events, 71.1 us)
Async XLA Ops:
  7.2 0.9 copy-start
  7.2 3.7 copy-start.6
  7.2 28.7 %reduce-scatter.5.cloned.1.call-start = ((), (), s32[]{:S(2)}) async-start(), calls=%async_computation.5 | async-start | bytes 327680 | tf_op jit(solution)/shard_map/reduce_scatter | solution.py:60
  12.1 35.1 %copy-start.1 = (f32[16,32,768]{2,1,0:T(8,128)S(1)}, f32[16,32,768]{2,1,0:T(8,128)}, u32[]{:S(2)}) copy-start(f32[16,32,768]{2,1,0:T(8,128)} %param.9) | copy-start | bytes 4718596
  13.0 75.0 %all-reduce.4.cloned.1.call-start = ((), (), s32[]{:S(2)}) async-start(), calls=%async_computation.6 | async-start | bytes 131072 | tf_op jit(solution)/shard_map/psum | solution.py:62
  59.9 3.8 copy-start.7
  59.9 131.4 %all-to-all-start = ((f32[8,1,49152]{2,1,0:T(1,128)}), f32[8,1,49152]{2,1,0:T(1,128)S(1)}, u32[]{:S(2)}, u32[]{:S(2)}) async-start(f32[8,1,49152]{2,1,0:T(1,128)} %reshape.61), calls=%async_computation.2 | async-start | bytes 3145728 | tf_op jit(solution)/shard_map/all_to_all | solution.py:73
  63.6 112.3 %reduce-scatter.7.cloned.1.call-start = ((), (), s32[]{:S(2)}) async-start(), calls=%async_computation.7 | async-start | bytes 589824 | tf_op jit(solution)/shard_map/reduce_scatter | solution.py:68
  88.0 41.2 %copy-start.4 = (f32[128,128]{1,0:T(8,128)S(1)}, f32[128,128]{1,0:T(8,128)}, u32[]{:S(2)}) copy-start(f32[128,128]{1,0:T(8,128)} %all-reduce.4.cloned.1.call-done) | copy-start | bytes 196612
  144.4 100.6 %all-reduce.6.cloned.1.call-start = ((), (), s32[]{:S(2)}) async-start(), calls=%async_computation.8 | async-start | bytes 131072 | tf_op jit(solution)/shard_map/psum | solution.py:70
  191.0 156.3 %reduce-scatter.9.cloned.1.call-start = ((), (), s32[]{:S(2)}) async-start(), calls=%async_computation.9 | async-start | bytes 2621440 | tf_op jit(solution)/shard_map/reduce_scatter | solution.py:79
  245.0 41.2 %copy-start.5 = (f32[128,128]{1,0:T(8,128)S(1)}, f32[128,128]{1,0:T(8,128)}, u32[]{:S(2)}) copy-start(f32[128,128]{1,0:T(8,128)} %all-reduce.6.cloned.1.call-done) | copy-start | bytes 196612
  304.1 76.8 %all-gather.6.cloned.1.call-start = ((), (), s32[]{:S(2)}) async-start(), calls=%async_computation.10 | async-start | bytes 3538944 | tf_op jit(solution)/shard_map/all_gather | solution.py:82
  347.3 33.6 %copy-start.2 = (f32[96,1024]{0,1:T(8,128)S(1)}, f32[96,1024]{0,1:T(8,128)}, u32[]{:S(2)}) copy-start(f32[96,1024]{0,1:T(8,128)} %reduce-scatter.9.cloned.1.call-done) | copy-start | bytes 1179652
  349.4 72.9 %all-reduce.8.cloned.1.call-start = ((), (), s32[]{:S(2)}) async-start(), calls=%async_computation.11 | async-start | bytes 589824 | tf_op jit(solution)/shard_map/psum | solution.py:83
  386.2 244.8 %reduce-scatter.11.cloned.1.call-start = ((), (), s32[]{:S(2)}) async-start(), calls=%async_computation.12 | async-start | bytes 589824 | tf_op jit(solution)/shard_map/reduce_scatter | solution.py:93
  422.3 46.0 %copy-start.3 = (f32[96,768]{1,0:T(8,128)S(1)}, f32[96,768]{1,0:T(8,128)}, u32[]{:S(2)}) copy-start(f32[96,768]{1,0:T(8,128)} %all-reduce.8.cloned.1.call-done) | copy-start | bytes 884740
Sparse Core Ops, SparseCore 0:
  13.2 22.7 reduce-scatter.4
  47.4 31.5 all-reduce.3
  144.5 31.4 reduce-scatter.6
  191.2 53.7 all-reduce.5
  304.3 43.0 reduce-scatter.8
  349.5 31.3 all-gather.5
  386.4 35.9 all-reduce.7
  598.9 32.0 reduce-scatter.10
where the time goes:
time: 644 us; the launch traced here: 638 us
  waiting for transfers between devices  205 us (32%)
  blocking collectives  190 us (30%)
  other arithmetic  151 us (23%)
  local copies, waits for them, and re-layouts  39.1 us (6%)
  matrix products  33.9 us (5%)
  between operations  15.1 us (2%)
    psum x4, blocking collectives, on_device(): inner = lax.psum(left_product(image, image), 'row')  93.5 us
    another operation x36, other arithmetic, orthonormal(): lower = jnp.linalg.cholesky(inner)  78.2 us
    another operation x24, other arithmetic, orthonormal(): return jax.scipy.linalg.solve_triangular(lower, matrix.T, lower=True).T  66.7 us
    reduce_scatter x1, waiting for transfers between devices, on_device(): lax.psum_scatter(part_three.reshape(cells_here, rank * rank), 'col', scat...  43.1 us
    psum x1, waiting for transfers between devices, on_device(): gram_three = lax.psum(gram_part_three, 'col')  35.4 us
    all_gather x4, blocking collectives, on_device(): basis_three = lax.all_gather(own_three, 'row', axis=0, tiled=True)  35.2 us
    all_gather x1, waiting for transfers between devices, on_device(): lax.all_gather(slab_three, 'row', axis=0, tiled=True)  31.5 us
    psum x1, waiting for transfers between devices, on_device(): gram_two = lax.psum(right_product(slab_rows_two, slab_rows_two), 'row')  31 us
  transfers between devices with their start and end apart: 9, of which 7 were waited for; matrix products, arithmetic and copies ran while one was open for 15% of the time, Pallas kernels for 0%

commit v1 on v0

--- a/solution.py
+++ b/solution.py
@@ -3,10 +3,15 @@
 import jax
 import jax.numpy as jnp
 from jax import lax
+from jax.experimental import pallas as pl
+from jax.experimental.pallas import tpu as pltpu
 from jax.sharding import PartitionSpec as P
 
 STEPS = 4
-
+PANEL = 8
+BLOCK = 128
+WIDE = 256
+AXES = ("row", "col")
 
 HIGHEST = lax.Precision.HIGHEST
 
@@ -42,14 +47,53 @@
     return right_product(local, block_rows)
 
 
+def spread(row, like):
+    return jnp.broadcast_to(row, like.shape)
+
+
+def lower_inverse(inner):
+    size = inner.shape[0]
+    eye = (
+        lax.broadcasted_iota(jnp.int32, (size, size), 0) == lax.broadcasted_iota(jnp.int32, (size, size), 1)
+    ).astype(jnp.float32)
+    whole = jnp.concatenate([inner, eye], axis=1)
+    panels = size // PANEL
+    work = [whole[p * PANEL : (p + 1) * PANEL] for p in range(panels)]
+    sub = lax.broadcasted_iota(jnp.int32, work[0].shape, 0)
+    out = []
+    for p in range(panels):
+        cols = {
+            i: [spread(work[i][:, p * PANEL + k : p * PANEL + k + 1], work[i]) for k in range(PANEL)]
+            for i in range(p, panels)
+        }
+        scale = jnp.zeros_like(work[p])
+        for k in range(PANEL):
+            row = spread(work[p][k : k + 1], work[p])
+            pivot = spread(cols[p][k][k : k + 1], work[p])
+            scale = jnp.where(sub == k, lax.rsqrt(pivot), scale)
+            recip = 1.0 / pivot
+            across = [spread(cols[p][m][k : k + 1], work[p]) * recip for m in range(k + 1, PANEL)]
+            row = row * recip
+            for i in range(p, panels):
+                factor = cols[i][k]
+                if i == p:
+                    factor = jnp.where(sub > k, factor, 0.0)
+                work[i] = work[i] - factor * row
+                for m in range(k + 1, PANEL):
+                    cols[i][m] = cols[i][m] - factor * across[m - k - 1]
+        out.append((work[p] * scale)[:, size:])
+    return jnp.concatenate(out, axis=0)
+
+
+def settle_kernel(gram_ref, start_ref, out_ref):
+    out_ref[...] = iterate(gram_ref[...], start_ref[...])
+
+
 def settle(gram_whole, basis):
-    for iteration in range(STEPS):
-        image = product(gram_whole, basis)
-        basis = orthonormal(image, left_product(image, image))
-    return basis
-
-
-def on_device(tensor, start_one, start_two, start_three):
+    return call(settle_kernel, "settle", [basis.shape], gram_whole, basis)[0]
+
+
+def general(tensor, start_one, start_two, start_three):
     rows_one, rows_two, depth = tensor.shape
     rank = start_three.shape[1]
     flat = tensor.reshape(rows_one * rows_two, depth)
@@ -97,6 +141,216 @@
     return (factor_one, factor_two, factor_three, core)
 
 
+VMEM = pl.BlockSpec(memory_space=pltpu.VMEM)
+
+
+def call(kernel, name, outs, *args):
+    return pl.pallas_call(
+        kernel,
+        out_shape=[jax.ShapeDtypeStruct(shape, jnp.float32) for shape in outs],
+        in_specs=[VMEM] * len(args),
+        out_specs=[VMEM] * len(outs),
+        name=name,
+    )(*args)
+
+
+def iterate(gram, start):
+    size = start.shape[0]
+    extra = -size % WIDE
+    gram = jnp.pad(gram, ((0, extra), (0, extra)))
+
+    def step(_, turned):
+        image = product(turned, gram)
+        return product(lower_inverse(right_product(image, image)), image)
+
+    return lax.fori_loop(0, STEPS, step, jnp.pad(start.T, ((0, 0), (0, extra))))[:, :size].T
+
+
+def gram_of(slabs):
+    total = right_product(slabs[0], slabs[0])
+    for slab in slabs[1:]:
+        total = total + right_product(slab, slab)
+    return total
+
+
+def open_kernel(cont_ref, start_ref, gram_ref):
+    slabs = [product(cont_ref[c], start_ref[...]) for c in range(cont_ref.shape[0])]
+    gram_ref[...] = gram_of(slabs)
+
+
+def first_kernel(gram_ref, start_ref, cont_ref, basis_ref, factor_ref, next_ref):
+    basis = iterate(gram_ref[...], start_ref[...])
+    basis_ref[...] = basis
+    factor_ref[...] = basis * math.sqrt(basis.shape[0])
+    slabs = [left_product(cont_ref[c], basis) for c in range(cont_ref.shape[0])]
+    next_ref[...] = gram_of(slabs)
+
+
+def second_kernel(gram_ref, start_ref, factor_ref):
+    basis = iterate(gram_ref[...], start_ref[...])
+    factor_ref[...] = basis
+
+
+def slab_kernel(left_ref, right_ref, tensor_ref, factor_ref, slab_ref):
+    right = right_ref[...]
+    factor_ref[...] = right * math.sqrt(right.shape[0])
+    count, rows, cols = tensor_ref.shape
+    half = product(tensor_ref[...].reshape(count * rows, cols), right)
+    for k in range(count):
+        slab_ref[k] = left_product(left_ref[...], half[k * rows : (k + 1) * rows])
+
+
+def pairs(blocks):
+    return [(i, j) for i in range(blocks) for j in range(i, blocks)]
+
+
+def pair_kernel(slab_ref, gram_ref):
+    for n, (i, j) in enumerate(pairs(slab_ref.shape[0] // BLOCK)):
+        gram_ref[n * BLOCK : (n + 1) * BLOCK] = right_product(
+            slab_ref[i * BLOCK : (i + 1) * BLOCK], slab_ref[j * BLOCK : (j + 1) * BLOCK]
+        )
+
+
+def third_kernel(packed_ref, start_ref, slab_ref, factor_ref, core_ref, gram_ref):
+    for n, (i, j) in enumerate(pairs(slab_ref.shape[0] // BLOCK)):
+        block = packed_ref[n * BLOCK : (n + 1) * BLOCK]
+        gram_ref[i * BLOCK : (i + 1) * BLOCK, j * BLOCK : (j + 1) * BLOCK] = block
+        if i != j:
+            gram_ref[j * BLOCK : (j + 1) * BLOCK, i * BLOCK : (i + 1) * BLOCK] = block.T
+    basis = iterate(gram_ref[...], start_ref[...])
+    factor_ref[...] = basis * math.sqrt(basis.shape[0])
+    core_ref[...] = left_product(basis, slab_ref[...])
+
+
+def swap(x, axis, mask):
+    count = lax.axis_size(axis)
+    return lax.ppermute(x, axis, [(i, i ^ mask) for i in range(count)])
+
+
+def tree(parts):
+    while len(parts) > 1:
+        parts = [parts[i] + parts[i + 1] for i in range(0, len(parts), 2)]
+    return parts[0]
+
+
+def sum_small(x):
+    x = x + swap(x, "row", 1)
+    x = tree([x] + [swap(x, "row", m) for m in range(2, lax.axis_size("row"), 2)])
+    return tree([x] + [swap(x, "col", m) for m in range(1, lax.axis_size("col"))])
+
+
+def bit(axis, mask):
+    return (lax.axis_index(axis) & mask) != 0
+
+
+def halve(x, axis, mask):
+    rows = x.shape[0] // 2
+    low, high = x[:rows], x[rows:]
+    upper = bit(axis, mask)
+    return jnp.where(upper, high, low) + swap(jnp.where(upper, low, high), axis, mask)
+
+
+def double(x, axis, mask):
+    other = swap(x, axis, mask)
+    upper = bit(axis, mask)
+    return jnp.concatenate([jnp.where(upper, other, x), jnp.where(upper, x, other)], axis=0)
+
+
+def spread_rows(x, axis):
+    mask = 1
+    while mask < lax.axis_size(axis):
+        x = double(x, axis, mask)
+        mask *= 2
+    return x
+
+
+def sum_large(x):
+    x = halve(x, "row", 1)
+    rows = x.shape[0] // 2
+    masks = [m for m in (2, 4, 8, 16) if m < lax.axis_size("row")]
+    lanes = [(x[:rows], masks), (x[rows:], masks[::-1])]
+    done = []
+    for part, order in lanes:
+        for mask in order:
+            part = halve(part, "row", mask)
+        mask = 1
+        while mask < lax.axis_size("col"):
+            part = part + swap(part, "col", mask)
+            mask *= 2
+        for mask in order[::-1]:
+            part = double(part, "row", mask)
+        done.append(part)
+    return double(jnp.concatenate(done, axis=0), "row", 1)
+
+
+def swift(tensor, start_one, start_two, start_three):
+    rows_one, rows_two, depth = tensor.shape
+    rank = start_three.shape[1]
+    ways_one, ways_two = lax.axis_size("row"), lax.axis_size("col")
+    ways = ways_one * ways_two
+    full_one, full_two = rows_one * ways_one, rows_two * ways_two
+    flat = tensor.reshape(rows_one * rows_two, depth)
+    two = spread_rows(start_two, "col")
+    one = spread_rows(start_one, "row")
+
+    def regroup(x):
+        count = x.shape[0] // ways
+        x = lax.all_to_all(x.reshape(ways, count, rows_one * rows_two), AXES, 0, 0, tiled=True)
+        x = x.reshape(ways_one, ways_two, count, rows_one, rows_two)
+        return x.transpose(2, 0, 3, 1, 4).reshape(count, full_one, full_two)
+
+    contracted = regroup(cross_product(start_three, flat))
+    cells = regroup(flat.T)
+    (gram,) = call(open_kernel, "open", [(full_one, full_one)], contracted, two)
+    basis_one, factor_one, gram = call(
+        first_kernel,
+        "first",
+        [(full_one, rank), (full_one, rank), (full_two, full_two)],
+        sum_small(gram),
+        one,
+        contracted,
+    )
+    (basis_two,) = call(second_kernel, "second", [(full_two, rank)], sum_small(gram), two)
+    count = depth // ways
+    factor_two, slab = call(
+        slab_kernel, "slab", [(full_two, rank), (count, rank, rank)], basis_one, basis_two, cells
+    )
+    own_a, own_b = rank // ways_one, rank // ways_two
+    slab = slab.reshape(count, ways_one, own_a, ways_two, own_b).transpose(1, 3, 0, 2, 4)
+    slab = lax.all_to_all(slab.reshape(ways, count, own_a * own_b), AXES, 0, 0, tiled=True)
+    slab = slab.reshape(depth, own_a * own_b)
+    blocks = len(pairs(depth // BLOCK))
+    (packed,) = call(pair_kernel, "pair", [(blocks * BLOCK, BLOCK)], slab)
+    factor_three, core = pl.pallas_call(
+        third_kernel,
+        out_shape=[
+            jax.ShapeDtypeStruct((depth, rank), jnp.float32),
+            jax.ShapeDtypeStruct((rank, own_a * own_b), jnp.float32),
+        ],
+        in_specs=[VMEM] * 3,
+        out_specs=[VMEM] * 2,
+        scratch_shapes=[pltpu.VMEM((depth, depth), jnp.float32)],
+        name="third",
+    )(sum_large(packed), start_three, slab)
+    return (factor_one, factor_two, factor_three, core.reshape(rank, own_a, own_b))
+
+
+def power_of_two(value):
+    return value & (value - 1) == 0
+
+
+def on_device(tensor, start_one, start_two, start_three):
+    rank, depth = start_three.shape[1], start_three.shape[0]
+    ways_one, ways_two = lax.axis_size("row"), lax.axis_size("col")
+    ways = ways_one * ways_two
+    even = power_of_two(ways_one) and power_of_two(ways_two) and ways_one > 1
+    blocks = len(pairs(depth // BLOCK)) * BLOCK
+    even = even and rank % ways == 0 and depth % ways == 0 and depth % BLOCK == 0
+    if even and blocks % (8 * 2 * ways_one) == 0:
+        return swift(tensor, start_one, start_two, start_three)
+    return general(tensor, start_one, start_two, start_three)
+
+
 def solution(mesh):
     return jax.shard_map(
         on_device,

time: 644 us -> 249 us (0.39)
  blocking collectives: 190 us -> 15.2 us
  other arithmetic: 151 us -> 7.6 us
  waiting for transfers between devices: 205 us -> 78.8 us
  Pallas kernels: 0 us -> 59.1 us
  starting transfers between devices: 4.25 us -> 47.1 us
  matrix products: 33.9 us -> 3.03 us
  between operations: 15.1 us -> 0.92 us
    another operation x60 -> x0, other arithmetic: 145 us -> none  [the longest x36 78.2 us: orthonormal(): lower = jnp.linalg.cholesky(inner)]
    reduce_scatter x4 -> x0, waiting for transfers between devices: 107 us -> none  [the longest x1 43.1 us: on_device(): lax.psum_scatter(part_three.reshape(cells_here, rank * rank), 'col', scat...]
    all_gather x8 -> x0, blocking collectives: 96.7 us -> none  [the longest x4 35.2 us: on_device(): basis_three = lax.all_gather(own_three, 'row', axis=0, tiled=True)]
    psum x4 -> x0, blocking collectives: 93.5 us -> none  [on_device(): inner = lax.psum(left_product(image, image), 'row')]
    ppermute x0 -> x33, waiting for transfers between devices: none -> 72 us  [swap(): return lax.ppermute(x, axis, [(i, i ^ mask) for i in range(count)])]
    psum x3 -> x0, waiting for transfers between devices: 66.5 us -> none  [the longest x1 35.4 us: on_device(): gram_three = lax.psum(gram_part_three, 'col')]
    pallas_call x0 -> x6, Pallas kernels: none -> 59.1 us  [the longest x5 39 us: call(): pl.pallas_call(kernel, out_shape=[jax.ShapeDtypeStruct(shape, jnp.float32...]
    ppermute x0 -> x33, starting transfers between devices: none -> 36.9 us  [swap(): return lax.ppermute(x, axis, [(i, i ^ mask) for i in range(count)])]
  transfers between devices with their start and end apart: 9 -> 35, of which waited for: 7 -> 27; matrix products, arithmetic and copies ran while one was open for 15% -> 4% of each run, Pallas kernels for 0% -> 11%
where the time goes in v1:
time: 249 us; the launch traced here: 248 us
  waiting for transfers between devices  78.8 us (32%)
  Pallas kernels  59.1 us (24%)
  starting transfers between devices  47.1 us (19%)
  local copies, waits for them, and re-layouts  36.2 us (15%)
  blocking collectives  15.2 us (6%)
  other arithmetic  7.6 us (3%)
  matrix products  3.03 us (1%)
    ppermute x33, waiting for transfers between devices, swap(): return lax.ppermute(x, axis, [(i, i ^ mask) for i in range(count)])  72 us
    pallas_call x5, Pallas kernels, call(): pl.pallas_call(kernel, out_shape=[jax.ShapeDtypeStruct(shape, jnp.float32...  39 us
    ppermute x33, starting transfers between devices, swap(): return lax.ppermute(x, axis, [(i, i ^ mask) for i in range(count)])  36.9 us
    pallas_call x1, Pallas kernels, swift(): pl.pallas_call(third_kernel, out_shape=[jax.ShapeDtypeStruct((depth, rank...  20.1 us
    all_to_all x1, blocking collectives, swift(): lax.all_to_all(slab.reshape(ways, count, own_a * own_b), AXES, 0, 0, tile...  15.2 us
    all_to_all x2, starting transfers between devices, regroup(): lax.all_to_all(x.reshape(ways, count, rows_one * rows_two), AXES, 0, 0, t...  10.1 us
    transpose x1, local copies, waits for them, and re-layouts, regroup(): return x.transpose(2, 0, 3, 1, 4).reshape(count, full_one, full_two)  9.51 us
    reshape x2, local copies, waits for them, and re-layouts, regroup(): return x.transpose(2, 0, 3, 1, 4).reshape(count, full_one, full_two)  6.74 us
  transfers between devices with their start and end apart: 35, of which 27 were waited for; matrix products, arithmetic and copies ran while one was open for 4% of the time, Pallas kernels for 11%

profile of v1, /device:TPU:0, one launch (start us, length us, event | category | flops | bytes accessed | tf_op | source)
XLA Modules:
  0.0 247.9 jit_solution(10303458509391597372)
XLA Ops:
  1.8 3.0 %fusion = f32[32,2,512]{2,0,1:T(8,128)S(1)} fusion(f32[512,768,1]{1,0,2:T(8,128)} %bitcast.21, f32[32,2,768]{2,1,0:T(2,128)S(1)} %dot_general.8), kind=kOutput, calls=%fused_computation.7 | convolution fusion | flops 301989888 | bytes 1900544 | tf_op jit(solution)/shard_map/dot_general | solution.py:36
  5.6 7.3 %all-to-all-start = ((f32[32,2,512]{2,1,0:T(2,128)}), f32[32,2,512]{2,1,0:T(2,128)S(1)}, u32[]{:S(2)}, u32[]{:S(2)}) async-start(f32[32,2,512]{2,1,0:T(2,128)} %copy.40), calls=%async_computation | async-start | bytes 262144 | tf_op jit(solution)/shard_map/all_to_all | solution.py:298
  12.9 1.6 copy.42
  14.6 6.7 %all-to-all-done = f32[32,2,512]{2,1,0:T(2,128)S(1)} async-done(((f32[32,2,512]{2,1,0:T(2,128)}), f32[32,2,512]{2,1,0:T(2,128)S(1)}, u32[]{:S(2)}, u32[]{:S(2)}) %all-to-all-start) | async-done | bytes 131104 | tf_op jit(solution)/shard_map/all_to_all | solution.py:298
  21.3 2.8 %all-to-all-start.1 = ((f32[32,24,512]{2,1,0:T(8,128)}), f32[32,24,512]{2,1,0:T(8,128)S(1)}, u32[]{:S(2)}, u32[]{:S(2)}) async-start(f32[32,24,512]{2,1,0:T(8,128)} %bitcast.5), calls=%async_computation.1 | async-start | bytes 3145728 | tf_op jit(solution)/shard_map/all_to_all | solution.py:298
  24.3 1.7 collective-permute-start
  26.0 1.5 collective-permute-start.10
  27.6 22.8 %collective-permute-done = f32[32,64]{1,0:T(8,128)S(1)} collective-permute-done((f32[32,64]{1,0:T(8,128)S(1)}, f32[32,64]{1,0:T(8,128)S(1)}, u32[]{:S(2)}, u32[]{:S(2)}) %collective-permute-start) | collective-permute-done | bytes 8224 | tf_op jit(solution)/shard_map/ppermute | solution.py:227
  50.4 4.7 %collective-permute-start.1 = (f32[64,64]{1,0:T(8,128)S(1)}, f32[64,64]{1,0:T(8,128)S(1)}, u32[]{:S(2)}, u32[]{:S(2)}) collective-permute-start(f32[64,64]{1,0:T(8,128)S(1)} %pad_maximum_fusion.6), channel_id=1, source_target_pairs={{0,2},{1,3},{2,0},{3,1},{4,6},{5,7},{6,4},{7,5},{8,10},{9,11},{10,... | collective-permute-start | bytes 49160 | tf_op jit(solution)/shard_map/ppermute | solution.py:227
  55.1 7.9 %collective-permute-done.1 = f32[64,64]{1,0:T(8,128)S(1)} collective-permute-done((f32[64,64]{1,0:T(8,128)S(1)}, f32[64,64]{1,0:T(8,128)S(1)}, u32[]{:S(2)}, u32[]{:S(2)}) %collective-permute-start.1) | collective-permute-done | bytes 16416 | tf_op jit(solution)/shard_map/ppermute | solution.py:227
  65.1 2.2 open.1
  67.3 1.6 collective-permute-start.11
  69.7 1.4 collective-permute-start.4
  71.2 1.6 collective-permute-start.5
  74.0 2.9 %collective-permute-done.5 = f32[128,128]{1,0:T(8,128)S(1)} collective-permute-done((f32[128,128]{1,0:T(8,128)S(1)}, f32[128,128]{1,0:T(8,128)S(1)}, u32[]{:S(2)}, u32[]{:S(2)}) %collective-permute-start.5) | collective-permute-done | bytes 65568 | tf_op jit(solution)/shard_map/ppermute | solution.py:227
  77.1 1.5 collective-permute-start.8
  78.5 2.0 collective-permute-start.6
  81.2 2.5 %collective-permute-done.7 = f32[128,128]{1,0:T(8,128)S(1)} collective-permute-done((f32[128,128]{1,0:T(8,128)S(1)}, f32[128,128]{1,0:T(8,128)S(1)}, u32[]{:S(2)}, u32[]{:S(2)}) %collective-permute-start.7) | collective-permute-done | bytes 65568 | tf_op jit(solution)/shard_map/ppermute | solution.py:227
  84.8 12.6 %first.1 = (f32[128,64]{1,0:T(8,128)}, f32[128,64]{1,0:T(8,128)}, f32[128,128]{1,0:T(8,128)}) custom-call(f32[128,128]{1,0:T(8,128)} %add_add_fusion.2.gram_ref, f32[128,64]{1,0:T(8,128)} %pad_maximum_fusion.5.start_ref, f32[2,128,128]{2,1,0:T(8,128)} %reshape.42.cont_ref), custom_call_target="tpu_custom_call" | custom-call | tf_op jit(solution)/shard_map/first/pallas_call | solution.py:148
  97.5 1.5 collective-permute-done.12
  99.8 1.4 collective-permute-start.14
  104.1 2.5 %collective-permute-done.15 = f32[128,128]{1,0:T(8,128)S(1)} collective-permute-done((f32[128,128]{1,0:T(8,128)S(1)}, f32[128,128]{1,0:T(8,128)S(1)}, u32[]{:S(2)}, u32[]{:S(2)}) %collective-permute-start.15) | collective-permute-done | bytes 65568 | tf_op jit(solution)/shard_map/ppermute | solution.py:227
  106.7 1.7 collective-permute-start.17
  108.4 1.9 collective-permute-start.18
  110.3 2.9 %collective-permute-done.17 = f32[128,128]{1,0:T(8,128)S(1)} collective-permute-done((f32[128,128]{1,0:T(8,128)S(1)}, f32[128,128]{1,0:T(8,128)S(1)}, u32[]{:S(2)}, u32[]{:S(2)}) %collective-permute-start.17) | collective-permute-done | bytes 65568 | tf_op jit(solution)/shard_map/ppermute | solution.py:227
  113.2 1.4 collective-permute-done.18
  115.9 12.0 %second.1.right_ref = f32[128,64]{1,0:T(8,128)} custom-call(f32[128,128]{1,0:T(8,128)} %add_add_fusion.gram_ref, f32[128,64]{1,0:T(8,128)} %pad_maximum_fusion.4.start_ref), custom_call_target="tpu_custom_call" | custom-call | tf_op jit(solution)/shard_map/second/pallas_call | solution.py:148
  127.9 3.9 %reshape.44 = f32[8,4,24,16,32]{4,3,2,1,0:T(8,128)} reshape(f32[32,24,512]{2,1,0:T(8,128)S(1)} %all-to-all-done.1) | data formatting | bytes 3145728 | tf_op jit(solution)/shard_map/reshape | solution.py:299
  131.7 9.5 %copy.43 = f32[24,8,16,4,32]{4,3,2,1,0:T(4,128)} copy(f32[24,8,16,4,32]{4,2,0,3,1:T(8,128)} %bitcast.19) | data formatting | bytes 3145728 | tf_op jit(solution)/shard_map/transpose | solution.py:300
  141.2 5.8 %reshape.45.tensor_ref = f32[24,128,128]{2,1,0:T(8,128)} reshape(f32[24,8,16,4,32]{4,3,2,1,0:T(4,128)} %copy.43) | data formatting | bytes 3145728 | tf_op jit(solution)/shard_map/reshape | solution.py:300
  147.1 7.2 %slab.1 = (f32[128,64]{1,0:T(8,128)}, f32[24,64,64]{2,1,0:T(8,128)}) custom-call(f32[128,64]{1,0:T(8,128)} %get-tuple-element.12.left_ref, f32[128,64]{1,0:T(8,128)} %second.1.right_ref, f32[24,128,128]{2,1,0:T(8,128)} %reshape.45.tensor_ref), custom_call_target="tpu_custom_call" | custom-call | tf_op jit(solution)/shard_map/slab/pallas_call | solution.py:148
  154.3 3.1 %copy.44 = f32[24,64,64]{0,2,1:T(8,128)} copy(f32[24,64,64]{2,1,0:T(8,128)} %get-tuple-element.15) | data formatting | bytes 786432 | tf_op jit(solution)/shard_map/slab/pallas_call | solution.py:148
  157.4 2.4 copy.45
  160.6 15.2 %all_to_all.15 = f32[32,24,128]{2,1,0:T(8,128)} all-to-all(f32[32,24,128]{2,1,0:T(8,128)S(1)} %reshape.47), channel_id=1, replica_groups=mesh['row'=8,'col'=4] {'row','col'}, dimensions={0} | all-to-all | bytes 786432 | tf_op jit(solution)/shard_map/all_to_all | solution.py:320
  175.7 5.1 %pair.1 = f32[2688,128]{1,0:T(8,128)} custom-call(f32[768,128]{1,0:T(8,128)} %bitcast.23), custom_call_target="tpu_custom_call" | custom-call | tf_op jit(solution)/shard_map/pair/pallas_call | solution.py:148
  180.8 1.5 slice_select_fusion
  183.6 1.8 collective-permute-done.19
  187.3 4.9 %collective-permute-done.20 = f32[336,128]{1,0:T(8,128)S(1)} collective-permute-done((f32[336,128]{1,0:T(8,128)S(1)}, f32[336,128]{1,0:T(8,128)S(1)}, u32[]{:S(2)}, u32[]{:S(2)}) %collective-permute-start.20) | collective-permute-done | bytes 172064 | tf_op jit(solution)/shard_map/ppermute | solution.py:227
  195.4 2.4 collective-permute-done.27
  200.0 2.4 collective-permute-done.28
  203.4 2.3 collective-permute-start.23
  205.7 3.0 %collective-permute-done.29 = f32[168,128]{1,0:T(8,128)S(1)} collective-permute-done((f32[168,128]{1,0:T(8,128)S(1)}, f32[168,128]{1,0:T(8,128)S(1)}, u32[]{:S(2)}, u32[]{:S(2)}) %collective-permute-start.29) | collective-permute-done | bytes 86048 | tf_op jit(solution)/shard_map/ppermute | solution.py:227
  208.8 1.7 collective-permute-done.23
  211.5 2.3 collective-permute-done.30
  216.5 2.8 %collective-permute-done.31 = f32[336,128]{1,0:T(8,128)S(1)} collective-permute-done((f32[336,128]{1,0:T(8,128)S(1)}, f32[336,128]{1,0:T(8,128)S(1)}, u32[]{:S(2)}, u32[]{:S(2)}) %collective-permute-start.31) | collective-permute-done | bytes 172064 | tf_op jit(solution)/shard_map/ppermute | solution.py:227
  224.5 20.1 %third.1 = (f32[768,64]{1,0:T(8,128)}, f32[64,128]{1,0:T(8,128)}) custom-call(f32[2688,128]{1,0:T(8,128)} %pad_maximum_fusion.packed_ref, f32[768,64]{1,0:T(8,128)} %copy.46.start_ref, f32[768,128]{1,0:T(8,128)} %bitcast.24), custom_call_target="tpu_custom_call" | custom-call | tf_op jit(solution)/shard_map/third/pallas_call | solution.py:324
  244.6 1.8 copy.50
  246.4 1.5 copy.47
  (98 shorter events, 32.7 us)
Async XLA Ops:
  0.6 12.3 %copy-start.1 = (f32[16,32,768]{2,1,0:T(8,128)S(1)}, f32[16,32,768]{2,1,0:T(8,128)}, u32[]{:S(2)}) copy-start(f32[16,32,768]{2,1,0:T(8,128)} %param.4) | copy-start | bytes 4718596
  5.6 15.7 %all-to-all-start = ((f32[32,2,512]{2,1,0:T(2,128)}), f32[32,2,512]{2,1,0:T(2,128)S(1)}, u32[]{:S(2)}, u32[]{:S(2)}) async-start(f32[32,2,512]{2,1,0:T(2,128)} %copy.40), calls=%async_computation | async-start | bytes 262144 | tf_op jit(solution)/shard_map/all_to_all | solution.py:298
  21.3 2.8 %copy-start.6 = (f32[16,64]{1,0:T(8,128)S(1)}, f32[16,64]{1,0:T(8,128)}, u32[]{:S(2)}) copy-start(f32[16,64]{1,0:T(8,128)} %param.5) | copy-start | bytes 12292
  21.3 3.0 %copy-start.5 = (f32[32,64]{1,0:T(8,128)S(1)}, f32[32,64]{1,0:T(8,128)}, u32[]{:S(2)}) copy-start(f32[32,64]{1,0:T(8,128)} %param.6) | copy-start | bytes 24580
  21.3 106.6 %all-to-all-start.1 = ((f32[32,24,512]{2,1,0:T(8,128)}), f32[32,24,512]{2,1,0:T(8,128)S(1)}, u32[]{:S(2)}, u32[]{:S(2)}) async-start(f32[32,24,512]{2,1,0:T(8,128)} %bitcast.5), calls=%async_computation.1 | async-start | bytes 3145728 | tf_op jit(solution)/shard_map/all_to_all | solution.py:298
  24.1 1.9 collective-permute-start.9
  24.3 26.1 %collective-permute-start = (f32[32,64]{1,0:T(8,128)S(1)}, f32[32,64]{1,0:T(8,128)S(1)}, u32[]{:S(2)}, u32[]{:S(2)}) collective-permute-start(f32[32,64]{1,0:T(8,128)S(1)} %copy-done.5), channel_id=1, source_target_pairs={{0,1},{1,0},{2,3},{3,2},{4,5},{5,4},{6,7},{7,6},{8,9},{9,8},{10,11... | collective-permute-start | bytes 24584 | tf_op jit(solution)/shard_map/ppermute | solution.py:227
  26.0 29.1 %collective-permute-start.10 = (f32[32,64]{1,0:T(8,128)S(1)}, f32[32,64]{1,0:T(8,128)S(1)}, u32[]{:S(2)}, u32[]{:S(2)}) collective-permute-start(f32[32,64]{1,0:T(8,128)S(1)} %pad_maximum_fusion.8), channel_id=1, source_target_pairs={{0,8},{4,12},{8,0},{12,4},{16,24},{20,28},{24,16},{28,20},{1,9},{5... | collective-permute-start | bytes 24584 | tf_op jit(solution)/shard_map/ppermute | solution.py:227
  50.4 12.5 %collective-permute-start.1 = (f32[64,64]{1,0:T(8,128)S(1)}, f32[64,64]{1,0:T(8,128)S(1)}, u32[]{:S(2)}, u32[]{:S(2)}) collective-permute-start(f32[64,64]{1,0:T(8,128)S(1)} %pad_maximum_fusion.6), channel_id=1, source_target_pairs={{0,2},{1,3},{2,0},{3,1},{4,6},{5,7},{6,4},{7,5},{8,10},{9,11},{10,... | collective-permute-start | bytes 49160 | tf_op jit(solution)/shard_map/ppermute | solution.py:227
  67.3 1.6 collective-permute-start.2
  67.3 6.0 %collective-permute-start.11 = (f32[64,64]{1,0:T(8,128)S(1)}, f32[64,64]{1,0:T(8,128)S(1)}, u32[]{:S(2)}, u32[]{:S(2)}) collective-permute-start(f32[64,64]{1,0:T(8,128)S(1)} %pad_maximum_fusion.7), channel_id=1, source_target_pairs={{0,16},{4,20},{8,24},{12,28},{16,0},{20,4},{24,8},{28,12},{1,17},{... | collective-permute-start | bytes 49160 | tf_op jit(solution)/shard_map/ppermute | solution.py:227
  69.7 4.3 %collective-permute-start.4 = (f32[128,128]{1,0:T(8,128)S(1)}, f32[128,128]{1,0:T(8,128)S(1)}, u32[]{:S(2)}, u32[]{:S(2)}) collective-permute-start(f32[128,128]{1,0:T(8,128)S(1)} %add.69), channel_id=1, source_target_pairs={{0,16},{4,20},{8,24},{12,28},{16,0},{20,4},{24,8},{28,12},{1,17},{... | collective-permute-start | bytes 196616 | tf_op jit(solution)/shard_map/ppermute | solution.py:227
  71.2 5.8 %collective-permute-start.5 = (f32[128,128]{1,0:T(8,128)S(1)}, f32[128,128]{1,0:T(8,128)S(1)}, u32[]{:S(2)}, u32[]{:S(2)}) collective-permute-start(f32[128,128]{1,0:T(8,128)S(1)} %add.69), channel_id=1, source_target_pairs={{0,24},{4,28},{8,16},{12,20},{16,8},{20,12},{24,0},{28,4},{1,25},{... | collective-permute-start | bytes 196616 | tf_op jit(solution)/shard_map/ppermute | solution.py:227
  72.7 4.3 %collective-permute-start.3 = (f32[128,128]{1,0:T(8,128)S(1)}, f32[128,128]{1,0:T(8,128)S(1)}, u32[]{:S(2)}, u32[]{:S(2)}) collective-permute-start(f32[128,128]{1,0:T(8,128)S(1)} %add.69), channel_id=1, source_target_pairs={{0,8},{4,12},{8,0},{12,4},{16,24},{20,28},{24,16},{28,20},{1,9},{5... | collective-permute-start | bytes 196616 | tf_op jit(solution)/shard_map/ppermute | solution.py:227
  77.0 6.7 %collective-permute-start.7 = (f32[128,128]{1,0:T(8,128)S(1)}, f32[128,128]{1,0:T(8,128)S(1)}, u32[]{:S(2)}, u32[]{:S(2)}) collective-permute-start(f32[128,128]{1,0:T(8,128)S(1)} %add_add_fusion.3), channel_id=1, source_target_pairs={{0,2},{1,3},{2,0},{3,1},{4,6},{5,7},{6,4},{7,5},{8,10},{9,11},{10,... | collective-permute-start | bytes 196616 | tf_op jit(solution)/shard_map/ppermute | solution.py:227
  77.1 6.6 %collective-permute-start.8 = (f32[128,128]{1,0:T(8,128)S(1)}, f32[128,128]{1,0:T(8,128)S(1)}, u32[]{:S(2)}, u32[]{:S(2)}) collective-permute-start(f32[128,128]{1,0:T(8,128)S(1)} %add_add_fusion.3), channel_id=1, source_target_pairs={{0,3},{1,2},{2,1},{3,0},{4,7},{5,6},{6,5},{7,4},{8,11},{9,10},{10,... | collective-permute-start | bytes 196616 | tf_op jit(solution)/shard_map/ppermute | solution.py:227
  78.5 5.6 %collective-permute-start.6 = (f32[128,128]{1,0:T(8,128)S(1)}, f32[128,128]{1,0:T(8,128)S(1)}, u32[]{:S(2)}, u32[]{:S(2)}) collective-permute-start(f32[128,128]{1,0:T(8,128)S(1)} %add_add_fusion.3), channel_id=1, source_target_pairs={{0,1},{1,0},{2,3},{3,2},{4,5},{5,4},{6,7},{7,6},{8,9},{9,8},{10,11... | collective-permute-start | bytes 196616 | tf_op jit(solution)/shard_map/ppermute | solution.py:227
  97.5 1.5 collective-permute-start.12
  99.8 4.3 %collective-permute-start.14 = (f32[128,128]{1,0:T(8,128)S(1)}, f32[128,128]{1,0:T(8,128)S(1)}, u32[]{:S(2)}, u32[]{:S(2)}) collective-permute-start(f32[128,128]{1,0:T(8,128)S(1)} %add.76), channel_id=1, source_target_pairs={{0,16},{4,20},{8,24},{12,28},{16,0},{20,4},{24,8},{28,12},{1,17},{... | collective-permute-start | bytes 196616 | tf_op jit(solution)/shard_map/ppermute | solution.py:227
  101.2 5.5 %collective-permute-start.15 = (f32[128,128]{1,0:T(8,128)S(1)}, f32[128,128]{1,0:T(8,128)S(1)}, u32[]{:S(2)}, u32[]{:S(2)}) collective-permute-start(f32[128,128]{1,0:T(8,128)S(1)} %add.76), channel_id=1, source_target_pairs={{0,24},{4,28},{8,16},{12,20},{16,8},{20,12},{24,0},{28,4},{1,25},{... | collective-permute-start | bytes 196616 | tf_op jit(solution)/shard_map/ppermute | solution.py:227
  102.2 4.5 %collective-permute-start.13 = (f32[128,128]{1,0:T(8,128)S(1)}, f32[128,128]{1,0:T(8,128)S(1)}, u32[]{:S(2)}, u32[]{:S(2)}) collective-permute-start(f32[128,128]{1,0:T(8,128)S(1)} %add.76), channel_id=1, source_target_pairs={{0,8},{4,12},{8,0},{12,4},{16,24},{20,28},{24,16},{28,20},{1,9},{5... | collective-permute-start | bytes 196616 | tf_op jit(solution)/shard_map/ppermute | solution.py:227
  106.7 6.5 %collective-permute-start.17 = (f32[128,128]{1,0:T(8,128)S(1)}, f32[128,128]{1,0:T(8,128)S(1)}, u32[]{:S(2)}, u32[]{:S(2)}) collective-permute-start(f32[128,128]{1,0:T(8,128)S(1)} %add_add_fusion.1), channel_id=1, source_target_pairs={{0,2},{1,3},{2,0},{3,1},{4,6},{5,7},{6,4},{7,5},{8,10},{9,11},{10,... | collective-permute-start | bytes 196616 | tf_op jit(solution)/shard_map/ppermute | solution.py:227
  108.4 6.2 %collective-permute-start.18 = (f32[128,128]{1,0:T(8,128)S(1)}, f32[128,128]{1,0:T(8,128)S(1)}, u32[]{:S(2)}, u32[]{:S(2)}) collective-permute-start(f32[128,128]{1,0:T(8,128)S(1)} %add_add_fusion.1), channel_id=1, source_target_pairs={{0,3},{1,2},{2,1},{3,0},{4,7},{5,6},{6,5},{7,4},{8,11},{9,10},{10,... | collective-permute-start | bytes 196616 | tf_op jit(solution)/shard_map/ppermute | solution.py:227
  110.3 4.9 %collective-permute-start.16 = (f32[128,128]{1,0:T(8,128)S(1)}, f32[128,128]{1,0:T(8,128)S(1)}, u32[]{:S(2)}, u32[]{:S(2)}) collective-permute-start(f32[128,128]{1,0:T(8,128)S(1)} %add_add_fusion.1), channel_id=1, source_target_pairs={{0,1},{1,0},{2,3},{3,2},{4,5},{5,4},{6,7},{7,6},{8,9},{9,8},{10,11... | collective-permute-start | bytes 196616 | tf_op jit(solution)/shard_map/ppermute | solution.py:227
  180.8 4.5 %copy-start = (f32[2688,128]{1,0:T(8,128)S(1)}, f32[2688,128]{1,0:T(8,128)}, u32[]{:S(2)}) copy-start(f32[2688,128]{1,0:T(8,128)} %pair.1) | copy-start | bytes 4128772
  182.3 3.1 %collective-permute-start.19 = (f32[1344,128]{1,0:T(8,128)S(1)}, f32[1344,128]{1,0:T(8,128)S(1)}, u32[]{:S(2)}, u32[]{:S(2)}) collective-permute-start(f32[1344,128]{1,0:T(8,128)S(1)} %slice_select_fusion), channel_id=1, source_target_pairs={{0,4},{4,0},{8,12},{12,8},{16,20},{20,16},{24,28},{28,24},{1,5},{5... | collective-permute-start | bytes 2064392 | tf_op jit(solution)/shard_map/ppermute | solution.py:227
  185.5 6.7 %collective-permute-start.20 = (f32[336,128]{1,0:T(8,128)S(1)}, f32[336,128]{1,0:T(8,128)S(1)}, u32[]{:S(2)}, u32[]{:S(2)}) collective-permute-start(f32[336,128]{1,0:T(8,128)S(1)} %get-tuple-element.38), channel_id=1, source_target_pairs={{0,8},{4,12},{8,0},{12,4},{16,24},{20,28},{24,16},{28,20},{1,9},{5... | collective-permute-start | bytes 516104 | tf_op jit(solution)/shard_map/ppermute | solution.py:227
  186.7 6.4 %collective-permute-start.26 = (f32[336,128]{1,0:T(8,128)S(1)}, f32[336,128]{1,0:T(8,128)S(1)}, u32[]{:S(2)}, u32[]{:S(2)}) collective-permute-start(f32[336,128]{1,0:T(8,128)S(1)} %get-tuple-element.39), channel_id=1, source_target_pairs={{0,16},{4,20},{8,24},{12,28},{16,0},{20,4},{24,8},{28,12},{1,17},{... | collective-permute-start | bytes 516104 | tf_op jit(solution)/shard_map/ppermute | solution.py:227
  193.2 4.6 %collective-permute-start.27 = (f32[168,128]{1,0:T(8,128)S(1)}, f32[168,128]{1,0:T(8,128)S(1)}, u32[]{:S(2)}, u32[]{:S(2)}) collective-permute-start(f32[168,128]{1,0:T(8,128)S(1)} %slice_select_fusion.3), channel_id=1, source_target_pairs={{0,8},{4,12},{8,0},{12,4},{16,24},{20,28},{24,16},{28,20},{1,9},{5... | collective-permute-start | bytes 258056 | tf_op jit(solution)/shard_map/ppermute | solution.py:227
  194.1 4.6 %collective-permute-start.21 = (f32[168,128]{1,0:T(8,128)S(1)}, f32[168,128]{1,0:T(8,128)S(1)}, u32[]{:S(2)}, u32[]{:S(2)}) collective-permute-start(f32[168,128]{1,0:T(8,128)S(1)} %slice_select_fusion.4), channel_id=1, source_target_pairs={{0,16},{4,20},{8,24},{12,28},{16,0},{20,4},{24,8},{28,12},{1,17},{... | collective-permute-start | bytes 258056 | tf_op jit(solution)/shard_map/ppermute | solution.py:227
  197.8 4.5 %collective-permute-start.28 = (f32[168,128]{1,0:T(8,128)S(1)}, f32[168,128]{1,0:T(8,128)S(1)}, u32[]{:S(2)}, u32[]{:S(2)}) collective-permute-start(f32[168,128]{1,0:T(8,128)S(1)} %select_add_fusion.3), channel_id=1, source_target_pairs={{0,1},{1,0},{2,3},{3,2},{4,5},{5,4},{6,7},{7,6},{8,9},{9,8},{10,11... | collective-permute-start | bytes 258056 | tf_op jit(solution)/shard_map/ppermute | solution.py:227
  198.7 4.7 %collective-permute-start.22 = (f32[168,128]{1,0:T(8,128)S(1)}, f32[168,128]{1,0:T(8,128)S(1)}, u32[]{:S(2)}, u32[]{:S(2)}) collective-permute-start(f32[168,128]{1,0:T(8,128)S(1)} %select_add_fusion.4), channel_id=1, source_target_pairs={{0,1},{1,0},{2,3},{3,2},{4,5},{5,4},{6,7},{7,6},{8,9},{9,8},{10,11... | collective-permute-start | bytes 258056 | tf_op jit(solution)/shard_map/ppermute | solution.py:227
  202.3 6.4 %collective-permute-start.29 = (f32[168,128]{1,0:T(8,128)S(1)}, f32[168,128]{1,0:T(8,128)S(1)}, u32[]{:S(2)}, u32[]{:S(2)}) collective-permute-start(f32[168,128]{1,0:T(8,128)S(1)} %add.90), channel_id=1, source_target_pairs={{0,2},{1,3},{2,0},{3,1},{4,6},{5,7},{6,4},{7,5},{8,10},{9,11},{10,... | collective-permute-start | bytes 258056 | tf_op jit(solution)/shard_map/ppermute | solution.py:227
  203.4 7.2 %collective-permute-start.23 = (f32[168,128]{1,0:T(8,128)S(1)}, f32[168,128]{1,0:T(8,128)S(1)}, u32[]{:S(2)}, u32[]{:S(2)}) collective-permute-start(f32[168,128]{1,0:T(8,128)S(1)} %add.86), channel_id=1, source_target_pairs={{0,2},{1,3},{2,0},{3,1},{4,6},{5,7},{6,4},{7,5},{8,10},{9,11},{10,... | collective-permute-start | bytes 258056 | tf_op jit(solution)/shard_map/ppermute | solution.py:227
  208.7 5.0 %collective-permute-start.30 = (f32[168,128]{1,0:T(8,128)S(1)}, f32[168,128]{1,0:T(8,128)S(1)}, u32[]{:S(2)}, u32[]{:S(2)}) collective-permute-start(f32[168,128]{1,0:T(8,128)S(1)} %add.91), channel_id=1, source_target_pairs={{0,8},{4,12},{8,0},{12,4},{16,24},{20,28},{24,16},{28,20},{1,9},{5... | collective-permute-start | bytes 258056 | tf_op jit(solution)/shard_map/ppermute | solution.py:227
  210.6 4.6 %collective-permute-start.24 = (f32[168,128]{1,0:T(8,128)S(1)}, f32[168,128]{1,0:T(8,128)S(1)}, u32[]{:S(2)}, u32[]{:S(2)}) collective-permute-start(f32[168,128]{1,0:T(8,128)S(1)} %add.87), channel_id=1, source_target_pairs={{0,16},{4,20},{8,24},{12,28},{16,0},{20,4},{24,8},{28,12},{1,17},{... | collective-permute-start | bytes 258056 | tf_op jit(solution)/shard_map/ppermute | solution.py:227
  213.8 5.5 %collective-permute-start.31 = (f32[336,128]{1,0:T(8,128)S(1)}, f32[336,128]{1,0:T(8,128)S(1)}, u32[]{:S(2)}, u32[]{:S(2)}) collective-permute-start(f32[336,128]{1,0:T(8,128)S(1)} %pad_maximum_fusion.3), channel_id=1, source_target_pairs={{0,16},{4,20},{8,24},{12,28},{16,0},{20,4},{24,8},{28,12},{1,17},{... | collective-permute-start | bytes 516104 | tf_op jit(solution)/shard_map/ppermute | solution.py:227
  215.1 5.7 %copy-start.2 = (f32[768,64]{0,1:T(8,128)S(1)}, f32[768,64]{0,1:T(8,128)}, u32[]{:S(2)}) copy-start(f32[768,64]{0,1:T(8,128)} %param.7) | copy-start | bytes 589828
  215.2 6.6 %copy-start.3 = (f32[128,64]{1,0:T(8,128)S(1)}, f32[128,64]{1,0:T(8,128)}, u32[]{:S(2)}) copy-start(f32[128,64]{1,0:T(8,128)} %get-tuple-element.30) | copy-start | bytes 98308
  215.2 7.3 %copy-start.4 = (f32[128,64]{1,0:T(8,128)S(1)}, f32[128,64]{1,0:T(8,128)}, u32[]{:S(2)}) copy-start(f32[128,64]{1,0:T(8,128)} %get-tuple-element.31) | copy-start | bytes 98308
  215.2 5.5 %collective-permute-start.25 = (f32[336,128]{1,0:T(8,128)S(1)}, f32[336,128]{1,0:T(8,128)S(1)}, u32[]{:S(2)}, u32[]{:S(2)}) collective-permute-start(f32[336,128]{1,0:T(8,128)S(1)} %pad_maximum_fusion.2), channel_id=1, source_target_pairs={{0,8},{4,12},{8,0},{12,4},{16,24},{20,28},{24,16},{28,20},{1,9},{5... | collective-permute-start | bytes 516104 | tf_op jit(solution)/shard_map/ppermute | solution.py:227
  220.7 2.4 collective-permute-start.32

commit v2 on v1

--- a/solution.py
+++ b/solution.py
@@ -1,3 +1,4 @@
+import functools
 import math
 
 import jax
@@ -144,12 +145,13 @@
 VMEM = pl.BlockSpec(memory_space=pltpu.VMEM)
 
 
-def call(kernel, name, outs, *args):
+def call(kernel, name, outs, *args, scratch=()):
     return pl.pallas_call(
         kernel,
         out_shape=[jax.ShapeDtypeStruct(shape, jnp.float32) for shape in outs],
         in_specs=[VMEM] * len(args),
         out_specs=[VMEM] * len(outs),
+        scratch_shapes=[pltpu.VMEM(shape, jnp.float32) for shape in scratch],
         name=name,
     )(*args)
 
@@ -191,13 +193,48 @@
     factor_ref[...] = basis
 
 
-def slab_kernel(left_ref, right_ref, tensor_ref, factor_ref, slab_ref):
+def mix_kernel(factor_ref, cells_ref, mixed_ref, turn_ref, groups):
+    ways, count, width = cells_ref.shape
+    full, rank = factor_ref.shape
+    span = BLOCK // groups
+    lane = lax.broadcasted_iota(jnp.int32, (count, BLOCK), 1) // span
+    tiles = width // BLOCK
+    for r in range(ways // groups):
+        for tile in range(tiles):
+            held = [
+                cells_ref[r * groups + c, :, tile * BLOCK : (tile + 1) * BLOCK] for c in range(groups)
+            ]
+            for inner in range(groups):
+                piece = held[inner]
+                for c in range(groups):
+                    if c != inner:
+                        moved = pltpu.roll(held[c], (c - inner) * span % BLOCK, 1)
+                        piece = jnp.where(lane == c, moved, piece)
+                index = (r * tiles + tile) * groups + inner
+                turn_ref[pl.ds(index, count, stride=full), :] = piece
+    for k in range(count):
+        mixed_ref[k * rank : (k + 1) * rank] = left_product(
+            factor_ref[...], turn_ref[k * full : (k + 1) * full]
+        )
+
+
+def slab_kernel(right_ref, mixed_ref, factor_ref, slab_ref, turn_ref, own_b):
     right = right_ref[...]
     factor_ref[...] = right * math.sqrt(right.shape[0])
-    count, rows, cols = tensor_ref.shape
-    half = product(tensor_ref[...].reshape(count * rows, cols), right)
-    for k in range(count):
-        slab_ref[k] = left_product(left_ref[...], half[k * rows : (k + 1) * rows])
+    count, width = slab_ref.shape[1:]
+    rank = right.shape[1]
+    own_a, ways_two = width // own_b, rank // own_b
+    turn_ref[...] = product(mixed_ref[...], jnp.pad(right, ((0, 0), (0, width - rank))))
+    lane = lax.broadcasted_iota(jnp.int32, (count, width), 1) // own_b
+    for r in range(rank // own_a):
+        held = [turn_ref[pl.ds(r * own_a + a, count, stride=rank), :] for a in range(own_a)]
+        for c in range(ways_two):
+            piece = held[c % own_a]
+            for a in range(own_a):
+                if a != c:
+                    moved = pltpu.roll(held[a], (a - c) * own_b % width, 1)
+                    piece = jnp.where(lane == a, moved, piece)
+            slab_ref[r * ways_two + c] = piece
 
 
 def pairs(blocks):
@@ -205,18 +242,19 @@
 
 
 def pair_kernel(slab_ref, gram_ref):
-    for n, (i, j) in enumerate(pairs(slab_ref.shape[0] // BLOCK)):
-        gram_ref[n * BLOCK : (n + 1) * BLOCK] = right_product(
-            slab_ref[i * BLOCK : (i + 1) * BLOCK], slab_ref[j * BLOCK : (j + 1) * BLOCK]
-        )
+    row = 0
+    for i in range(slab_ref.shape[0] // BLOCK):
+        part = right_product(slab_ref[i * BLOCK :], slab_ref[i * BLOCK : (i + 1) * BLOCK])
+        gram_ref[row : row + part.shape[0]] = part
+        row += part.shape[0]
 
 
 def third_kernel(packed_ref, start_ref, slab_ref, factor_ref, core_ref, gram_ref):
     for n, (i, j) in enumerate(pairs(slab_ref.shape[0] // BLOCK)):
         block = packed_ref[n * BLOCK : (n + 1) * BLOCK]
-        gram_ref[i * BLOCK : (i + 1) * BLOCK, j * BLOCK : (j + 1) * BLOCK] = block
+        gram_ref[j * BLOCK : (j + 1) * BLOCK, i * BLOCK : (i + 1) * BLOCK] = block
         if i != j:
-            gram_ref[j * BLOCK : (j + 1) * BLOCK, i * BLOCK : (i + 1) * BLOCK] = block.T
+            gram_ref[i * BLOCK : (i + 1) * BLOCK, j * BLOCK : (j + 1) * BLOCK] = block.T
     basis = iterate(gram_ref[...], start_ref[...])
     factor_ref[...] = basis * math.sqrt(basis.shape[0])
     core_ref[...] = left_product(basis, slab_ref[...])
@@ -257,11 +295,14 @@
 
 
 def spread_rows(x, axis):
+    count = lax.axis_size(axis)
+    parts = [x] + [swap(x, axis, m) for m in range(1, count)]
     mask = 1
-    while mask < lax.axis_size(axis):
-        x = double(x, axis, mask)
+    while mask < count:
+        upper = bit(axis, mask)
+        parts = [jnp.where(upper, parts[i ^ mask], parts[i]) for i in range(count)]
         mask *= 2
-    return x
+    return jnp.concatenate(parts, axis=0)
 
 
 def sum_large(x):
@@ -293,32 +334,44 @@
     two = spread_rows(start_two, "col")
     one = spread_rows(start_one, "row")
 
-    def regroup(x):
-        count = x.shape[0] // ways
-        x = lax.all_to_all(x.reshape(ways, count, rows_one * rows_two), AXES, 0, 0, tiled=True)
-        x = x.reshape(ways_one, ways_two, count, rows_one, rows_two)
-        return x.transpose(2, 0, 3, 1, 4).reshape(count, full_one, full_two)
-
-    contracted = regroup(cross_product(start_three, flat))
-    cells = regroup(flat.T)
+    def trade(x):
+        shape = (ways, x.shape[0] // ways, x.shape[1])
+        return lax.all_to_all(x.reshape(shape), AXES, 0, 0, tiled=True)
+
+    contracted = trade(cross_product(start_three, flat))
+    contracted = contracted.reshape(ways_one, ways_two, rank // ways, rows_one, rows_two)
+    contracted = contracted.transpose(2, 0, 3, 1, 4).reshape(rank // ways, full_one, full_two)
     (gram,) = call(open_kernel, "open", [(full_one, full_one)], contracted, two)
+    gram, one, turned = lax.optimization_barrier((sum_small(gram), one, flat.T))
+    cells = trade(turned)
     basis_one, factor_one, gram = call(
         first_kernel,
         "first",
         [(full_one, rank), (full_one, rank), (full_two, full_two)],
-        sum_small(gram),
+        gram,
         one,
         contracted,
     )
     (basis_two,) = call(second_kernel, "second", [(full_two, rank)], sum_small(gram), two)
     count = depth // ways
+    (mixed,) = call(
+        functools.partial(mix_kernel, groups=ways_two),
+        "mix",
+        [(count * rank, full_two)],
+        basis_one,
+        cells,
+        scratch=[(count * full_one, full_two)],
+    )
+    own_a, own_b = rank // ways_one, rank // ways_two
     factor_two, slab = call(
-        slab_kernel, "slab", [(full_two, rank), (count, rank, rank)], basis_one, basis_two, cells
-    )
-    own_a, own_b = rank // ways_one, rank // ways_two
-    slab = slab.reshape(count, ways_one, own_a, ways_two, own_b).transpose(1, 3, 0, 2, 4)
-    slab = lax.all_to_all(slab.reshape(ways, count, own_a * own_b), AXES, 0, 0, tiled=True)
-    slab = slab.reshape(depth, own_a * own_b)
+        functools.partial(slab_kernel, own_b=own_b),
+        "slab",
+        [(full_two, rank), (ways, count, own_a * own_b)],
+        basis_two,
+        mixed,
+        scratch=[(count * rank, own_a * own_b)],
+    )
+    slab = lax.all_to_all(slab, AXES, 0, 0, tiled=True).reshape(depth, own_a * own_b)
     blocks = len(pairs(depth // BLOCK))
     (packed,) = call(pair_kernel, "pair", [(blocks * BLOCK, BLOCK)], slab)
     factor_three, core = pl.pallas_call(
@@ -345,6 +398,8 @@
     ways = ways_one * ways_two
     even = power_of_two(ways_one) and power_of_two(ways_two) and ways_one > 1
     blocks = len(pairs(depth // BLOCK)) * BLOCK
+    even = even and tensor.shape[1] * ways_two == BLOCK and tensor.shape[0] % ways_two == 0
+    even = even and rank * rank == BLOCK * ways and rank // ways_one >= ways_two
     even = even and rank % ways == 0 and depth % ways == 0 and depth % BLOCK == 0
     if even and blocks % (8 * 2 * ways_one) == 0:
         return swift(tensor, start_one, start_two, start_three)

time: 249 us -> 207 us (0.83)
  local copies, waits for them, and re-layouts: 36.2 us -> 11.8 us
  waiting for transfers between devices: 78.8 us -> 57.7 us
  starting transfers between devices: 47.1 us -> 51.8 us
    ppermute x33 -> x38, waiting for transfers between devices: 72 us -> 57.7 us  [swap(): return lax.ppermute(x, axis, [(i, i ^ mask) for i in range(count)])]
    transpose x3 -> x0, local copies, waits for them, and re-layouts: 13.5 us -> none  [the longest x1 9.51 us: regroup(): return x.transpose(2, 0, 3, 1, 4).reshape(count, full_one, full_two)]
    reshape x6 -> x3, local copies, waits for them, and re-layouts: 12 us -> 1.48 us  [the longest x1 0.91 us: swift(): contracted.transpose(2, 0, 3, 1, 4)]
    all_to_all x2, waiting for transfers between devices: 6.72 us -> 0.01 us  [trade(): return lax.all_to_all(x.reshape(shape), AXES, 0, 0, tiled=True)]
    ppermute x33 -> x38, starting transfers between devices: 36.9 us -> 41.8 us  [swap(): return lax.ppermute(x, axis, [(i, i ^ mask) for i in range(count)])]
    pallas_call x1 -> x0, local copies, waits for them, and re-layouts: 3.11 us -> none  [call(): pl.pallas_call(kernel, out_shape=[jax.ShapeDtypeStruct(shape, jnp.float32...]
    unnamed x18 -> x22, local copies, waits for them, and re-layouts: 4.18 us -> 5.38 us
    pallas_call x5 -> x6, Pallas kernels: 39 us -> 38.7 us  [call(): pl.pallas_call(kernel, out_shape=[jax.ShapeDtypeStruct(shape, jnp.float32...]
  transfers between devices with their start and end apart: 35 -> 40, of which waited for: 27 -> 24; matrix products, arithmetic and copies ran while one was open for 4% -> 5% of each run, Pallas kernels for 11% -> 12%
where the time goes in v2:
time: 207 us
  Pallas kernels  58.8 us (28%)
  waiting for transfers between devices  57.7 us (28%)
  starting transfers between devices  51.8 us (25%)
  blocking collectives  15.6 us (8%)
  local copies, waits for them, and re-layouts  11.8 us (6%)
  other arithmetic  6.96 us (3%)
  matrix products  3.02 us (1%)
    ppermute x38, waiting for transfers between devices, swap(): return lax.ppermute(x, axis, [(i, i ^ mask) for i in range(count)])  57.7 us
    ppermute x38, starting transfers between devices, swap(): return lax.ppermute(x, axis, [(i, i ^ mask) for i in range(count)])  41.8 us
    pallas_call x6, Pallas kernels, call(): pl.pallas_call(kernel, out_shape=[jax.ShapeDtypeStruct(shape, jnp.float32...  38.7 us
    pallas_call x1, Pallas kernels, swift(): pl.pallas_call(third_kernel, out_shape=[jax.ShapeDtypeStruct((depth, rank...  20.1 us
    all_to_all x1, blocking collectives, swift(): lax.all_to_all(slab, AXES, 0, 0, tiled=True).reshape(depth, own_a * own_b)  15.6 us
    all_to_all x2, starting transfers between devices, trade(): return lax.all_to_all(x.reshape(shape), AXES, 0, 0, tiled=True)  9.97 us
    unnamed x22, local copies, waits for them, and re-layouts  5.38 us
  transfers between devices with their start and end apart: 40, of which 24 were waited for; matrix products, arithmetic and copies ran while one was open for 5% of the time, Pallas kernels for 12%

profile of v2, /device:TPU:0, one launch (start us, length us, event | category | flops | bytes accessed | tf_op | source)
XLA Modules:
  0.0 206.6 jit_solution(7392267625867643087)
XLA Ops:
  1.2 2.6 %collective-permute-start.14 = (f32[16,64]{1,0:T(8,128)}, f32[16,64]{1,0:T(8,128)S(1)}, u32[]{:S(2)}, u32[]{:S(2)}) collective-permute-start(f32[16,64]{1,0:T(8,128)} %param.5), channel_id=1, source_target_pairs={{0,12},{4,8},{8,4},{12,0},{16,28},{20,24},{24,20},{28,16},{1,13},{... | collective-permute-start | bytes 12296 | tf_op jit(solution)/shard_map/ppermute | solution.py:265
  3.8 1.4 collective-permute-start.12
  6.9 2.5 %collective-permute-start.10 = (f32[16,64]{1,0:T(8,128)}, f32[16,64]{1,0:T(8,128)S(1)}, u32[]{:S(2)}, u32[]{:S(2)}) collective-permute-start(f32[16,64]{1,0:T(8,128)} %param.5), channel_id=1, source_target_pairs={{0,28},{4,24},{8,20},{12,16},{16,12},{20,8},{24,4},{28,0},{1,29},{... | collective-permute-start | bytes 12296 | tf_op jit(solution)/shard_map/ppermute | solution.py:265
  9.6 3.0 %fusion = f32[32,2,512]{2,0,1:T(8,128)S(1)} fusion(f32[512,768,1]{1,0,2:T(8,128)} %bitcast.13, f32[32,2,768]{2,1,0:T(2,128)S(1)} %dot_general.8), kind=kOutput, calls=%fused_computation.7 | convolution fusion | flops 301989888 | bytes 1900544 | tf_op jit(solution)/shard_map/dot_general | solution.py:37
  13.4 6.1 %all-to-all-start = ((f32[32,2,512]{2,1,0:T(2,128)}), f32[32,2,512]{2,1,0:T(2,128)S(1)}, u32[]{:S(2)}, u32[]{:S(2)}) async-start(f32[32,2,512]{2,1,0:T(2,128)} %copy.25), calls=%async_computation | async-start | bytes 262144 | tf_op jit(solution)/shard_map/all_to_all | solution.py:339
  19.5 3.7 %collective-permute-start = (f32[32,64]{1,0:T(8,128)S(1)}, f32[32,64]{1,0:T(8,128)S(1)}, u32[]{:S(2)}, u32[]{:S(2)}) collective-permute-start(f32[32,64]{1,0:T(8,128)S(1)} %copy-done.8), channel_id=1, source_target_pairs={{0,3},{1,2},{2,1},{3,0},{4,7},{5,6},{6,5},{7,4},{8,11},{9,10},{10,... | collective-permute-start | bytes 24584 | tf_op jit(solution)/shard_map/ppermute | solution.py:265
  24.1 2.7 %collective-permute-done = f32[32,64]{1,0:T(8,128)S(1)} collective-permute-done((f32[32,64]{1,0:T(8,128)S(1)}, f32[32,64]{1,0:T(8,128)S(1)}, u32[]{:S(2)}, u32[]{:S(2)}) %collective-permute-start) | collective-permute-done | bytes 8224 | tf_op jit(solution)/shard_map/ppermute | solution.py:265
  30.0 2.2 %open.1 = f32[128,128]{1,0:T(8,128)} custom-call(f32[2,128,128]{2,1,0:T(8,128)} %reshape.30.cont_ref, f32[128,64]{1,0:T(8,128)} %pad_maximum_fusion.4.start_ref), custom_call_target="tpu_custom_call" | custom-call | tf_op jit(solution)/shard_map/open/pallas_call | solution.py:149
  32.2 1.5 collective-permute-done.3
  34.5 1.5 collective-permute-start.5
  36.0 1.5 collective-permute-start.6
  38.8 3.0 %collective-permute-done.6 = f32[128,128]{1,0:T(8,128)S(1)} collective-permute-done((f32[128,128]{1,0:T(8,128)S(1)}, f32[128,128]{1,0:T(8,128)S(1)}, u32[]{:S(2)}, u32[]{:S(2)}) %collective-permute-start.6) | collective-permute-done | bytes 65568 | tf_op jit(solution)/shard_map/ppermute | solution.py:265
  41.8 2.1 %collective-permute-start.8 = (f32[128,128]{1,0:T(8,128)S(1)}, f32[128,128]{1,0:T(8,128)S(1)}, u32[]{:S(2)}, u32[]{:S(2)}) collective-permute-start(f32[128,128]{1,0:T(8,128)S(1)} %add_add_fusion.3), channel_id=1, source_target_pairs={{0,2},{1,3},{2,0},{3,1},{4,6},{5,7},{6,4},{7,5},{8,10},{9,11},{10,... | collective-permute-start | bytes 196616 | tf_op jit(solution)/shard_map/ppermute | solution.py:265
  45.4 2.9 %collective-permute-done.8 = f32[128,128]{1,0:T(8,128)S(1)} collective-permute-done((f32[128,128]{1,0:T(8,128)S(1)}, f32[128,128]{1,0:T(8,128)S(1)}, u32[]{:S(2)}, u32[]{:S(2)}) %collective-permute-start.8) | collective-permute-done | bytes 65568 | tf_op jit(solution)/shard_map/ppermute | solution.py:265
  48.3 1.7 collective-permute-done.9
  50.6 1.7 copy.27
  52.3 3.9 %all-to-all-start.1 = ((f32[32,24,512]{2,1,0:T(8,128)}), f32[32,24,512]{2,1,0:T(8,128)S(1)}, u32[]{:S(2)}, u32[]{:S(2)}) async-start(f32[32,24,512]{2,1,0:T(8,128)} %bitcast.5), calls=%async_computation.1 | async-start | bytes 3145728 | tf_op jit(solution)/shard_map/all_to_all | solution.py:339
  56.2 12.6 %first.1 = (f32[128,64]{1,0:T(8,128)}, f32[128,64]{1,0:T(8,128)}, f32[128,128]{1,0:T(8,128)}) custom-call(f32[128,128]{1,0:T(8,128)} %add_add_fusion.2.gram_ref, f32[128,64]{1,0:T(8,128)} %copy-done.4, f32[2,128,128]{2,1,0:T(8,128)} %reshape.30.cont_ref), custom_call_target="tpu_custom_call" | custom-call | tf_op jit(solution)/shard_map/first/pallas_call | solution.py:149
  68.9 1.4 collective-permute-done.17
  71.1 1.7 collective-permute-start.19
  72.8 1.5 collective-permute-start.20
  74.7 1.3 collective-permute-done.19
  76.0 3.0 %collective-permute-done.20 = f32[128,128]{1,0:T(8,128)S(1)} collective-permute-done((f32[128,128]{1,0:T(8,128)S(1)}, f32[128,128]{1,0:T(8,128)S(1)}, u32[]{:S(2)}, u32[]{:S(2)}) %collective-permute-start.20) | collective-permute-done | bytes 65568 | tf_op jit(solution)/shard_map/ppermute | solution.py:265
  79.0 5.0 %collective-permute-start.22 = (f32[128,128]{1,0:T(8,128)S(1)}, f32[128,128]{1,0:T(8,128)S(1)}, u32[]{:S(2)}, u32[]{:S(2)}) collective-permute-start(f32[128,128]{1,0:T(8,128)S(1)} %add_add_fusion.1), channel_id=1, source_target_pairs={{0,2},{1,3},{2,0},{3,1},{4,6},{5,7},{6,4},{7,5},{8,10},{9,11},{10,... | collective-permute-start | bytes 196616 | tf_op jit(solution)/shard_map/ppermute | solution.py:265
  84.7 13.6 %collective-permute-done.22 = f32[128,128]{1,0:T(8,128)S(1)} collective-permute-done((f32[128,128]{1,0:T(8,128)S(1)}, f32[128,128]{1,0:T(8,128)S(1)}, u32[]{:S(2)}, u32[]{:S(2)}) %collective-permute-start.22) | collective-permute-done | bytes 65568 | tf_op jit(solution)/shard_map/ppermute | solution.py:265
  98.9 11.9 %second.1.right_ref = f32[128,64]{1,0:T(8,128)} custom-call(f32[128,128]{1,0:T(8,128)} %add_add_fusion.gram_ref, f32[128,64]{1,0:T(8,128)} %pad_maximum_fusion.4.start_ref), custom_call_target="tpu_custom_call" | custom-call | tf_op jit(solution)/shard_map/second/pallas_call | solution.py:149
  112.0 5.2 %mix.1.mixed_ref = f32[1536,128]{1,0:T(8,128)} custom-call(f32[128,64]{1,0:T(8,128)} %get-tuple-element.18.factor_ref, f32[32,24,512]{2,1,0:T(8,128)} %copy-done.1), custom_call_target="tpu_custom_call" | custom-call | tf_op jit(solution)/shard_map/mix/pallas_call | solution.py:149
  117.3 3.3 %slab.1 = (f32[128,64]{1,0:T(8,128)}, f32[32,24,128]{2,1,0:T(8,128)}) custom-call(f32[128,64]{1,0:T(8,128)} %second.1.right_ref, f32[1536,128]{1,0:T(8,128)} %mix.1.mixed_ref), custom_call_target="tpu_custom_call" | custom-call | tf_op jit(solution)/shard_map/slab/pallas_call | solution.py:149
  120.6 15.6 %all_to_all.15 = f32[32,24,128]{2,1,0:T(8,128)} all-to-all(f32[32,24,128]{2,1,0:T(8,128)} %get-tuple-element.21), channel_id=1, replica_groups=mesh['row'=8,'col'=4] {'row','col'}, dimensions={0} | all-to-all | bytes 786432 | tf_op jit(solution)/shard_map/all_to_all | solution.py:374
  136.2 3.4 %pair.1 = f32[2688,128]{1,0:T(8,128)} custom-call(f32[768,128]{1,0:T(8,128)} %bitcast.15), custom_call_target="tpu_custom_call" | custom-call | tf_op jit(solution)/shard_map/pair/pallas_call | solution.py:149
  139.6 1.5 slice_select_fusion
  141.1 1.3 collective-permute-start.24
  142.3 1.8 collective-permute-done.24
  146.0 4.9 %collective-permute-done.25 = f32[336,128]{1,0:T(8,128)S(1)} collective-permute-done((f32[336,128]{1,0:T(8,128)S(1)}, f32[336,128]{1,0:T(8,128)S(1)}, u32[]{:S(2)}, u32[]{:S(2)}) %collective-permute-start.25) | collective-permute-done | bytes 172064 | tf_op jit(solution)/shard_map/ppermute | solution.py:265
  152.9 1.3 collective-permute-start.26
  154.1 2.4 %collective-permute-done.32 = f32[168,128]{1,0:T(8,128)S(1)} collective-permute-done((f32[168,128]{1,0:T(8,128)S(1)}, f32[168,128]{1,0:T(8,128)S(1)}, u32[]{:S(2)}, u32[]{:S(2)}) %collective-permute-start.32) | collective-permute-done | bytes 86048 | tf_op jit(solution)/shard_map/ppermute | solution.py:265
  157.5 1.3 collective-permute-start.27
  158.7 2.4 %collective-permute-done.33 = f32[168,128]{1,0:T(8,128)S(1)} collective-permute-done((f32[168,128]{1,0:T(8,128)S(1)}, f32[168,128]{1,0:T(8,128)S(1)}, u32[]{:S(2)}, u32[]{:S(2)}) %collective-permute-start.33) | collective-permute-done | bytes 86048 | tf_op jit(solution)/shard_map/ppermute | solution.py:265
  162.2 2.3 %collective-permute-start.28 = (f32[168,128]{1,0:T(8,128)S(1)}, f32[168,128]{1,0:T(8,128)S(1)}, u32[]{:S(2)}, u32[]{:S(2)}) collective-permute-start(f32[168,128]{1,0:T(8,128)S(1)} %add.86), channel_id=1, source_target_pairs={{0,2},{1,3},{2,0},{3,1},{4,6},{5,7},{6,4},{7,5},{8,10},{9,11},{10,... | collective-permute-start | bytes 258056 | tf_op jit(solution)/shard_map/ppermute | solution.py:265
  164.5 3.0 %collective-permute-done.34 = f32[168,128]{1,0:T(8,128)S(1)} collective-permute-done((f32[168,128]{1,0:T(8,128)S(1)}, f32[168,128]{1,0:T(8,128)S(1)}, u32[]{:S(2)}, u32[]{:S(2)}) %collective-permute-start.34) | collective-permute-done | bytes 86048 | tf_op jit(solution)/shard_map/ppermute | solution.py:265
  167.6 1.7 collective-permute-done.28
  170.3 2.3 %collective-permute-done.35 = f32[168,128]{1,0:T(8,128)S(1)} collective-permute-done((f32[168,128]{1,0:T(8,128)S(1)}, f32[168,128]{1,0:T(8,128)S(1)}, u32[]{:S(2)}, u32[]{:S(2)}) %collective-permute-start.35) | collective-permute-done | bytes 86048 | tf_op jit(solution)/shard_map/ppermute | solution.py:265
  173.9 1.3 collective-permute-start.30
  175.3 2.8 %collective-permute-done.36 = f32[336,128]{1,0:T(8,128)S(1)} collective-permute-done((f32[336,128]{1,0:T(8,128)S(1)}, f32[336,128]{1,0:T(8,128)S(1)}, u32[]{:S(2)}, u32[]{:S(2)}) %collective-permute-start.36) | collective-permute-done | bytes 172064 | tf_op jit(solution)/shard_map/ppermute | solution.py:265
  178.1 1.3 collective-permute-done.30
  183.2 20.1 %third.1 = (f32[768,64]{1,0:T(8,128)}, f32[64,128]{1,0:T(8,128)}) custom-call(f32[2688,128]{1,0:T(8,128)} %pad_maximum_fusion.packed_ref, f32[768,64]{1,0:T(8,128)} %copy.28.start_ref, f32[768,128]{1,0:T(8,128)} %bitcast.16), custom_call_target="tpu_custom_call" | custom-call | tf_op jit(solution)/shard_map/third/pallas_call | solution.py:377
  203.3 1.8 copy.32
  205.1 1.5 copy.29
  (107 shorter events, 27.4 us)
Async XLA Ops:
  0.6 6.3 %collective-permute-start.16 = (f32[16,64]{1,0:T(8,128)}, f32[16,64]{1,0:T(8,128)S(1)}, u32[]{:S(2)}, u32[]{:S(2)}) collective-permute-start(f32[16,64]{1,0:T(8,128)} %param.5), channel_id=1, source_target_pairs={{0,4},{4,0},{8,12},{12,8},{16,20},{20,16},{24,28},{28,24},{1,5},{5... | collective-permute-start | bytes 12296 | tf_op jit(solution)/shard_map/ppermute | solution.py:265
  1.2 8.2 %collective-permute-start.14 = (f32[16,64]{1,0:T(8,128)}, f32[16,64]{1,0:T(8,128)S(1)}, u32[]{:S(2)}, u32[]{:S(2)}) collective-permute-start(f32[16,64]{1,0:T(8,128)} %param.5), channel_id=1, source_target_pairs={{0,12},{4,8},{8,4},{12,0},{16,28},{20,24},{24,20},{28,16},{1,13},{... | collective-permute-start | bytes 12296 | tf_op jit(solution)/shard_map/ppermute | solution.py:265
  3.8 15.7 %collective-permute-start.15 = (f32[16,64]{1,0:T(8,128)}, f32[16,64]{1,0:T(8,128)S(1)}, u32[]{:S(2)}, u32[]{:S(2)}) collective-permute-start(f32[16,64]{1,0:T(8,128)} %param.5), channel_id=1, source_target_pairs={{0,8},{4,12},{8,0},{12,4},{16,24},{20,28},{24,16},{28,20},{1,9},{5... | collective-permute-start | bytes 12296 | tf_op jit(solution)/shard_map/ppermute | solution.py:265
  3.8 19.4 %collective-permute-start.12 = (f32[16,64]{1,0:T(8,128)}, f32[16,64]{1,0:T(8,128)S(1)}, u32[]{:S(2)}, u32[]{:S(2)}) collective-permute-start(f32[16,64]{1,0:T(8,128)} %param.5), channel_id=1, source_target_pairs={{0,20},{4,16},{8,28},{12,24},{16,4},{20,0},{24,12},{28,8},{1,21},{... | collective-permute-start | bytes 12296 | tf_op jit(solution)/shard_map/ppermute | solution.py:265
  5.2 18.0 %collective-permute-start.13 = (f32[16,64]{1,0:T(8,128)}, f32[16,64]{1,0:T(8,128)S(1)}, u32[]{:S(2)}, u32[]{:S(2)}) collective-permute-start(f32[16,64]{1,0:T(8,128)} %param.5), channel_id=1, source_target_pairs={{0,16},{4,20},{8,24},{12,28},{16,0},{20,4},{24,8},{28,12},{1,17},{... | collective-permute-start | bytes 12296 | tf_op jit(solution)/shard_map/ppermute | solution.py:265
  5.8 13.7 %copy-start.8 = (f32[32,64]{1,0:T(8,128)S(1)}, f32[32,64]{1,0:T(8,128)}, u32[]{:S(2)}) copy-start(f32[32,64]{1,0:T(8,128)} %param.6) | copy-start | bytes 24580
  5.8 18.2 %copy-start.7 = (f32[16,64]{1,0:T(8,128)S(1)}, f32[16,64]{1,0:T(8,128)}, u32[]{:S(2)}) copy-start(f32[16,64]{1,0:T(8,128)} %param.5) | copy-start | bytes 12292
  6.9 17.1 %collective-permute-start.10 = (f32[16,64]{1,0:T(8,128)}, f32[16,64]{1,0:T(8,128)S(1)}, u32[]{:S(2)}, u32[]{:S(2)}) collective-permute-start(f32[16,64]{1,0:T(8,128)} %param.5), channel_id=1, source_target_pairs={{0,28},{4,24},{8,20},{12,16},{16,12},{20,8},{24,4},{28,0},{1,29},{... | collective-permute-start | bytes 12296 | tf_op jit(solution)/shard_map/ppermute | solution.py:265
  9.4 14.6 %collective-permute-start.11 = (f32[16,64]{1,0:T(8,128)}, f32[16,64]{1,0:T(8,128)S(1)}, u32[]{:S(2)}, u32[]{:S(2)}) collective-permute-start(f32[16,64]{1,0:T(8,128)} %param.5), channel_id=1, source_target_pairs={{0,24},{4,28},{8,16},{12,20},{16,8},{20,12},{24,0},{28,4},{1,25},{... | collective-permute-start | bytes 12296 | tf_op jit(solution)/shard_map/ppermute | solution.py:265
  13.4 15.1 %all-to-all-start = ((f32[32,2,512]{2,1,0:T(2,128)}), f32[32,2,512]{2,1,0:T(2,128)S(1)}, u32[]{:S(2)}, u32[]{:S(2)}) async-start(f32[32,2,512]{2,1,0:T(2,128)} %copy.25), calls=%async_computation | async-start | bytes 262144 | tf_op jit(solution)/shard_map/all_to_all | solution.py:339
  19.5 7.3 %collective-permute-start = (f32[32,64]{1,0:T(8,128)S(1)}, f32[32,64]{1,0:T(8,128)S(1)}, u32[]{:S(2)}, u32[]{:S(2)}) collective-permute-start(f32[32,64]{1,0:T(8,128)S(1)} %copy-done.8), channel_id=1, source_target_pairs={{0,3},{1,2},{2,1},{3,0},{4,7},{5,6},{6,5},{7,4},{8,11},{9,10},{10,... | collective-permute-start | bytes 24584 | tf_op jit(solution)/shard_map/ppermute | solution.py:265
  23.2 4.6 %collective-permute-start.1 = (f32[32,64]{1,0:T(8,128)S(1)}, f32[32,64]{1,0:T(8,128)S(1)}, u32[]{:S(2)}, u32[]{:S(2)}) collective-permute-start(f32[32,64]{1,0:T(8,128)S(1)} %copy-done.8), channel_id=1, source_target_pairs={{0,2},{1,3},{2,0},{3,1},{4,6},{5,7},{6,4},{7,5},{8,10},{9,11},{10,... | collective-permute-start | bytes 24584 | tf_op jit(solution)/shard_map/ppermute | solution.py:265
  23.2 4.6 %collective-permute-start.2 = (f32[32,64]{1,0:T(8,128)S(1)}, f32[32,64]{1,0:T(8,128)S(1)}, u32[]{:S(2)}, u32[]{:S(2)}) collective-permute-start(f32[32,64]{1,0:T(8,128)S(1)} %copy-done.8), channel_id=1, source_target_pairs={{0,1},{1,0},{2,3},{3,2},{4,5},{5,4},{6,7},{7,6},{8,9},{9,8},{10,11... | collective-permute-start | bytes 24584 | tf_op jit(solution)/shard_map/ppermute | solution.py:265
  28.7 21.9 %copy-start.2 = (f32[16,32,768]{2,1,0:T(8,128)S(1)}, f32[16,32,768]{2,1,0:T(8,128)}, u32[]{:S(2)}) copy-start(f32[16,32,768]{2,1,0:T(8,128)} %param.4) | copy-start | bytes 4718596
  32.2 1.5 collective-permute-start.3
  34.5 4.3 %collective-permute-start.5 = (f32[128,128]{1,0:T(8,128)S(1)}, f32[128,128]{1,0:T(8,128)S(1)}, u32[]{:S(2)}, u32[]{:S(2)}) collective-permute-start(f32[128,128]{1,0:T(8,128)S(1)} %add.69), channel_id=1, source_target_pairs={{0,16},{4,20},{8,24},{12,28},{16,0},{20,4},{24,8},{28,12},{1,17},{... | collective-permute-start | bytes 196616 | tf_op jit(solution)/shard_map/ppermute | solution.py:265
  36.0 5.8 %collective-permute-start.6 = (f32[128,128]{1,0:T(8,128)S(1)}, f32[128,128]{1,0:T(8,128)S(1)}, u32[]{:S(2)}, u32[]{:S(2)}) collective-permute-start(f32[128,128]{1,0:T(8,128)S(1)} %add.69), channel_id=1, source_target_pairs={{0,24},{4,28},{8,16},{12,20},{16,8},{20,12},{24,0},{28,4},{1,25},{... | collective-permute-start | bytes 196616 | tf_op jit(solution)/shard_map/ppermute | solution.py:265
  37.5 4.3 %collective-permute-start.4 = (f32[128,128]{1,0:T(8,128)S(1)}, f32[128,128]{1,0:T(8,128)S(1)}, u32[]{:S(2)}, u32[]{:S(2)}) collective-permute-start(f32[128,128]{1,0:T(8,128)S(1)} %add.69), channel_id=1, source_target_pairs={{0,8},{4,12},{8,0},{12,4},{16,24},{20,28},{24,16},{28,20},{1,9},{5... | collective-permute-start | bytes 196616 | tf_op jit(solution)/shard_map/ppermute | solution.py:265
  41.8 6.5 %collective-permute-start.8 = (f32[128,128]{1,0:T(8,128)S(1)}, f32[128,128]{1,0:T(8,128)S(1)}, u32[]{:S(2)}, u32[]{:S(2)}) collective-permute-start(f32[128,128]{1,0:T(8,128)S(1)} %add_add_fusion.3), channel_id=1, source_target_pairs={{0,2},{1,3},{2,0},{3,1},{4,6},{5,7},{6,4},{7,5},{8,10},{9,11},{10,... | collective-permute-start | bytes 196616 | tf_op jit(solution)/shard_map/ppermute | solution.py:265
  43.9 6.1 %collective-permute-start.9 = (f32[128,128]{1,0:T(8,128)S(1)}, f32[128,128]{1,0:T(8,128)S(1)}, u32[]{:S(2)}, u32[]{:S(2)}) collective-permute-start(f32[128,128]{1,0:T(8,128)S(1)} %add_add_fusion.3), channel_id=1, source_target_pairs={{0,3},{1,2},{2,1},{3,0},{4,7},{5,6},{6,5},{7,4},{8,11},{9,10},{10,... | collective-permute-start | bytes 196616 | tf_op jit(solution)/shard_map/ppermute | solution.py:265
  44.4 5.6 %collective-permute-start.7 = (f32[128,128]{1,0:T(8,128)S(1)}, f32[128,128]{1,0:T(8,128)S(1)}, u32[]{:S(2)}, u32[]{:S(2)}) collective-permute-start(f32[128,128]{1,0:T(8,128)S(1)} %add_add_fusion.3), channel_id=1, source_target_pairs={{0,1},{1,0},{2,3},{3,2},{4,5},{5,4},{6,7},{7,6},{8,9},{9,8},{10,11... | collective-permute-start | bytes 196616 | tf_op jit(solution)/shard_map/ppermute | solution.py:265
  45.4 6.9 %copy-start.4 = (f32[128,64]{1,0:T(8,128)}, f32[128,64]{1,0:T(8,128)S(1)}, u32[]{:S(2)}) copy-start(f32[128,64]{1,0:T(8,128)S(1)} %constant_dynamic-update-slice_fusion.start_ref) | copy-start | bytes 98308
  52.3 58.6 %all-to-all-start.1 = ((f32[32,24,512]{2,1,0:T(8,128)}), f32[32,24,512]{2,1,0:T(8,128)S(1)}, u32[]{:S(2)}, u32[]{:S(2)}) async-start(f32[32,24,512]{2,1,0:T(8,128)} %bitcast.5), calls=%async_computation.1 | async-start | bytes 3145728 | tf_op jit(solution)/shard_map/all_to_all | solution.py:339
  68.8 1.5 collective-permute-start.17
  71.1 4.9 %collective-permute-start.19 = (f32[128,128]{1,0:T(8,128)S(1)}, f32[128,128]{1,0:T(8,128)S(1)}, u32[]{:S(2)}, u32[]{:S(2)}) collective-permute-start(f32[128,128]{1,0:T(8,128)S(1)} %add.76), channel_id=1, source_target_pairs={{0,16},{4,20},{8,24},{12,28},{16,0},{20,4},{24,8},{28,12},{1,17},{... | collective-permute-start | bytes 196616 | tf_op jit(solution)/shard_map/ppermute | solution.py:265
  72.8 6.2 %collective-permute-start.20 = (f32[128,128]{1,0:T(8,128)S(1)}, f32[128,128]{1,0:T(8,128)S(1)}, u32[]{:S(2)}, u32[]{:S(2)}) collective-permute-start(f32[128,128]{1,0:T(8,128)S(1)} %add.76), channel_id=1, source_target_pairs={{0,24},{4,28},{8,16},{12,20},{16,8},{20,12},{24,0},{28,4},{1,25},{... | collective-permute-start | bytes 196616 | tf_op jit(solution)/shard_map/ppermute | solution.py:265
  74.2 4.7 %collective-permute-start.18 = (f32[128,128]{1,0:T(8,128)S(1)}, f32[128,128]{1,0:T(8,128)S(1)}, u32[]{:S(2)}, u32[]{:S(2)}) collective-permute-start(f32[128,128]{1,0:T(8,128)S(1)} %add.76), channel_id=1, source_target_pairs={{0,8},{4,12},{8,0},{12,4},{16,24},{20,28},{24,16},{28,20},{1,9},{5... | collective-permute-start | bytes 196616 | tf_op jit(solution)/shard_map/ppermute | solution.py:265
  79.0 19.2 %collective-permute-start.22 = (f32[128,128]{1,0:T(8,128)S(1)}, f32[128,128]{1,0:T(8,128)S(1)}, u32[]{:S(2)}, u32[]{:S(2)}) collective-permute-start(f32[128,128]{1,0:T(8,128)S(1)} %add_add_fusion.1), channel_id=1, source_target_pairs={{0,2},{1,3},{2,0},{3,1},{4,6},{5,7},{6,4},{7,5},{8,10},{9,11},{10,... | collective-permute-start | bytes 196616 | tf_op jit(solution)/shard_map/ppermute | solution.py:265
  84.0 14.2 %collective-permute-start.23 = (f32[128,128]{1,0:T(8,128)S(1)}, f32[128,128]{1,0:T(8,128)S(1)}, u32[]{:S(2)}, u32[]{:S(2)}) collective-permute-start(f32[128,128]{1,0:T(8,128)S(1)} %add_add_fusion.1), channel_id=1, source_target_pairs={{0,3},{1,2},{2,1},{3,0},{4,7},{5,6},{6,5},{7,4},{8,11},{9,10},{10,... | collective-permute-start | bytes 196616 | tf_op jit(solution)/shard_map/ppermute | solution.py:265
  84.1 14.1 %collective-permute-start.21 = (f32[128,128]{1,0:T(8,128)S(1)}, f32[128,128]{1,0:T(8,128)S(1)}, u32[]{:S(2)}, u32[]{:S(2)}) collective-permute-start(f32[128,128]{1,0:T(8,128)S(1)} %add_add_fusion.1), channel_id=1, source_target_pairs={{0,1},{1,0},{2,3},{3,2},{4,5},{5,4},{6,7},{7,6},{8,9},{9,8},{10,11... | collective-permute-start | bytes 196616 | tf_op jit(solution)/shard_map/ppermute | solution.py:265
  139.6 4.5 %copy-start = (f32[2688,128]{1,0:T(8,128)S(1)}, f32[2688,128]{1,0:T(8,128)}, u32[]{:S(2)}) copy-start(f32[2688,128]{1,0:T(8,128)} %pair.1) | copy-start | bytes 4128772
  141.1 3.0 %collective-permute-start.24 = (f32[1344,128]{1,0:T(8,128)S(1)}, f32[1344,128]{1,0:T(8,128)S(1)}, u32[]{:S(2)}, u32[]{:S(2)}) collective-permute-start(f32[1344,128]{1,0:T(8,128)S(1)} %slice_select_fusion), channel_id=1, source_target_pairs={{0,4},{4,0},{8,12},{12,8},{16,20},{20,16},{24,28},{28,24},{1,5},{5... | collective-permute-start | bytes 2064392 | tf_op jit(solution)/shard_map/ppermute | solution.py:265
  144.3 6.7 %collective-permute-start.25 = (f32[336,128]{1,0:T(8,128)S(1)}, f32[336,128]{1,0:T(8,128)S(1)}, u32[]{:S(2)}, u32[]{:S(2)}) collective-permute-start(f32[336,128]{1,0:T(8,128)S(1)} %get-tuple-element.50), channel_id=1, source_target_pairs={{0,8},{4,12},{8,0},{12,4},{16,24},{20,28},{24,16},{28,20},{1,9},{5... | collective-permute-start | bytes 516104 | tf_op jit(solution)/shard_map/ppermute | solution.py:265
  145.5 6.4 %collective-permute-start.31 = (f32[336,128]{1,0:T(8,128)S(1)}, f32[336,128]{1,0:T(8,128)S(1)}, u32[]{:S(2)}, u32[]{:S(2)}) collective-permute-start(f32[336,128]{1,0:T(8,128)S(1)} %get-tuple-element.51), channel_id=1, source_target_pairs={{0,16},{4,20},{8,24},{12,28},{16,0},{20,4},{24,8},{28,12},{1,17},{... | collective-permute-start | bytes 516104 | tf_op jit(solution)/shard_map/ppermute | solution.py:265
  152.0 4.6 %collective-permute-start.32 = (f32[168,128]{1,0:T(8,128)S(1)}, f32[168,128]{1,0:T(8,128)S(1)}, u32[]{:S(2)}, u32[]{:S(2)}) collective-permute-start(f32[168,128]{1,0:T(8,128)S(1)} %slice_select_fusion.3), channel_id=1, source_target_pairs={{0,8},{4,12},{8,0},{12,4},{16,24},{20,28},{24,16},{28,20},{1,9},{5... | collective-permute-start | bytes 258056 | tf_op jit(solution)/shard_map/ppermute | solution.py:265
  152.9 4.6 %collective-permute-start.26 = (f32[168,128]{1,0:T(8,128)S(1)}, f32[168,128]{1,0:T(8,128)S(1)}, u32[]{:S(2)}, u32[]{:S(2)}) collective-permute-start(f32[168,128]{1,0:T(8,128)S(1)} %slice_select_fusion.4), channel_id=1, source_target_pairs={{0,16},{4,20},{8,24},{12,28},{16,0},{20,4},{24,8},{28,12},{1,17},{... | collective-permute-start | bytes 258056 | tf_op jit(solution)/shard_map/ppermute | solution.py:265
  156.5 4.5 %collective-permute-start.33 = (f32[168,128]{1,0:T(8,128)S(1)}, f32[168,128]{1,0:T(8,128)S(1)}, u32[]{:S(2)}, u32[]{:S(2)}) collective-permute-start(f32[168,128]{1,0:T(8,128)S(1)} %select_add_fusion.3), channel_id=1, source_target_pairs={{0,1},{1,0},{2,3},{3,2},{4,5},{5,4},{6,7},{7,6},{8,9},{9,8},{10,11... | collective-permute-start | bytes 258056 | tf_op jit(solution)/shard_map/ppermute | solution.py:265
  157.5 4.7 %collective-permute-start.27 = (f32[168,128]{1,0:T(8,128)S(1)}, f32[168,128]{1,0:T(8,128)S(1)}, u32[]{:S(2)}, u32[]{:S(2)}) collective-permute-start(f32[168,128]{1,0:T(8,128)S(1)} %select_add_fusion.4), channel_id=1, source_target_pairs={{0,1},{1,0},{2,3},{3,2},{4,5},{5,4},{6,7},{7,6},{8,9},{9,8},{10,11... | collective-permute-start | bytes 258056 | tf_op jit(solution)/shard_map/ppermute | solution.py:265
  161.1 6.4 %collective-permute-start.34 = (f32[168,128]{1,0:T(8,128)S(1)}, f32[168,128]{1,0:T(8,128)S(1)}, u32[]{:S(2)}, u32[]{:S(2)}) collective-permute-start(f32[168,128]{1,0:T(8,128)S(1)} %add.90), channel_id=1, source_target_pairs={{0,2},{1,3},{2,0},{3,1},{4,6},{5,7},{6,4},{7,5},{8,10},{9,11},{10,... | collective-permute-start | bytes 258056 | tf_op jit(solution)/shard_map/ppermute | solution.py:265
  162.2 7.2 %collective-permute-start.28 = (f32[168,128]{1,0:T(8,128)S(1)}, f32[168,128]{1,0:T(8,128)S(1)}, u32[]{:S(2)}, u32[]{:S(2)}) collective-permute-start(f32[168,128]{1,0:T(8,128)S(1)} %add.86), channel_id=1, source_target_pairs={{0,2},{1,3},{2,0},{3,1},{4,6},{5,7},{6,4},{7,5},{8,10},{9,11},{10,... | collective-permute-start | bytes 258056 | tf_op jit(solution)/shard_map/ppermute | solution.py:265
  167.5 5.1 %collective-permute-start.35 = (f32[168,128]{1,0:T(8,128)S(1)}, f32[168,128]{1,0:T(8,128)S(1)}, u32[]{:S(2)}, u32[]{:S(2)}) collective-permute-start(f32[168,128]{1,0:T(8,128)S(1)} %add.91), channel_id=1, source_target_pairs={{0,8},{4,12},{8,0},{12,4},{16,24},{20,28},{24,16},{28,20},{1,9},{5... | collective-permute-start | bytes 258056 | tf_op jit(solution)/shard_map/ppermute | solution.py:265
  169.3 4.6 %collective-permute-start.29 = (f32[168,128]{1,0:T(8,128)S(1)}, f32[168,128]{1,0:T(8,128)S(1)}, u32[]{:S(2)}, u32[]{:S(2)}) collective-permute-start(f32[168,128]{1,0:T(8,128)S(1)} %add.87), channel_id=1, source_target_pairs={{0,16},{4,20},{8,24},{12,28},{16,0},{20,4},{24,8},{28,12},{1,17},{... | collective-permute-start | bytes 258056 | tf_op jit(solution)/shard_map/ppermute | solution.py:265
  172.6 5.5 %collective-permute-start.36 = (f32[336,128]{1,0:T(8,128)S(1)}, f32[336,128]{1,0:T(8,128)S(1)}, u32[]{:S(2)}, u32[]{:S(2)}) collective-permute-start(f32[336,128]{1,0:T(8,128)S(1)} %pad_maximum_fusion.3), channel_id=1, source_target_pairs={{0,16},{4,20},{8,24},{12,28},{16,0},{20,4},{24,8},{28,12},{1,17},{... | collective-permute-start | bytes 516104 | tf_op jit(solution)/shard_map/ppermute | solution.py:265
  173.9 5.7 %copy-start.3 = (f32[768,64]{0,1:T(8,128)S(1)}, f32[768,64]{0,1:T(8,128)}, u32[]{:S(2)}) copy-start(f32[768,64]{0,1:T(8,128)} %param.7) | copy-start | bytes 589828
  173.9 5.5 %collective-permute-start.30 = (f32[336,128]{1,0:T(8,128)S(1)}, f32[336,128]{1,0:T(8,128)S(1)}, u32[]{:S(2)}, u32[]{:S(2)}) collective-permute-start(f32[336,128]{1,0:T(8,128)S(1)} %pad_maximum_fusion.2), channel_id=1, source_target_pairs={{0,8},{4,12},{8,0},{12,4},{16,24},{20,28},{24,16},{28,20},{1,9},{5... | collective-permute-start | bytes 516104 | tf_op jit(solution)/shard_map/ppermute | solution.py:265
  178.1 2.4 %copy-start.5 = (f32[128,64]{1,0:T(8,128)S(1)}, f32[128,64]{1,0:T(8,128)}, u32[]{:S(2)}) copy-start(f32[128,64]{1,0:T(8,128)} %get-tuple-element.32) | copy-start | bytes 98308
  178.1 3.1 %copy-start.6 = (f32[128,64]{1,0:T(8,128)S(1)}, f32[128,64]{1,0:T(8,128)}, u32[]{:S(2)}) copy-start(f32[128,64]{1,0:T(8,128)} %get-tuple-element.33) | copy-start | bytes 98308
  179.5 2.4 %collective-permute-start.37 = (f32[1344,128]{1,0:T(8,128)S(1)}, f32[1344,128]{1,0:T(8,128)S(1)}, u32[]{:S(2)}, u32[]{:S(2)}) collective-permute-start(f32[1344,128]{1,0:T(8,128)S(1)} %pad_maximum_fusion.1), channel_id=1, source_target_pairs={{0,4},{4,0},{8,12},{12,8},{16,20},{20,16},{24,28},{28,24},{1,5},{5... | collective-permute-start | bytes 2064392 | tf_op jit(solution)/shard_map/ppermute | solution.py:265
  (1 other events, 1.2 us)

commit v3 on v2

--- a/solution.py
+++ b/solution.py
@@ -87,7 +87,7 @@
 
 
 def settle_kernel(gram_ref, start_ref, out_ref):
-    out_ref[...] = iterate(gram_ref[...], start_ref[...])
+    out_ref[...] = iterate(gram_ref[...], start_ref[...].T).T
 
 
 def settle(gram_whole, basis):
@@ -156,16 +156,32 @@
     )(*args)
 
 
-def iterate(gram, start):
-    size = start.shape[0]
+def pieces(x):
+    high = x.astype(jnp.bfloat16)
+    rest = x - high.astype(jnp.float32)
+    middle = rest.astype(jnp.bfloat16)
+    low = (rest - middle.astype(jnp.float32)).astype(jnp.bfloat16)
+    return high, middle, low
+
+
+def iterate(gram, turned):
+    rank, size = turned.shape
     extra = -size % WIDE
-    gram = jnp.pad(gram, ((0, extra), (0, extra)))
+    high, middle, low = pieces(jnp.pad(gram, ((0, extra), (0, extra))))
+
+    def times(parts, matrix):
+        whole = jnp.dot(jnp.concatenate(parts, axis=0), matrix, preferred_element_type=jnp.float32)
+        return [whole[n * rank : (n + 1) * rank] for n in range(len(parts))]
 
     def step(_, turned):
-        image = product(turned, gram)
+        top, mid, end = pieces(turned)
+        first = times([top, mid, end], high)
+        second = times([top, mid], middle)
+        (third,) = times([top], low)
+        image = first[0] + ((first[1] + second[0]) + ((first[2] + second[1]) + third))
         return product(lower_inverse(right_product(image, image)), image)
 
-    return lax.fori_loop(0, STEPS, step, jnp.pad(start.T, ((0, 0), (0, extra))))[:, :size].T
+    return lax.fori_loop(0, STEPS, step, jnp.pad(turned, ((0, 0), (0, extra))))[:, :size]
 
 
 def gram_of(slabs):
@@ -181,16 +197,18 @@
 
 
 def first_kernel(gram_ref, start_ref, cont_ref, basis_ref, factor_ref, next_ref):
-    basis = iterate(gram_ref[...], start_ref[...])
+    turned = iterate(gram_ref[...], start_ref[...].T)
+    factor_ref[...] = turned * math.sqrt(turned.shape[1])
+    basis = turned.T
     basis_ref[...] = basis
-    factor_ref[...] = basis * math.sqrt(basis.shape[0])
     slabs = [left_product(cont_ref[c], basis) for c in range(cont_ref.shape[0])]
     next_ref[...] = gram_of(slabs)
 
 
-def second_kernel(gram_ref, start_ref, factor_ref):
-    basis = iterate(gram_ref[...], start_ref[...])
-    factor_ref[...] = basis
+def second_kernel(gram_ref, start_ref, basis_ref, factor_ref):
+    turned = iterate(gram_ref[...], start_ref[...].T)
+    factor_ref[...] = turned * math.sqrt(turned.shape[1])
+    basis_ref[...] = turned.T
 
 
 def mix_kernel(factor_ref, cells_ref, mixed_ref, turn_ref, groups):
@@ -218,9 +236,8 @@
         )
 
 
-def slab_kernel(right_ref, mixed_ref, factor_ref, slab_ref, turn_ref, own_b):
+def slab_kernel(right_ref, mixed_ref, slab_ref, turn_ref, own_b):
     right = right_ref[...]
-    factor_ref[...] = right * math.sqrt(right.shape[0])
     count, width = slab_ref.shape[1:]
     rank = right.shape[1]
     own_a, ways_two = width // own_b, rank // own_b
@@ -255,9 +272,9 @@
         gram_ref[j * BLOCK : (j + 1) * BLOCK, i * BLOCK : (i + 1) * BLOCK] = block
         if i != j:
             gram_ref[i * BLOCK : (i + 1) * BLOCK, j * BLOCK : (j + 1) * BLOCK] = block.T
-    basis = iterate(gram_ref[...], start_ref[...])
-    factor_ref[...] = basis * math.sqrt(basis.shape[0])
-    core_ref[...] = left_product(basis, slab_ref[...])
+    turned = iterate(gram_ref[...], start_ref[...])
+    factor_ref[...] = turned * math.sqrt(turned.shape[1])
+    core_ref[...] = product(turned, slab_ref[...]).T
 
 
 def swap(x, axis, mask):
@@ -303,6 +320,14 @@
         parts = [jnp.where(upper, parts[i ^ mask], parts[i]) for i in range(count)]
         mask *= 2
     return jnp.concatenate(parts, axis=0)
+
+
+def gather_rows(x, axis):
+    mask = 1
+    while mask < lax.axis_size(axis):
+        x = double(x, axis, mask)
+        mask *= 2
+    return x
 
 
 def sum_large(x):
@@ -331,14 +356,16 @@
     ways = ways_one * ways_two
     full_one, full_two = rows_one * ways_one, rows_two * ways_two
     flat = tensor.reshape(rows_one * rows_two, depth)
-    two = spread_rows(start_two, "col")
-    one = spread_rows(start_one, "row")
 
     def trade(x):
         shape = (ways, x.shape[0] // ways, x.shape[1])
         return lax.all_to_all(x.reshape(shape), AXES, 0, 0, tiled=True)
 
-    contracted = trade(cross_product(start_three, flat))
+    local = cross_product(start_three, flat)
+    local, start_one, start_two = lax.optimization_barrier((local, start_one, start_two))
+    two = spread_rows(start_two, "col")
+    one = gather_rows(start_one, "row")
+    contracted = trade(local)
     contracted = contracted.reshape(ways_one, ways_two, rank // ways, rows_one, rows_two)
     contracted = contracted.transpose(2, 0, 3, 1, 4).reshape(rank // ways, full_one, full_two)
     (gram,) = call(open_kernel, "open", [(full_one, full_one)], contracted, two)
@@ -347,12 +374,14 @@
     basis_one, factor_one, gram = call(
         first_kernel,
         "first",
-        [(full_one, rank), (full_one, rank), (full_two, full_two)],
+        [(full_one, rank), (rank, full_one), (full_two, full_two)],
         gram,
         one,
         contracted,
     )
-    (basis_two,) = call(second_kernel, "second", [(full_two, rank)], sum_small(gram), two)
+    basis_two, factor_two = call(
+        second_kernel, "second", [(full_two, rank), (rank, full_two)], sum_small(gram), two
+    )
     count = depth // ways
     (mixed,) = call(
         functools.partial(mix_kernel, groups=ways_two),
@@ -363,10 +392,10 @@
         scratch=[(count * full_one, full_two)],
     )
     own_a, own_b = rank // ways_one, rank // ways_two
-    factor_two, slab = call(
+    (slab,) = call(
         functools.partial(slab_kernel, own_b=own_b),
         "slab",
-        [(full_two, rank), (ways, count, own_a * own_b)],
+        [(ways, count, own_a * own_b)],
         basis_two,
         mixed,
         scratch=[(count * rank, own_a * own_b)],
@@ -377,15 +406,15 @@
     factor_three, core = pl.pallas_call(
         third_kernel,
         out_shape=[
-            jax.ShapeDtypeStruct((depth, rank), jnp.float32),
-            jax.ShapeDtypeStruct((rank, own_a * own_b), jnp.float32),
+            jax.ShapeDtypeStruct((rank, depth), jnp.float32),
+            jax.ShapeDtypeStruct((own_a * own_b, rank), jnp.float32),
         ],
         in_specs=[VMEM] * 3,
         out_specs=[VMEM] * 2,
         scratch_shapes=[pltpu.VMEM((depth, depth), jnp.float32)],
         name="third",
-    )(sum_large(packed), start_three, slab)
-    return (factor_one, factor_two, factor_three, core.reshape(rank, own_a, own_b))
+    )(sum_large(packed), start_three.T, slab)
+    return (factor_one.T, factor_two.T, factor_three.T, core.T.reshape(rank, own_a, own_b))
 
 
 def power_of_two(value):

time: 207 us -> 194 us (0.937)
  local copies, waits for them, and re-layouts: 11.8 us -> 4.88 us
  starting transfers between devices: 51.8 us -> 47.5 us
  Pallas kernels: 58.8 us -> 55.9 us
    all_to_all x2, waiting for transfers between devices: 0.01 us -> 4.51 us  [trade(): return lax.all_to_all(x.reshape(shape), AXES, 0, 0, tiled=True)]
    unnamed x22 -> x12, local copies, waits for them, and re-layouts: 5.38 us -> 1.2 us
    ppermute x38 -> x34, waiting for transfers between devices: 57.7 us -> 54.2 us  [swap(): return lax.ppermute(x, axis, [(i, i ^ mask) for i in range(count)])]
    ppermute x38 -> x34, starting transfers between devices: 41.8 us -> 38.3 us  [swap(): return lax.ppermute(x, axis, [(i, i ^ mask) for i in range(count)])]
    pallas_call x1, Pallas kernels: 20.1 us -> 17.2 us  [swift(): pl.pallas_call(third_kernel, out_shape=[jax.ShapeDtypeStruct((rank, depth...]
    reshape x0 -> x2, local copies, waits for them, and re-layouts: none -> 2.37 us  [the longest x1 1.65 us: swift(): flat = tensor.reshape(rows_one * rows_two, depth)]
  transfers between devices with their start and end apart: 40 -> 36, of which waited for: 24 -> 24; matrix products, arithmetic and copies ran while one was open for 5% -> 3% of each run, Pallas kernels for 12% -> 13%
where the time goes in v3:
time: 194 us; the launch traced here: 193 us
  waiting for transfers between devices  58.7 us (30%)
  Pallas kernels  55.9 us (29%)
  starting transfers between devices  47.5 us (24%)
  blocking collectives  15.6 us (8%)
  other arithmetic  6.75 us (3%)
  local copies, waits for them, and re-layouts  4.88 us (3%)
  matrix products  3.15 us (2%)
    ppermute x34, waiting for transfers between devices, swap(): return lax.ppermute(x, axis, [(i, i ^ mask) for i in range(count)])  54.2 us
    pallas_call x6, Pallas kernels, call(): pl.pallas_call(kernel, out_shape=[jax.ShapeDtypeStruct(shape, jnp.float32...  38.7 us
    ppermute x34, starting transfers between devices, swap(): return lax.ppermute(x, axis, [(i, i ^ mask) for i in range(count)])  38.3 us
    pallas_call x1, Pallas kernels, swift(): pl.pallas_call(third_kernel, out_shape=[jax.ShapeDtypeStruct((rank, depth...  17.2 us
    all_to_all x1, blocking collectives, swift(): lax.all_to_all(slab, AXES, 0, 0, tiled=True).reshape(depth, own_a * own_b)  15.6 us
    all_to_all x2, starting transfers between devices, trade(): return lax.all_to_all(x.reshape(shape), AXES, 0, 0, tiled=True)  9.24 us
    all_to_all x2, waiting for transfers between devices, trade(): return lax.all_to_all(x.reshape(shape), AXES, 0, 0, tiled=True)  4.51 us
  transfers between devices with their start and end apart: 36, of which 24 were waited for; matrix products, arithmetic and copies ran while one was open for 3% of the time, Pallas kernels for 13%

profile of v3, /device:TPU:0, one launch (start us, length us, event | category | flops | bytes accessed | tf_op | source)
XLA Modules:
  0.0 193.4 jit_solution(17822593332423279823)
XLA Ops:
  0.7 3.2 %fusion = f32[64,512]{1,0:T(8,128)S(1)} fusion(f32[768,64]{0,1:T(8,128)} %param.7, f32[512,768]{1,0:T(8,128)} %bitcast.16), kind=kOutput, calls=%fused_computation.46 | convolution fusion | flops 301989888 | bytes 1900544 | tf_op jit(solution)/shard_map/dot_general | solution.py:37
  4.4 4.7 %collective-permute-start = (f32[32,64]{1,0:T(8,128)S(1)}, f32[32,64]{1,0:T(8,128)S(1)}, u32[]{:S(2)}, u32[]{:S(2)}) collective-permute-start(f32[32,64]{1,0:T(8,128)S(1)} %copy-done.4), channel_id=1, source_target_pairs={{0,3},{1,2},{2,1},{3,0},{4,7},{5,6},{6,5},{7,4},{8,11},{9,10},{10,... | collective-permute-start | bytes 24584 | tf_op jit(solution)/shard_map/ppermute | solution.py:282
  10.4 6.0 %all-to-all-start = ((f32[32,2,512]{2,1,0:T(2,128)}), f32[32,2,512]{2,1,0:T(2,128)S(1)}, u32[]{:S(2)}, u32[]{:S(2)}) async-start(f32[32,2,512]{2,1,0:T(2,128)} %reshape.30), calls=%async_computation | async-start | bytes 262144 | tf_op jit(solution)/shard_map/all_to_all | solution.py:362
  16.5 1.8 collective-permute-start.11
  19.0 1.3 collective-permute-done.11
  20.3 4.5 %all-to-all-done = f32[32,2,512]{2,1,0:T(2,128)S(1)} async-done(((f32[32,2,512]{2,1,0:T(2,128)}), f32[32,2,512]{2,1,0:T(2,128)S(1)}, u32[]{:S(2)}, u32[]{:S(2)}) %all-to-all-start) | async-done | bytes 131104 | tf_op jit(solution)/shard_map/all_to_all | solution.py:362
  26.1 2.2 %open.1 = f32[128,128]{1,0:T(8,128)} custom-call(f32[2,128,128]{2,1,0:T(8,128)} %reshape.32.cont_ref, f32[128,64]{1,0:T(8,128)} %pad_maximum_fusion.4.start_ref), custom_call_target="tpu_custom_call" | custom-call | tf_op jit(solution)/shard_map/open/pallas_call | solution.py:149
  29.2 1.6 copy.14
  30.8 1.3 collective-permute-start.5
  32.9 1.5 collective-permute-start.4
  35.2 2.5 %collective-permute-done.6 = f32[128,128]{1,0:T(8,128)S(1)} collective-permute-done((f32[128,128]{1,0:T(8,128)S(1)}, f32[128,128]{1,0:T(8,128)S(1)}, u32[]{:S(2)}, u32[]{:S(2)}) %collective-permute-start.6) | collective-permute-done | bytes 65568 | tf_op jit(solution)/shard_map/ppermute | solution.py:282
  38.1 2.0 %collective-permute-start.9 = (f32[128,128]{1,0:T(8,128)S(1)}, f32[128,128]{1,0:T(8,128)S(1)}, u32[]{:S(2)}, u32[]{:S(2)}) collective-permute-start(f32[128,128]{1,0:T(8,128)S(1)} %add_add_fusion.3), channel_id=1, source_target_pairs={{0,3},{1,2},{2,1},{3,0},{4,7},{5,6},{6,5},{7,4},{8,11},{9,10},{10,... | collective-permute-start | bytes 196616 | tf_op jit(solution)/shard_map/ppermute | solution.py:282
  40.1 1.2 collective-permute-start.7
  41.9 2.7 %collective-permute-done.8 = f32[128,128]{1,0:T(8,128)S(1)} collective-permute-done((f32[128,128]{1,0:T(8,128)S(1)}, f32[128,128]{1,0:T(8,128)S(1)}, u32[]{:S(2)}, u32[]{:S(2)}) %collective-permute-start.8) | collective-permute-done | bytes 65568 | tf_op jit(solution)/shard_map/ppermute | solution.py:282
  45.9 3.3 %all-to-all-start.1 = ((f32[32,24,512]{2,1,0:T(8,128)}), f32[32,24,512]{2,1,0:T(8,128)S(1)}, u32[]{:S(2)}, u32[]{:S(2)}) async-start(f32[32,24,512]{2,1,0:T(8,128)} %bitcast.5), calls=%async_computation.1 | async-start | bytes 3145728 | tf_op jit(solution)/shard_map/all_to_all | solution.py:362
  49.2 12.6 %first.1 = (f32[128,64]{1,0:T(8,128)}, f32[64,128]{1,0:T(8,128)}, f32[128,128]{1,0:T(8,128)}) custom-call(f32[128,128]{1,0:T(8,128)} %add_add_fusion.2.gram_ref, f32[128,64]{1,0:T(8,128)} %pad_maximum_fusion.5.start_ref, f32[2,128,128]{2,1,0:T(8,128)} %reshape.32.cont_ref), custom_call_target="tpu_custom_call" | custom-call | tf_op jit(solution)/shard_map/first/pallas_call | solution.py:149
  62.1 1.2 collective-permute-done.13
  64.1 1.8 collective-permute-start.15
  66.0 1.5 collective-permute-start.16
  67.7 1.5 collective-permute-done.15
  69.1 3.0 %collective-permute-done.16 = f32[128,128]{1,0:T(8,128)S(1)} collective-permute-done((f32[128,128]{1,0:T(8,128)S(1)}, f32[128,128]{1,0:T(8,128)S(1)}, u32[]{:S(2)}, u32[]{:S(2)}) %collective-permute-start.16) | collective-permute-done | bytes 65568 | tf_op jit(solution)/shard_map/ppermute | solution.py:282
  72.2 5.0 %collective-permute-start.18 = (f32[128,128]{1,0:T(8,128)S(1)}, f32[128,128]{1,0:T(8,128)S(1)}, u32[]{:S(2)}, u32[]{:S(2)}) collective-permute-start(f32[128,128]{1,0:T(8,128)S(1)} %add_add_fusion.1), channel_id=1, source_target_pairs={{0,2},{1,3},{2,0},{3,1},{4,6},{5,7},{6,4},{7,5},{8,10},{9,11},{10,... | collective-permute-start | bytes 196616 | tf_op jit(solution)/shard_map/ppermute | solution.py:282
  77.8 13.6 %collective-permute-done.18 = f32[128,128]{1,0:T(8,128)S(1)} collective-permute-done((f32[128,128]{1,0:T(8,128)S(1)}, f32[128,128]{1,0:T(8,128)S(1)}, u32[]{:S(2)}, u32[]{:S(2)}) %collective-permute-start.18) | collective-permute-done | bytes 65568 | tf_op jit(solution)/shard_map/ppermute | solution.py:282
  92.1 11.9 %second.1 = (f32[128,64]{1,0:T(8,128)}, f32[64,128]{1,0:T(8,128)}) custom-call(f32[128,128]{1,0:T(8,128)} %add_add_fusion.gram_ref, f32[128,64]{1,0:T(8,128)} %pad_maximum_fusion.4.start_ref), custom_call_target="tpu_custom_call" | custom-call | tf_op jit(solution)/shard_map/second/pallas_call | solution.py:149
  104.0 1.2 copy-done.1
  105.2 5.2 %mix.1.mixed_ref = f32[1536,128]{1,0:T(8,128)} custom-call(f32[128,64]{1,0:T(8,128)} %get-tuple-element.26.factor_ref, f32[32,24,512]{2,1,0:T(8,128)} %copy-done.1), custom_call_target="tpu_custom_call" | custom-call | tf_op jit(solution)/shard_map/mix/pallas_call | solution.py:149
  110.4 3.4 %slab.1 = f32[32,24,128]{2,1,0:T(8,128)} custom-call(f32[128,64]{1,0:T(8,128)} %get-tuple-element.25.right_ref, f32[1536,128]{1,0:T(8,128)} %mix.1.mixed_ref), custom_call_target="tpu_custom_call" | custom-call | tf_op jit(solution)/shard_map/slab/pallas_call | solution.py:149
  113.8 15.6 %all_to_all.15 = f32[32,24,128]{2,1,0:T(8,128)} all-to-all(f32[32,24,128]{2,1,0:T(8,128)} %slab.1), channel_id=1, replica_groups=mesh['row'=8,'col'=4] {'row','col'}, dimensions={0} | all-to-all | bytes 786432 | tf_op jit(solution)/shard_map/all_to_all | solution.py:403
  129.4 3.4 %pair.1 = f32[2688,128]{1,0:T(8,128)} custom-call(f32[768,128]{1,0:T(8,128)} %bitcast.18), custom_call_target="tpu_custom_call" | custom-call | tf_op jit(solution)/shard_map/pair/pallas_call | solution.py:149
  132.8 1.5 slice_select_fusion
  134.2 1.3 collective-permute-start.20
  135.5 1.8 collective-permute-done.20
  137.5 1.2 collective-permute-start.21
  139.2 4.9 %collective-permute-done.21 = f32[336,128]{1,0:T(8,128)S(1)} collective-permute-done((f32[336,128]{1,0:T(8,128)S(1)}, f32[336,128]{1,0:T(8,128)S(1)}, u32[]{:S(2)}, u32[]{:S(2)}) %collective-permute-start.21) | collective-permute-done | bytes 172064 | tf_op jit(solution)/shard_map/ppermute | solution.py:282
  146.1 1.3 collective-permute-start.22
  147.3 2.4 %collective-permute-done.28 = f32[168,128]{1,0:T(8,128)S(1)} collective-permute-done((f32[168,128]{1,0:T(8,128)S(1)}, f32[168,128]{1,0:T(8,128)S(1)}, u32[]{:S(2)}, u32[]{:S(2)}) %collective-permute-start.28) | collective-permute-done | bytes 86048 | tf_op jit(solution)/shard_map/ppermute | solution.py:282
  150.7 1.2 collective-permute-start.23
  151.9 2.4 %collective-permute-done.29 = f32[168,128]{1,0:T(8,128)S(1)} collective-permute-done((f32[168,128]{1,0:T(8,128)S(1)}, f32[168,128]{1,0:T(8,128)S(1)}, u32[]{:S(2)}, u32[]{:S(2)}) %collective-permute-start.29) | collective-permute-done | bytes 86048 | tf_op jit(solution)/shard_map/ppermute | solution.py:282
  155.3 2.3 %collective-permute-start.24 = (f32[168,128]{1,0:T(8,128)S(1)}, f32[168,128]{1,0:T(8,128)S(1)}, u32[]{:S(2)}, u32[]{:S(2)}) collective-permute-start(f32[168,128]{1,0:T(8,128)S(1)} %add.86), channel_id=1, source_target_pairs={{0,2},{1,3},{2,0},{3,1},{4,6},{5,7},{6,4},{7,5},{8,10},{9,11},{10,... | collective-permute-start | bytes 258056 | tf_op jit(solution)/shard_map/ppermute | solution.py:282
  157.7 3.0 %collective-permute-done.30 = f32[168,128]{1,0:T(8,128)S(1)} collective-permute-done((f32[168,128]{1,0:T(8,128)S(1)}, f32[168,128]{1,0:T(8,128)S(1)}, u32[]{:S(2)}, u32[]{:S(2)}) %collective-permute-start.30) | collective-permute-done | bytes 86048 | tf_op jit(solution)/shard_map/ppermute | solution.py:282
  160.8 1.7 collective-permute-done.24
  163.5 2.3 %collective-permute-done.31 = f32[168,128]{1,0:T(8,128)S(1)} collective-permute-done((f32[168,128]{1,0:T(8,128)S(1)}, f32[168,128]{1,0:T(8,128)S(1)}, u32[]{:S(2)}, u32[]{:S(2)}) %collective-permute-start.31) | collective-permute-done | bytes 86048 | tf_op jit(solution)/shard_map/ppermute | solution.py:282
  167.1 1.3 collective-permute-start.26
  168.4 2.8 %collective-permute-done.32 = f32[336,128]{1,0:T(8,128)S(1)} collective-permute-done((f32[336,128]{1,0:T(8,128)S(1)}, f32[336,128]{1,0:T(8,128)S(1)}, u32[]{:S(2)}, u32[]{:S(2)}) %collective-permute-start.32) | collective-permute-done | bytes 172064 | tf_op jit(solution)/shard_map/ppermute | solution.py:282
  171.3 1.3 collective-permute-done.26
  172.7 2.1 %collective-permute-done.33 = f32[1344,128]{1,0:T(8,128)S(1)} collective-permute-done((f32[1344,128]{1,0:T(8,128)S(1)}, f32[1344,128]{1,0:T(8,128)S(1)}, u32[]{:S(2)}, u32[]{:S(2)}) %collective-permute-start.33) | collective-permute-done | bytes 688160 | tf_op jit(solution)/shard_map/ppermute | solution.py:282
  175.0 1.2 pad_maximum_fusion.packed_ref
  176.2 17.2 %third.1 = (f32[64,768]{1,0:T(8,128)}, f32[128,64]{1,0:T(8,128)}) custom-call(f32[2688,128]{1,0:T(8,128)} %pad_maximum_fusion.packed_ref, f32[64,768]{1,0:T(8,128)} %bitcast.21, f32[768,128]{1,0:T(8,128)} %bitcast.19), custom_call_target="tpu_custom_call" | custom-call | tf_op jit(solution)/shard_map/third/pallas_call | solution.py:406
  (86 shorter events, 18.7 us)
Async XLA Ops:
  0.6 3.2 %copy-start.5 = (f32[16,64]{1,0:T(8,128)S(1)}, f32[16,64]{1,0:T(8,128)}, u32[]{:S(2)}) copy-start(f32[16,64]{1,0:T(8,128)} %param.5) | copy-start | bytes 12292
  0.6 3.7 %copy-start.4 = (f32[32,64]{1,0:T(8,128)S(1)}, f32[32,64]{1,0:T(8,128)}, u32[]{:S(2)}) copy-start(f32[32,64]{1,0:T(8,128)} %param.6) | copy-start | bytes 24580
  3.8 12.6 %collective-permute-start.10 = (f32[16,64]{1,0:T(8,128)S(1)}, f32[16,64]{1,0:T(8,128)S(1)}, u32[]{:S(2)}, u32[]{:S(2)}) collective-permute-start(f32[16,64]{1,0:T(8,128)S(1)} %copy-done.5), channel_id=1, source_target_pairs={{0,4},{4,0},{8,12},{12,8},{16,20},{20,16},{24,28},{28,24},{1,5},{5... | collective-permute-start | bytes 12296 | tf_op jit(solution)/shard_map/ppermute | solution.py:282
  4.4 13.9 %collective-permute-start = (f32[32,64]{1,0:T(8,128)S(1)}, f32[32,64]{1,0:T(8,128)S(1)}, u32[]{:S(2)}, u32[]{:S(2)}) collective-permute-start(f32[32,64]{1,0:T(8,128)S(1)} %copy-done.4), channel_id=1, source_target_pairs={{0,3},{1,2},{2,1},{3,0},{4,7},{5,6},{6,5},{7,4},{8,11},{9,10},{10,... | collective-permute-start | bytes 24584 | tf_op jit(solution)/shard_map/ppermute | solution.py:282
  9.0 9.3 %collective-permute-start.1 = (f32[32,64]{1,0:T(8,128)S(1)}, f32[32,64]{1,0:T(8,128)S(1)}, u32[]{:S(2)}, u32[]{:S(2)}) collective-permute-start(f32[32,64]{1,0:T(8,128)S(1)} %copy-done.4), channel_id=1, source_target_pairs={{0,2},{1,3},{2,0},{3,1},{4,6},{5,7},{6,4},{7,5},{8,10},{9,11},{10,... | collective-permute-start | bytes 24584 | tf_op jit(solution)/shard_map/ppermute | solution.py:282
  9.0 9.3 %collective-permute-start.2 = (f32[32,64]{1,0:T(8,128)S(1)}, f32[32,64]{1,0:T(8,128)S(1)}, u32[]{:S(2)}, u32[]{:S(2)}) collective-permute-start(f32[32,64]{1,0:T(8,128)S(1)} %copy-done.4), channel_id=1, source_target_pairs={{0,1},{1,0},{2,3},{3,2},{4,5},{5,4},{6,7},{7,6},{8,9},{9,8},{10,11... | collective-permute-start | bytes 24584 | tf_op jit(solution)/shard_map/ppermute | solution.py:282
  10.4 14.4 %all-to-all-start = ((f32[32,2,512]{2,1,0:T(2,128)}), f32[32,2,512]{2,1,0:T(2,128)S(1)}, u32[]{:S(2)}, u32[]{:S(2)}) async-start(f32[32,2,512]{2,1,0:T(2,128)} %reshape.30), calls=%async_computation | async-start | bytes 262144 | tf_op jit(solution)/shard_map/all_to_all | solution.py:362
  16.5 3.8 %collective-permute-start.11 = (f32[32,64]{1,0:T(8,128)S(1)}, f32[32,64]{1,0:T(8,128)S(1)}, u32[]{:S(2)}, u32[]{:S(2)}) collective-permute-start(f32[32,64]{1,0:T(8,128)S(1)} %pad_maximum_fusion.7), channel_id=1, source_target_pairs={{0,8},{4,12},{8,0},{12,4},{16,24},{20,28},{24,16},{28,20},{1,9},{5... | collective-permute-start | bytes 24584 | tf_op jit(solution)/shard_map/ppermute | solution.py:282
  24.8 4.4 %copy-start.2 = (f32[16,32,768]{2,1,0:T(8,128)S(1)}, f32[16,32,768]{2,1,0:T(8,128)}, u32[]{:S(2)}) copy-start(f32[16,32,768]{2,1,0:T(8,128)} %param.4) | copy-start | bytes 4718596
  28.3 2.5 %collective-permute-start.3 = (f32[128,128]{1,0:T(8,128)}, f32[128,128]{1,0:T(8,128)S(1)}, u32[]{:S(2)}, u32[]{:S(2)}) collective-permute-start(f32[128,128]{1,0:T(8,128)} %open.1), channel_id=1, source_target_pairs={{0,4},{4,0},{8,12},{12,8},{16,20},{20,16},{24,28},{28,24},{1,5},{5... | collective-permute-start | bytes 196616 | tf_op jit(solution)/shard_map/ppermute | solution.py:282
  28.3 2.5 %copy-start.3 = (f32[128,128]{1,0:T(8,128)S(1)}, f32[128,128]{1,0:T(8,128)}, u32[]{:S(2)}) copy-start(f32[128,128]{1,0:T(8,128)} %open.1) | copy-start | bytes 196612
  28.3 6.1 %collective-permute-start.12 = (f32[64,64]{1,0:T(8,128)S(1)}, f32[64,64]{1,0:T(8,128)S(1)}, u32[]{:S(2)}, u32[]{:S(2)}) collective-permute-start(f32[64,64]{1,0:T(8,128)S(1)} %pad_maximum_fusion.6), channel_id=1, source_target_pairs={{0,16},{4,20},{8,24},{12,28},{16,0},{20,4},{24,8},{28,12},{1,17},{... | collective-permute-start | bytes 49160 | tf_op jit(solution)/shard_map/ppermute | solution.py:282
  30.8 4.3 %collective-permute-start.5 = (f32[128,128]{1,0:T(8,128)S(1)}, f32[128,128]{1,0:T(8,128)S(1)}, u32[]{:S(2)}, u32[]{:S(2)}) collective-permute-start(f32[128,128]{1,0:T(8,128)S(1)} %add.69), channel_id=1, source_target_pairs={{0,16},{4,20},{8,24},{12,28},{16,0},{20,4},{24,8},{28,12},{1,17},{... | collective-permute-start | bytes 196616 | tf_op jit(solution)/shard_map/ppermute | solution.py:282
  32.1 5.5 %collective-permute-start.6 = (f32[128,128]{1,0:T(8,128)S(1)}, f32[128,128]{1,0:T(8,128)S(1)}, u32[]{:S(2)}, u32[]{:S(2)}) collective-permute-start(f32[128,128]{1,0:T(8,128)S(1)} %add.69), channel_id=1, source_target_pairs={{0,24},{4,28},{8,16},{12,20},{16,8},{20,12},{24,0},{28,4},{1,25},{... | collective-permute-start | bytes 196616 | tf_op jit(solution)/shard_map/ppermute | solution.py:282
  32.9 4.8 %collective-permute-start.4 = (f32[128,128]{1,0:T(8,128)S(1)}, f32[128,128]{1,0:T(8,128)S(1)}, u32[]{:S(2)}, u32[]{:S(2)}) collective-permute-start(f32[128,128]{1,0:T(8,128)S(1)} %add.69), channel_id=1, source_target_pairs={{0,8},{4,12},{8,0},{12,4},{16,24},{20,28},{24,16},{28,20},{1,9},{5... | collective-permute-start | bytes 196616 | tf_op jit(solution)/shard_map/ppermute | solution.py:282
  37.7 6.9 %collective-permute-start.8 = (f32[128,128]{1,0:T(8,128)S(1)}, f32[128,128]{1,0:T(8,128)S(1)}, u32[]{:S(2)}, u32[]{:S(2)}) collective-permute-start(f32[128,128]{1,0:T(8,128)S(1)} %add_add_fusion.3), channel_id=1, source_target_pairs={{0,2},{1,3},{2,0},{3,1},{4,6},{5,7},{6,4},{7,5},{8,10},{9,11},{10,... | collective-permute-start | bytes 196616 | tf_op jit(solution)/shard_map/ppermute | solution.py:282
  38.1 6.5 %collective-permute-start.9 = (f32[128,128]{1,0:T(8,128)S(1)}, f32[128,128]{1,0:T(8,128)S(1)}, u32[]{:S(2)}, u32[]{:S(2)}) collective-permute-start(f32[128,128]{1,0:T(8,128)S(1)} %add_add_fusion.3), channel_id=1, source_target_pairs={{0,3},{1,2},{2,1},{3,0},{4,7},{5,6},{6,5},{7,4},{8,11},{9,10},{10,... | collective-permute-start | bytes 196616 | tf_op jit(solution)/shard_map/ppermute | solution.py:282
  40.1 5.2 %collective-permute-start.7 = (f32[128,128]{1,0:T(8,128)S(1)}, f32[128,128]{1,0:T(8,128)S(1)}, u32[]{:S(2)}, u32[]{:S(2)}) collective-permute-start(f32[128,128]{1,0:T(8,128)S(1)} %add_add_fusion.3), channel_id=1, source_target_pairs={{0,1},{1,0},{2,3},{3,2},{4,5},{5,4},{6,7},{7,6},{8,9},{9,8},{10,11... | collective-permute-start | bytes 196616 | tf_op jit(solution)/shard_map/ppermute | solution.py:282
  45.9 58.1 %all-to-all-start.1 = ((f32[32,24,512]{2,1,0:T(8,128)}), f32[32,24,512]{2,1,0:T(8,128)S(1)}, u32[]{:S(2)}, u32[]{:S(2)}) async-start(f32[32,24,512]{2,1,0:T(8,128)} %bitcast.5), calls=%async_computation.1 | async-start | bytes 3145728 | tf_op jit(solution)/shard_map/all_to_all | solution.py:362
  61.8 1.5 collective-permute-start.13
  64.1 5.0 %collective-permute-start.15 = (f32[128,128]{1,0:T(8,128)S(1)}, f32[128,128]{1,0:T(8,128)S(1)}, u32[]{:S(2)}, u32[]{:S(2)}) collective-permute-start(f32[128,128]{1,0:T(8,128)S(1)} %add.76), channel_id=1, source_target_pairs={{0,16},{4,20},{8,24},{12,28},{16,0},{20,4},{24,8},{28,12},{1,17},{... | collective-permute-start | bytes 196616 | tf_op jit(solution)/shard_map/ppermute | solution.py:282
  66.0 6.2 %collective-permute-start.16 = (f32[128,128]{1,0:T(8,128)S(1)}, f32[128,128]{1,0:T(8,128)S(1)}, u32[]{:S(2)}, u32[]{:S(2)}) collective-permute-start(f32[128,128]{1,0:T(8,128)S(1)} %add.76), channel_id=1, source_target_pairs={{0,24},{4,28},{8,16},{12,20},{16,8},{20,12},{24,0},{28,4},{1,25},{... | collective-permute-start | bytes 196616 | tf_op jit(solution)/shard_map/ppermute | solution.py:282
  67.4 4.7 %collective-permute-start.14 = (f32[128,128]{1,0:T(8,128)S(1)}, f32[128,128]{1,0:T(8,128)S(1)}, u32[]{:S(2)}, u32[]{:S(2)}) collective-permute-start(f32[128,128]{1,0:T(8,128)S(1)} %add.76), channel_id=1, source_target_pairs={{0,8},{4,12},{8,0},{12,4},{16,24},{20,28},{24,16},{28,20},{1,9},{5... | collective-permute-start | bytes 196616 | tf_op jit(solution)/shard_map/ppermute | solution.py:282
  72.2 19.3 %collective-permute-start.18 = (f32[128,128]{1,0:T(8,128)S(1)}, f32[128,128]{1,0:T(8,128)S(1)}, u32[]{:S(2)}, u32[]{:S(2)}) collective-permute-start(f32[128,128]{1,0:T(8,128)S(1)} %add_add_fusion.1), channel_id=1, source_target_pairs={{0,2},{1,3},{2,0},{3,1},{4,6},{5,7},{6,4},{7,5},{8,10},{9,11},{10,... | collective-permute-start | bytes 196616 | tf_op jit(solution)/shard_map/ppermute | solution.py:282
  77.2 14.2 %collective-permute-start.19 = (f32[128,128]{1,0:T(8,128)S(1)}, f32[128,128]{1,0:T(8,128)S(1)}, u32[]{:S(2)}, u32[]{:S(2)}) collective-permute-start(f32[128,128]{1,0:T(8,128)S(1)} %add_add_fusion.1), channel_id=1, source_target_pairs={{0,3},{1,2},{2,1},{3,0},{4,7},{5,6},{6,5},{7,4},{8,11},{9,10},{10,... | collective-permute-start | bytes 196616 | tf_op jit(solution)/shard_map/ppermute | solution.py:282
  77.3 14.1 %collective-permute-start.17 = (f32[128,128]{1,0:T(8,128)S(1)}, f32[128,128]{1,0:T(8,128)S(1)}, u32[]{:S(2)}, u32[]{:S(2)}) collective-permute-start(f32[128,128]{1,0:T(8,128)S(1)} %add_add_fusion.1), channel_id=1, source_target_pairs={{0,1},{1,0},{2,3},{3,2},{4,5},{5,4},{6,7},{7,6},{8,9},{9,8},{10,11... | collective-permute-start | bytes 196616 | tf_op jit(solution)/shard_map/ppermute | solution.py:282
  104.0 1.2 copy-start.1
  132.8 4.6 %copy-start = (f32[2688,128]{1,0:T(8,128)S(1)}, f32[2688,128]{1,0:T(8,128)}, u32[]{:S(2)}) copy-start(f32[2688,128]{1,0:T(8,128)} %pair.1) | copy-start | bytes 4128772
  134.2 3.1 %collective-permute-start.20 = (f32[1344,128]{1,0:T(8,128)S(1)}, f32[1344,128]{1,0:T(8,128)S(1)}, u32[]{:S(2)}, u32[]{:S(2)}) collective-permute-start(f32[1344,128]{1,0:T(8,128)S(1)} %slice_select_fusion), channel_id=1, source_target_pairs={{0,4},{4,0},{8,12},{12,8},{16,20},{20,16},{24,28},{28,24},{1,5},{5... | collective-permute-start | bytes 2064392 | tf_op jit(solution)/shard_map/ppermute | solution.py:282
  137.5 6.7 %collective-permute-start.21 = (f32[336,128]{1,0:T(8,128)S(1)}, f32[336,128]{1,0:T(8,128)S(1)}, u32[]{:S(2)}, u32[]{:S(2)}) collective-permute-start(f32[336,128]{1,0:T(8,128)S(1)} %get-tuple-element.34), channel_id=1, source_target_pairs={{0,8},{4,12},{8,0},{12,4},{16,24},{20,28},{24,16},{28,20},{1,9},{5... | collective-permute-start | bytes 516104 | tf_op jit(solution)/shard_map/ppermute | solution.py:282
  138.7 6.4 %collective-permute-start.27 = (f32[336,128]{1,0:T(8,128)S(1)}, f32[336,128]{1,0:T(8,128)S(1)}, u32[]{:S(2)}, u32[]{:S(2)}) collective-permute-start(f32[336,128]{1,0:T(8,128)S(1)} %get-tuple-element.35), channel_id=1, source_target_pairs={{0,16},{4,20},{8,24},{12,28},{16,0},{20,4},{24,8},{28,12},{1,17},{... | collective-permute-start | bytes 516104 | tf_op jit(solution)/shard_map/ppermute | solution.py:282
  145.1 4.6 %collective-permute-start.28 = (f32[168,128]{1,0:T(8,128)S(1)}, f32[168,128]{1,0:T(8,128)S(1)}, u32[]{:S(2)}, u32[]{:S(2)}) collective-permute-start(f32[168,128]{1,0:T(8,128)S(1)} %slice_select_fusion.3), channel_id=1, source_target_pairs={{0,8},{4,12},{8,0},{12,4},{16,24},{20,28},{24,16},{28,20},{1,9},{5... | collective-permute-start | bytes 258056 | tf_op jit(solution)/shard_map/ppermute | solution.py:282
  146.1 4.6 %collective-permute-start.22 = (f32[168,128]{1,0:T(8,128)S(1)}, f32[168,128]{1,0:T(8,128)S(1)}, u32[]{:S(2)}, u32[]{:S(2)}) collective-permute-start(f32[168,128]{1,0:T(8,128)S(1)} %slice_select_fusion.4), channel_id=1, source_target_pairs={{0,16},{4,20},{8,24},{12,28},{16,0},{20,4},{24,8},{28,12},{1,17},{... | collective-permute-start | bytes 258056 | tf_op jit(solution)/shard_map/ppermute | solution.py:282
  149.7 4.5 %collective-permute-start.29 = (f32[168,128]{1,0:T(8,128)S(1)}, f32[168,128]{1,0:T(8,128)S(1)}, u32[]{:S(2)}, u32[]{:S(2)}) collective-permute-start(f32[168,128]{1,0:T(8,128)S(1)} %select_add_fusion.3), channel_id=1, source_target_pairs={{0,1},{1,0},{2,3},{3,2},{4,5},{5,4},{6,7},{7,6},{8,9},{9,8},{10,11... | collective-permute-start | bytes 258056 | tf_op jit(solution)/shard_map/ppermute | solution.py:282
  150.7 4.7 %collective-permute-start.23 = (f32[168,128]{1,0:T(8,128)S(1)}, f32[168,128]{1,0:T(8,128)S(1)}, u32[]{:S(2)}, u32[]{:S(2)}) collective-permute-start(f32[168,128]{1,0:T(8,128)S(1)} %select_add_fusion.4), channel_id=1, source_target_pairs={{0,1},{1,0},{2,3},{3,2},{4,5},{5,4},{6,7},{7,6},{8,9},{9,8},{10,11... | collective-permute-start | bytes 258056 | tf_op jit(solution)/shard_map/ppermute | solution.py:282
  154.3 6.4 %collective-permute-start.30 = (f32[168,128]{1,0:T(8,128)S(1)}, f32[168,128]{1,0:T(8,128)S(1)}, u32[]{:S(2)}, u32[]{:S(2)}) collective-permute-start(f32[168,128]{1,0:T(8,128)S(1)} %add.90), channel_id=1, source_target_pairs={{0,2},{1,3},{2,0},{3,1},{4,6},{5,7},{6,4},{7,5},{8,10},{9,11},{10,... | collective-permute-start | bytes 258056 | tf_op jit(solution)/shard_map/ppermute | solution.py:282
  155.3 7.2 %collective-permute-start.24 = (f32[168,128]{1,0:T(8,128)S(1)}, f32[168,128]{1,0:T(8,128)S(1)}, u32[]{:S(2)}, u32[]{:S(2)}) collective-permute-start(f32[168,128]{1,0:T(8,128)S(1)} %add.86), channel_id=1, source_target_pairs={{0,2},{1,3},{2,0},{3,1},{4,6},{5,7},{6,4},{7,5},{8,10},{9,11},{10,... | collective-permute-start | bytes 258056 | tf_op jit(solution)/shard_map/ppermute | solution.py:282
  160.7 5.1 %collective-permute-start.31 = (f32[168,128]{1,0:T(8,128)S(1)}, f32[168,128]{1,0:T(8,128)S(1)}, u32[]{:S(2)}, u32[]{:S(2)}) collective-permute-start(f32[168,128]{1,0:T(8,128)S(1)} %add.91), channel_id=1, source_target_pairs={{0,8},{4,12},{8,0},{12,4},{16,24},{20,28},{24,16},{28,20},{1,9},{5... | collective-permute-start | bytes 258056 | tf_op jit(solution)/shard_map/ppermute | solution.py:282
  162.5 4.6 %collective-permute-start.25 = (f32[168,128]{1,0:T(8,128)S(1)}, f32[168,128]{1,0:T(8,128)S(1)}, u32[]{:S(2)}, u32[]{:S(2)}) collective-permute-start(f32[168,128]{1,0:T(8,128)S(1)} %add.87), channel_id=1, source_target_pairs={{0,16},{4,20},{8,24},{12,28},{16,0},{20,4},{24,8},{28,12},{1,17},{... | collective-permute-start | bytes 258056 | tf_op jit(solution)/shard_map/ppermute | solution.py:282
  165.8 5.5 %collective-permute-start.32 = (f32[336,128]{1,0:T(8,128)S(1)}, f32[336,128]{1,0:T(8,128)S(1)}, u32[]{:S(2)}, u32[]{:S(2)}) collective-permute-start(f32[336,128]{1,0:T(8,128)S(1)} %pad_maximum_fusion.3), channel_id=1, source_target_pairs={{0,16},{4,20},{8,24},{12,28},{16,0},{20,4},{24,8},{28,12},{1,17},{... | collective-permute-start | bytes 516104 | tf_op jit(solution)/shard_map/ppermute | solution.py:282
  167.1 5.5 %collective-permute-start.26 = (f32[336,128]{1,0:T(8,128)S(1)}, f32[336,128]{1,0:T(8,128)S(1)}, u32[]{:S(2)}, u32[]{:S(2)}) collective-permute-start(f32[336,128]{1,0:T(8,128)S(1)} %pad_maximum_fusion.2), channel_id=1, source_target_pairs={{0,8},{4,12},{8,0},{12,4},{16,24},{20,28},{24,16},{28,20},{1,9},{5... | collective-permute-start | bytes 516104 | tf_op jit(solution)/shard_map/ppermute | solution.py:282
  172.7 2.2 %collective-permute-start.33 = (f32[1344,128]{1,0:T(8,128)S(1)}, f32[1344,128]{1,0:T(8,128)S(1)}, u32[]{:S(2)}, u32[]{:S(2)}) collective-permute-start(f32[1344,128]{1,0:T(8,128)S(1)} %pad_maximum_fusion.1), channel_id=1, source_target_pairs={{0,4},{4,0},{8,12},{12,8},{16,20},{20,16},{24,28},{28,24},{1,5},{5... | collective-permute-start | bytes 2064392 | tf_op jit(solution)/shard_map/ppermute | solution.py:282

commit v4 on v3

--- a/solution.py
+++ b/solution.py
@@ -164,23 +164,28 @@
     return high, middle, low
 
 
-def iterate(gram, turned):
-    rank, size = turned.shape
-    extra = -size % WIDE
-    high, middle, low = pieces(jnp.pad(gram, ((0, extra), (0, extra))))
+def stacked(left, right):
+    rows = left[0].shape[0]
 
     def times(parts, matrix):
         whole = jnp.dot(jnp.concatenate(parts, axis=0), matrix, preferred_element_type=jnp.float32)
-        return [whole[n * rank : (n + 1) * rank] for n in range(len(parts))]
+        return [whole[n * rows : (n + 1) * rows] for n in range(len(parts))]
+
+    first = times(left, right[0])
+    second = times(left[:2], right[1])
+    (third,) = times(left[:1], right[2])
+    return first[0] + ((first[1] + second[0]) + ((first[2] + second[1]) + third))
+
+
+def iterate(gram, turned):
+    extra = -turned.shape[1] % WIDE
+    parts = pieces(jnp.pad(gram, ((0, extra), (0, extra))))
 
     def step(_, turned):
-        top, mid, end = pieces(turned)
-        first = times([top, mid, end], high)
-        second = times([top, mid], middle)
-        (third,) = times([top], low)
-        image = first[0] + ((first[1] + second[0]) + ((first[2] + second[1]) + third))
+        image = stacked(pieces(turned), parts)
         return product(lower_inverse(right_product(image, image)), image)
 
+    size = turned.shape[1]
     return lax.fori_loop(0, STEPS, step, jnp.pad(turned, ((0, 0), (0, extra))))[:, :size]
 
 
@@ -196,8 +201,9 @@
     gram_ref[...] = gram_of(slabs)
 
 
-def first_kernel(gram_ref, start_ref, cont_ref, basis_ref, factor_ref, next_ref):
-    turned = iterate(gram_ref[...], start_ref[...].T)
+def first_kernel(*refs):
+    start_ref, cont_ref, basis_ref, factor_ref, next_ref = refs[-5:]
+    turned = iterate(tree([ref[...] for ref in refs[:-5]]), start_ref[...].T)
     factor_ref[...] = turned * math.sqrt(turned.shape[1])
     basis = turned.T
     basis_ref[...] = basis
@@ -205,8 +211,9 @@
     next_ref[...] = gram_of(slabs)
 
 
-def second_kernel(gram_ref, start_ref, basis_ref, factor_ref):
-    turned = iterate(gram_ref[...], start_ref[...].T)
+def second_kernel(*refs):
+    start_ref, basis_ref, factor_ref = refs[-3:]
+    turned = iterate(tree([ref[...] for ref in refs[:-3]]), start_ref[...].T)
     factor_ref[...] = turned * math.sqrt(turned.shape[1])
     basis_ref[...] = turned.T
 
@@ -230,10 +237,9 @@
                         piece = jnp.where(lane == c, moved, piece)
                 index = (r * tiles + tile) * groups + inner
                 turn_ref[pl.ds(index, count, stride=full), :] = piece
+    parts = pieces(factor_ref[...].T)
     for k in range(count):
-        mixed_ref[k * rank : (k + 1) * rank] = left_product(
-            factor_ref[...], turn_ref[k * full : (k + 1) * full]
-        )
+        mixed_ref[k * rank : (k + 1) * rank] = stacked(parts, pieces(turn_ref[k * full : (k + 1) * full]))
 
 
 def slab_kernel(right_ref, mixed_ref, slab_ref, turn_ref, own_b):
@@ -291,7 +297,7 @@
 def sum_small(x):
     x = x + swap(x, "row", 1)
     x = tree([x] + [swap(x, "row", m) for m in range(2, lax.axis_size("row"), 2)])
-    return tree([x] + [swap(x, "col", m) for m in range(1, lax.axis_size("col"))])
+    return [x] + [swap(x, "col", m) for m in range(1, lax.axis_size("col"))]
 
 
 def bit(axis, mask):
@@ -375,12 +381,12 @@
         first_kernel,
         "first",
         [(full_one, rank), (rank, full_one), (full_two, full_two)],
-        gram,
+        *gram,
         one,
         contracted,
     )
     basis_two, factor_two = call(
-        second_kernel, "second", [(full_two, rank), (rank, full_two)], sum_small(gram), two
+        second_kernel, "second", [(full_two, rank), (rank, full_two)], *sum_small(gram), two
     )
     count = depth // ways
     (mixed,) = call(

time: 194 us -> 195 us (level)
  starting transfers between devices: 47.5 us -> 49.8 us
  transfers between devices with their start and end apart: 36 -> 36, of which waited for: 24 -> 24; matrix products, arithmetic and copies ran while one was open for 3% -> 2% of each run, Pallas kernels for 13% -> 13%
where the time goes in v4:
time: 195 us
  waiting for transfers between devices  57.5 us (29%)
  Pallas kernels  55.6 us (29%)
  starting transfers between devices  49.8 us (26%)
  blocking collectives  15.6 us (8%)
  local copies, waits for them, and re-layouts  6.76 us (3%)
  other arithmetic  5.44 us (3%)
  matrix products  3.15 us (2%)
    ppermute x34, waiting for transfers between devices, swap(): return lax.ppermute(x, axis, [(i, i ^ mask) for i in range(count)])  53 us
    ppermute x34, starting transfers between devices, swap(): return lax.ppermute(x, axis, [(i, i ^ mask) for i in range(count)])  39.8 us
    pallas_call x6, Pallas kernels, call(): pl.pallas_call(kernel, out_shape=[jax.ShapeDtypeStruct(shape, jnp.float32...  38.4 us
    pallas_call x1, Pallas kernels, swift(): pl.pallas_call(third_kernel, out_shape=[jax.ShapeDtypeStruct((rank, depth...  17.2 us
    all_to_all x1, blocking collectives, swift(): lax.all_to_all(slab, AXES, 0, 0, tiled=True).reshape(depth, own_a * own_b)  15.6 us
    all_to_all x2, starting transfers between devices, trade(): return lax.all_to_all(x.reshape(shape), AXES, 0, 0, tiled=True)  10.1 us
    all_to_all x2, waiting for transfers between devices, trade(): return lax.all_to_all(x.reshape(shape), AXES, 0, 0, tiled=True)  4.51 us
  transfers between devices with their start and end apart: 36, of which 24 were waited for; matrix products, arithmetic and copies ran while one was open for 2% of the time, Pallas kernels for 13%

profile of v4, /device:TPU:0, one launch (start us, length us, event | category | flops | bytes accessed | tf_op | source)
XLA Modules:
  0.0 194.7 jit_solution(11885613016231119506)
XLA Ops:
  0.7 3.2 %fusion = f32[64,512]{1,0:T(8,128)S(1)} fusion(f32[768,64]{0,1:T(8,128)} %param.7, f32[512,768]{1,0:T(8,128)} %bitcast.16), kind=kOutput, calls=%fused_computation.44 | convolution fusion | flops 301989888 | bytes 1900544 | tf_op jit(solution)/shard_map/dot_general | solution.py:37
  4.4 4.7 %collective-permute-start = (f32[32,64]{1,0:T(8,128)S(1)}, f32[32,64]{1,0:T(8,128)S(1)}, u32[]{:S(2)}, u32[]{:S(2)}) collective-permute-start(f32[32,64]{1,0:T(8,128)S(1)} %copy-done.12), channel_id=1, source_target_pairs={{0,3},{1,2},{2,1},{3,0},{4,7},{5,6},{6,5},{7,4},{8,11},{9,10},{10,... | collective-permute-start | bytes 24584 | tf_op jit(solution)/shard_map/ppermute | solution.py:288
  10.4 6.0 %all-to-all-start = ((f32[32,2,512]{2,1,0:T(2,128)}), f32[32,2,512]{2,1,0:T(2,128)S(1)}, u32[]{:S(2)}, u32[]{:S(2)}) async-start(f32[32,2,512]{2,1,0:T(2,128)} %reshape.30), calls=%async_computation | async-start | bytes 262144 | tf_op jit(solution)/shard_map/all_to_all | solution.py:368
  16.5 1.8 collective-permute-start.11
  19.0 1.3 collective-permute-done.11
  20.3 4.5 %all-to-all-done = f32[32,2,512]{2,1,0:T(2,128)S(1)} async-done(((f32[32,2,512]{2,1,0:T(2,128)}), f32[32,2,512]{2,1,0:T(2,128)S(1)}, u32[]{:S(2)}, u32[]{:S(2)}) %all-to-all-start) | async-done | bytes 131104 | tf_op jit(solution)/shard_map/all_to_all | solution.py:368
  26.1 2.2 %open.1 = f32[128,128]{1,0:T(8,128)} custom-call(f32[2,128,128]{2,1,0:T(8,128)} %reshape.32.cont_ref.refs_5_, f32[128,64]{1,0:T(8,128)} %pad_maximum_fusion.4.start_ref.refs_4_), custom_call_target="tpu_custom_call" | custom-call | tf_op jit(solution)/shard_map/open/pallas_call | solution.py:149
  29.2 1.7 copy.14
  30.8 1.3 collective-permute-start.5
  32.9 1.5 collective-permute-start.4
  35.2 2.5 %collective-permute-done.6 = f32[128,128]{1,0:T(8,128)S(1)} collective-permute-done((f32[128,128]{1,0:T(8,128)S(1)}, f32[128,128]{1,0:T(8,128)S(1)}, u32[]{:S(2)}, u32[]{:S(2)}) %collective-permute-start.6) | collective-permute-done | bytes 65568 | tf_op jit(solution)/shard_map/ppermute | solution.py:288
  37.8 1.7 collective-permute-start.8
  39.5 2.7 %collective-permute-start.9 = (f32[128,128]{1,0:T(8,128)S(1)}, f32[128,128]{1,0:T(8,128)S(1)}, u32[]{:S(2)}, u32[]{:S(2)}) collective-permute-start(f32[128,128]{1,0:T(8,128)S(1)} %add_add_fusion.1.refs_0_), channel_id=1, source_target_pairs={{0,3},{1,2},{2,1},{3,0},{4,7},{5,6},{6,5},{7,4},{8,11},{9,10},{10,... | collective-permute-start | bytes 196616 | tf_op jit(solution)/shard_map/ppermute | solution.py:288
  42.8 1.9 collective-permute-done.8.refs_2_
  46.3 4.1 %all-to-all-start.1 = ((f32[32,24,512]{2,1,0:T(8,128)}), f32[32,24,512]{2,1,0:T(8,128)S(1)}, u32[]{:S(2)}, u32[]{:S(2)}) async-start(f32[32,24,512]{2,1,0:T(8,128)} %bitcast.5), calls=%async_computation.1 | async-start | bytes 3145728 | tf_op jit(solution)/shard_map/all_to_all | solution.py:368
  50.4 12.7 %first.1 = (f32[128,64]{1,0:T(8,128)}, f32[64,128]{1,0:T(8,128)}, f32[128,128]{1,0:T(8,128)}) custom-call(f32[128,128]{1,0:T(8,128)} %copy-done.3, f32[128,128]{1,0:T(8,128)} %copy-done.6, f32[128,128]{1,0:T(8,128)} %copy-done.7, f32[128,128]{1,0:T(8,128)} %copy-done.8, f32[128,64]{1,0:T(8,128)} %pad_maximum_fusion.5.refs_4_, ...), custom_call_target="tpu_custom_call" | custom-call | tf_op jit(solution)/shard_map/first/pallas_call | solution.py:149
  63.4 1.2 collective-permute-done.13
  65.5 1.8 collective-permute-start.15
  67.3 1.5 collective-permute-start.16
  69.0 1.4 collective-permute-done.15
  70.4 3.1 %collective-permute-done.16 = f32[128,128]{1,0:T(8,128)S(1)} collective-permute-done((f32[128,128]{1,0:T(8,128)S(1)}, f32[128,128]{1,0:T(8,128)S(1)}, u32[]{:S(2)}, u32[]{:S(2)}) %collective-permute-start.16) | collective-permute-done | bytes 65568 | tf_op jit(solution)/shard_map/ppermute | solution.py:288
  73.5 2.7 %collective-permute-start.17 = (f32[128,128]{1,0:T(8,128)S(1)}, f32[128,128]{1,0:T(8,128)S(1)}, u32[]{:S(2)}, u32[]{:S(2)}) collective-permute-start(f32[128,128]{1,0:T(8,128)S(1)} %add_add_fusion.refs_0_), channel_id=1, source_target_pairs={{0,1},{1,0},{2,3},{3,2},{4,5},{5,4},{6,7},{7,6},{8,9},{9,8},{10,11... | collective-permute-start | bytes 196616 | tf_op jit(solution)/shard_map/ppermute | solution.py:288
  76.2 2.3 %collective-permute-start.18 = (f32[128,128]{1,0:T(8,128)S(1)}, f32[128,128]{1,0:T(8,128)S(1)}, u32[]{:S(2)}, u32[]{:S(2)}) collective-permute-start(f32[128,128]{1,0:T(8,128)S(1)} %add_add_fusion.refs_0_), channel_id=1, source_target_pairs={{0,2},{1,3},{2,0},{3,1},{4,6},{5,7},{6,4},{7,5},{8,10},{9,11},{10,... | collective-permute-start | bytes 196616 | tf_op jit(solution)/shard_map/ppermute | solution.py:288
  78.5 1.4 collective-permute-start.19
  79.9 12.7 %collective-permute-done.18.refs_2_ = f32[128,128]{1,0:T(8,128)S(1)} collective-permute-done((f32[128,128]{1,0:T(8,128)S(1)}, f32[128,128]{1,0:T(8,128)S(1)}, u32[]{:S(2)}, u32[]{:S(2)}) %collective-permute-start.18) | collective-permute-done | bytes 65568 | tf_op jit(solution)/shard_map/ppermute | solution.py:288
  93.9 12.0 %second.1 = (f32[128,64]{1,0:T(8,128)}, f32[64,128]{1,0:T(8,128)}) custom-call(f32[128,128]{1,0:T(8,128)} %copy-done.4, f32[128,128]{1,0:T(8,128)} %copy-done.9, f32[128,128]{1,0:T(8,128)} %copy-done.10, f32[128,128]{1,0:T(8,128)} %copy-done.11, f32[128,64]{1,0:T(8,128)} %pad_maximum_fusion.4.start_ref.refs_4_), custom_call_target="tpu_custom_call" | custom-call | tf_op jit(solution)/shard_map/second/pallas_call | solution.py:149
  107.1 4.7 %mix.1.mixed_ref = f32[1536,128]{1,0:T(8,128)} custom-call(f32[128,64]{1,0:T(8,128)} %get-tuple-element.32.factor_ref, f32[32,24,512]{2,1,0:T(8,128)} %copy-done.1), custom_call_target="tpu_custom_call" | custom-call | tf_op jit(solution)/shard_map/mix/pallas_call | solution.py:149
  111.8 3.3 %slab.1 = f32[32,24,128]{2,1,0:T(8,128)} custom-call(f32[128,64]{1,0:T(8,128)} %get-tuple-element.31.right_ref, f32[1536,128]{1,0:T(8,128)} %mix.1.mixed_ref), custom_call_target="tpu_custom_call" | custom-call | tf_op jit(solution)/shard_map/slab/pallas_call | solution.py:149
  115.2 15.6 %all_to_all.15 = f32[32,24,128]{2,1,0:T(8,128)} all-to-all(f32[32,24,128]{2,1,0:T(8,128)} %slab.1), channel_id=1, replica_groups=mesh['row'=8,'col'=4] {'row','col'}, dimensions={0} | all-to-all | bytes 786432 | tf_op jit(solution)/shard_map/all_to_all | solution.py:409
  130.7 3.4 %pair.1 = f32[2688,128]{1,0:T(8,128)} custom-call(f32[768,128]{1,0:T(8,128)} %bitcast.18), custom_call_target="tpu_custom_call" | custom-call | tf_op jit(solution)/shard_map/pair/pallas_call | solution.py:149
  134.1 1.5 slice_select_fusion
  135.6 1.3 collective-permute-start.20
  136.9 1.8 collective-permute-done.20
  138.8 1.2 collective-permute-start.21
  140.6 4.9 %collective-permute-done.21 = f32[336,128]{1,0:T(8,128)S(1)} collective-permute-done((f32[336,128]{1,0:T(8,128)S(1)}, f32[336,128]{1,0:T(8,128)S(1)}, u32[]{:S(2)}, u32[]{:S(2)}) %collective-permute-start.21) | collective-permute-done | bytes 172064 | tf_op jit(solution)/shard_map/ppermute | solution.py:288
  147.5 1.2 collective-permute-start.22
  148.7 2.4 %collective-permute-done.28 = f32[168,128]{1,0:T(8,128)S(1)} collective-permute-done((f32[168,128]{1,0:T(8,128)S(1)}, f32[168,128]{1,0:T(8,128)S(1)}, u32[]{:S(2)}, u32[]{:S(2)}) %collective-permute-start.28) | collective-permute-done | bytes 86048 | tf_op jit(solution)/shard_map/ppermute | solution.py:288
  152.0 1.2 collective-permute-start.23
  153.3 2.4 %collective-permute-done.29 = f32[168,128]{1,0:T(8,128)S(1)} collective-permute-done((f32[168,128]{1,0:T(8,128)S(1)}, f32[168,128]{1,0:T(8,128)S(1)}, u32[]{:S(2)}, u32[]{:S(2)}) %collective-permute-start.29) | collective-permute-done | bytes 86048 | tf_op jit(solution)/shard_map/ppermute | solution.py:288
  156.7 2.3 %collective-permute-start.24 = (f32[168,128]{1,0:T(8,128)S(1)}, f32[168,128]{1,0:T(8,128)S(1)}, u32[]{:S(2)}, u32[]{:S(2)}) collective-permute-start(f32[168,128]{1,0:T(8,128)S(1)} %add.62), channel_id=1, source_target_pairs={{0,2},{1,3},{2,0},{3,1},{4,6},{5,7},{6,4},{7,5},{8,10},{9,11},{10,... | collective-permute-start | bytes 258056 | tf_op jit(solution)/shard_map/ppermute | solution.py:288
  159.0 3.0 %collective-permute-done.30 = f32[168,128]{1,0:T(8,128)S(1)} collective-permute-done((f32[168,128]{1,0:T(8,128)S(1)}, f32[168,128]{1,0:T(8,128)S(1)}, u32[]{:S(2)}, u32[]{:S(2)}) %collective-permute-start.30) | collective-permute-done | bytes 86048 | tf_op jit(solution)/shard_map/ppermute | solution.py:288
  162.1 1.7 collective-permute-done.24
  164.8 2.3 %collective-permute-done.31 = f32[168,128]{1,0:T(8,128)S(1)} collective-permute-done((f32[168,128]{1,0:T(8,128)S(1)}, f32[168,128]{1,0:T(8,128)S(1)}, u32[]{:S(2)}, u32[]{:S(2)}) %collective-permute-start.31) | collective-permute-done | bytes 86048 | tf_op jit(solution)/shard_map/ppermute | solution.py:288
  168.5 1.3 collective-permute-start.26
  169.8 2.9 %collective-permute-done.32 = f32[336,128]{1,0:T(8,128)S(1)} collective-permute-done((f32[336,128]{1,0:T(8,128)S(1)}, f32[336,128]{1,0:T(8,128)S(1)}, u32[]{:S(2)}, u32[]{:S(2)}) %collective-permute-start.32) | collective-permute-done | bytes 172064 | tf_op jit(solution)/shard_map/ppermute | solution.py:288
  172.7 1.3 collective-permute-done.26
  174.1 2.1 %collective-permute-done.33 = f32[1344,128]{1,0:T(8,128)S(1)} collective-permute-done((f32[1344,128]{1,0:T(8,128)S(1)}, f32[1344,128]{1,0:T(8,128)S(1)}, u32[]{:S(2)}, u32[]{:S(2)}) %collective-permute-start.33) | collective-permute-done | bytes 688160 | tf_op jit(solution)/shard_map/ppermute | solution.py:288
  177.5 17.2 %third.1 = (f32[64,768]{1,0:T(8,128)}, f32[128,64]{1,0:T(8,128)}) custom-call(f32[2688,128]{1,0:T(8,128)} %pad_maximum_fusion.packed_ref, f32[64,768]{1,0:T(8,128)} %bitcast.21, f32[768,128]{1,0:T(8,128)} %bitcast.19), custom_call_target="tpu_custom_call" | custom-call | tf_op jit(solution)/shard_map/third/pallas_call | solution.py:412
  (100 shorter events, 20.9 us)
Async XLA Ops:
  0.6 3.2 %copy-start.13 = (f32[16,64]{1,0:T(8,128)S(1)}, f32[16,64]{1,0:T(8,128)}, u32[]{:S(2)}) copy-start(f32[16,64]{1,0:T(8,128)} %param.5) | copy-start | bytes 12292
  0.6 3.7 %copy-start.12 = (f32[32,64]{1,0:T(8,128)S(1)}, f32[32,64]{1,0:T(8,128)}, u32[]{:S(2)}) copy-start(f32[32,64]{1,0:T(8,128)} %param.6) | copy-start | bytes 24580
  3.8 12.6 %collective-permute-start.10 = (f32[16,64]{1,0:T(8,128)S(1)}, f32[16,64]{1,0:T(8,128)S(1)}, u32[]{:S(2)}, u32[]{:S(2)}) collective-permute-start(f32[16,64]{1,0:T(8,128)S(1)} %copy-done.13), channel_id=1, source_target_pairs={{0,4},{4,0},{8,12},{12,8},{16,20},{20,16},{24,28},{28,24},{1,5},{5... | collective-permute-start | bytes 12296 | tf_op jit(solution)/shard_map/ppermute | solution.py:288
  4.4 13.9 %collective-permute-start = (f32[32,64]{1,0:T(8,128)S(1)}, f32[32,64]{1,0:T(8,128)S(1)}, u32[]{:S(2)}, u32[]{:S(2)}) collective-permute-start(f32[32,64]{1,0:T(8,128)S(1)} %copy-done.12), channel_id=1, source_target_pairs={{0,3},{1,2},{2,1},{3,0},{4,7},{5,6},{6,5},{7,4},{8,11},{9,10},{10,... | collective-permute-start | bytes 24584 | tf_op jit(solution)/shard_map/ppermute | solution.py:288
  9.0 9.3 %collective-permute-start.1 = (f32[32,64]{1,0:T(8,128)S(1)}, f32[32,64]{1,0:T(8,128)S(1)}, u32[]{:S(2)}, u32[]{:S(2)}) collective-permute-start(f32[32,64]{1,0:T(8,128)S(1)} %copy-done.12), channel_id=1, source_target_pairs={{0,2},{1,3},{2,0},{3,1},{4,6},{5,7},{6,4},{7,5},{8,10},{9,11},{10,... | collective-permute-start | bytes 24584 | tf_op jit(solution)/shard_map/ppermute | solution.py:288
  9.0 9.3 %collective-permute-start.2 = (f32[32,64]{1,0:T(8,128)S(1)}, f32[32,64]{1,0:T(8,128)S(1)}, u32[]{:S(2)}, u32[]{:S(2)}) collective-permute-start(f32[32,64]{1,0:T(8,128)S(1)} %copy-done.12), channel_id=1, source_target_pairs={{0,1},{1,0},{2,3},{3,2},{4,5},{5,4},{6,7},{7,6},{8,9},{9,8},{10,11... | collective-permute-start | bytes 24584 | tf_op jit(solution)/shard_map/ppermute | solution.py:288
  10.4 14.4 %all-to-all-start = ((f32[32,2,512]{2,1,0:T(2,128)}), f32[32,2,512]{2,1,0:T(2,128)S(1)}, u32[]{:S(2)}, u32[]{:S(2)}) async-start(f32[32,2,512]{2,1,0:T(2,128)} %reshape.30), calls=%async_computation | async-start | bytes 262144 | tf_op jit(solution)/shard_map/all_to_all | solution.py:368
  16.5 3.8 %collective-permute-start.11 = (f32[32,64]{1,0:T(8,128)S(1)}, f32[32,64]{1,0:T(8,128)S(1)}, u32[]{:S(2)}, u32[]{:S(2)}) collective-permute-start(f32[32,64]{1,0:T(8,128)S(1)} %pad_maximum_fusion.7), channel_id=1, source_target_pairs={{0,8},{4,12},{8,0},{12,4},{16,24},{20,28},{24,16},{28,20},{1,9},{5... | collective-permute-start | bytes 24584 | tf_op jit(solution)/shard_map/ppermute | solution.py:288
  24.8 4.3 %copy-start.2 = (f32[16,32,768]{2,1,0:T(8,128)S(1)}, f32[16,32,768]{2,1,0:T(8,128)}, u32[]{:S(2)}) copy-start(f32[16,32,768]{2,1,0:T(8,128)} %param.4) | copy-start | bytes 4718596
  28.3 2.5 %collective-permute-start.3 = (f32[128,128]{1,0:T(8,128)}, f32[128,128]{1,0:T(8,128)S(1)}, u32[]{:S(2)}, u32[]{:S(2)}) collective-permute-start(f32[128,128]{1,0:T(8,128)} %open.1), channel_id=1, source_target_pairs={{0,4},{4,0},{8,12},{12,8},{16,20},{20,16},{24,28},{28,24},{1,5},{5... | collective-permute-start | bytes 196616 | tf_op jit(solution)/shard_map/ppermute | solution.py:288
  28.3 2.5 %copy-start.5 = (f32[128,128]{1,0:T(8,128)S(1)}, f32[128,128]{1,0:T(8,128)}, u32[]{:S(2)}) copy-start(f32[128,128]{1,0:T(8,128)} %open.1) | copy-start | bytes 196612
  28.3 6.1 %collective-permute-start.12 = (f32[64,64]{1,0:T(8,128)S(1)}, f32[64,64]{1,0:T(8,128)S(1)}, u32[]{:S(2)}, u32[]{:S(2)}) collective-permute-start(f32[64,64]{1,0:T(8,128)S(1)} %pad_maximum_fusion.6), channel_id=1, source_target_pairs={{0,16},{4,20},{8,24},{12,28},{16,0},{20,4},{24,8},{28,12},{1,17},{... | collective-permute-start | bytes 49160 | tf_op jit(solution)/shard_map/ppermute | solution.py:288
  30.8 4.3 %collective-permute-start.5 = (f32[128,128]{1,0:T(8,128)S(1)}, f32[128,128]{1,0:T(8,128)S(1)}, u32[]{:S(2)}, u32[]{:S(2)}) collective-permute-start(f32[128,128]{1,0:T(8,128)S(1)} %add.51), channel_id=1, source_target_pairs={{0,16},{4,20},{8,24},{12,28},{16,0},{20,4},{24,8},{28,12},{1,17},{... | collective-permute-start | bytes 196616 | tf_op jit(solution)/shard_map/ppermute | solution.py:288
  32.1 5.5 %collective-permute-start.6 = (f32[128,128]{1,0:T(8,128)S(1)}, f32[128,128]{1,0:T(8,128)S(1)}, u32[]{:S(2)}, u32[]{:S(2)}) collective-permute-start(f32[128,128]{1,0:T(8,128)S(1)} %add.51), channel_id=1, source_target_pairs={{0,24},{4,28},{8,16},{12,20},{16,8},{20,12},{24,0},{28,4},{1,25},{... | collective-permute-start | bytes 196616 | tf_op jit(solution)/shard_map/ppermute | solution.py:288
  32.9 4.8 %collective-permute-start.4 = (f32[128,128]{1,0:T(8,128)S(1)}, f32[128,128]{1,0:T(8,128)S(1)}, u32[]{:S(2)}, u32[]{:S(2)}) collective-permute-start(f32[128,128]{1,0:T(8,128)S(1)} %add.51), channel_id=1, source_target_pairs={{0,8},{4,12},{8,0},{12,4},{16,24},{20,28},{24,16},{28,20},{1,9},{5... | collective-permute-start | bytes 196616 | tf_op jit(solution)/shard_map/ppermute | solution.py:288
  37.7 8.0 %copy-start.3 = (f32[128,128]{1,0:T(8,128)}, f32[128,128]{1,0:T(8,128)S(1)}, u32[]{:S(2)}) copy-start(f32[128,128]{1,0:T(8,128)S(1)} %add_add_fusion.1.refs_0_) | copy-start | bytes 196612
  37.7 5.1 %collective-permute-start.7 = (f32[128,128]{1,0:T(8,128)S(1)}, f32[128,128]{1,0:T(8,128)S(1)}, u32[]{:S(2)}, u32[]{:S(2)}) collective-permute-start(f32[128,128]{1,0:T(8,128)S(1)} %add_add_fusion.1.refs_0_), channel_id=1, source_target_pairs={{0,1},{1,0},{2,3},{3,2},{4,5},{5,4},{6,7},{7,6},{8,9},{9,8},{10,11... | collective-permute-start | bytes 196616 | tf_op jit(solution)/shard_map/ppermute | solution.py:288
  37.8 6.9 %collective-permute-start.8 = (f32[128,128]{1,0:T(8,128)S(1)}, f32[128,128]{1,0:T(8,128)S(1)}, u32[]{:S(2)}, u32[]{:S(2)}) collective-permute-start(f32[128,128]{1,0:T(8,128)S(1)} %add_add_fusion.1.refs_0_), channel_id=1, source_target_pairs={{0,2},{1,3},{2,0},{3,1},{4,6},{5,7},{6,4},{7,5},{8,10},{9,11},{10,... | collective-permute-start | bytes 196616 | tf_op jit(solution)/shard_map/ppermute | solution.py:288
  39.5 6.2 %collective-permute-start.9 = (f32[128,128]{1,0:T(8,128)S(1)}, f32[128,128]{1,0:T(8,128)S(1)}, u32[]{:S(2)}, u32[]{:S(2)}) collective-permute-start(f32[128,128]{1,0:T(8,128)S(1)} %add_add_fusion.1.refs_0_), channel_id=1, source_target_pairs={{0,3},{1,2},{2,1},{3,0},{4,7},{5,6},{6,5},{7,4},{8,11},{9,10},{10,... | collective-permute-start | bytes 196616 | tf_op jit(solution)/shard_map/ppermute | solution.py:288
  42.8 2.9 %copy-start.6 = (f32[128,128]{1,0:T(8,128)}, f32[128,128]{1,0:T(8,128)S(1)}, u32[]{:S(2)}) copy-start(f32[128,128]{1,0:T(8,128)S(1)} %collective-permute-done.7.refs_1_) | copy-start | bytes 196612
  44.7 1.0 copy-start.7
  46.3 59.6 %all-to-all-start.1 = ((f32[32,24,512]{2,1,0:T(8,128)}), f32[32,24,512]{2,1,0:T(8,128)S(1)}, u32[]{:S(2)}, u32[]{:S(2)}) async-start(f32[32,24,512]{2,1,0:T(8,128)} %bitcast.5), calls=%async_computation.1 | async-start | bytes 3145728 | tf_op jit(solution)/shard_map/all_to_all | solution.py:368
  63.1 1.5 collective-permute-start.13
  65.5 5.0 %collective-permute-start.15 = (f32[128,128]{1,0:T(8,128)S(1)}, f32[128,128]{1,0:T(8,128)S(1)}, u32[]{:S(2)}, u32[]{:S(2)}) collective-permute-start(f32[128,128]{1,0:T(8,128)S(1)} %add.55), channel_id=1, source_target_pairs={{0,16},{4,20},{8,24},{12,28},{16,0},{20,4},{24,8},{28,12},{1,17},{... | collective-permute-start | bytes 196616 | tf_op jit(solution)/shard_map/ppermute | solution.py:288
  67.3 6.2 %collective-permute-start.16 = (f32[128,128]{1,0:T(8,128)S(1)}, f32[128,128]{1,0:T(8,128)S(1)}, u32[]{:S(2)}, u32[]{:S(2)}) collective-permute-start(f32[128,128]{1,0:T(8,128)S(1)} %add.55), channel_id=1, source_target_pairs={{0,24},{4,28},{8,16},{12,20},{16,8},{20,12},{24,0},{28,4},{1,25},{... | collective-permute-start | bytes 196616 | tf_op jit(solution)/shard_map/ppermute | solution.py:288
  68.7 4.7 %collective-permute-start.14 = (f32[128,128]{1,0:T(8,128)S(1)}, f32[128,128]{1,0:T(8,128)S(1)}, u32[]{:S(2)}, u32[]{:S(2)}) collective-permute-start(f32[128,128]{1,0:T(8,128)S(1)} %add.55), channel_id=1, source_target_pairs={{0,8},{4,12},{8,0},{12,4},{16,24},{20,28},{24,16},{28,20},{1,9},{5... | collective-permute-start | bytes 196616 | tf_op jit(solution)/shard_map/ppermute | solution.py:288
  73.5 19.1 %copy-start.4 = (f32[128,128]{1,0:T(8,128)}, f32[128,128]{1,0:T(8,128)S(1)}, u32[]{:S(2)}) copy-start(f32[128,128]{1,0:T(8,128)S(1)} %add_add_fusion.refs_0_) | copy-start | bytes 196612
  73.5 6.4 %collective-permute-start.17 = (f32[128,128]{1,0:T(8,128)S(1)}, f32[128,128]{1,0:T(8,128)S(1)}, u32[]{:S(2)}, u32[]{:S(2)}) collective-permute-start(f32[128,128]{1,0:T(8,128)S(1)} %add_add_fusion.refs_0_), channel_id=1, source_target_pairs={{0,1},{1,0},{2,3},{3,2},{4,5},{5,4},{6,7},{7,6},{8,9},{9,8},{10,11... | collective-permute-start | bytes 196616 | tf_op jit(solution)/shard_map/ppermute | solution.py:288
  76.2 16.4 %collective-permute-start.18 = (f32[128,128]{1,0:T(8,128)S(1)}, f32[128,128]{1,0:T(8,128)S(1)}, u32[]{:S(2)}, u32[]{:S(2)}) collective-permute-start(f32[128,128]{1,0:T(8,128)S(1)} %add_add_fusion.refs_0_), channel_id=1, source_target_pairs={{0,2},{1,3},{2,0},{3,1},{4,6},{5,7},{6,4},{7,5},{8,10},{9,11},{10,... | collective-permute-start | bytes 196616 | tf_op jit(solution)/shard_map/ppermute | solution.py:288
  78.5 14.1 %collective-permute-start.19 = (f32[128,128]{1,0:T(8,128)S(1)}, f32[128,128]{1,0:T(8,128)S(1)}, u32[]{:S(2)}, u32[]{:S(2)}) collective-permute-start(f32[128,128]{1,0:T(8,128)S(1)} %add_add_fusion.refs_0_), channel_id=1, source_target_pairs={{0,3},{1,2},{2,1},{3,0},{4,7},{5,6},{6,5},{7,4},{8,11},{9,10},{10,... | collective-permute-start | bytes 196616 | tf_op jit(solution)/shard_map/ppermute | solution.py:288
  79.9 12.7 %copy-start.9 = (f32[128,128]{1,0:T(8,128)}, f32[128,128]{1,0:T(8,128)S(1)}, u32[]{:S(2)}) copy-start(f32[128,128]{1,0:T(8,128)S(1)} %collective-permute-done.17.refs_1_) | copy-start | bytes 196612
  93.2 0.6 copy-start.11
  105.9 1.2 copy-start.1
  134.1 4.5 %copy-start = (f32[2688,128]{1,0:T(8,128)S(1)}, f32[2688,128]{1,0:T(8,128)}, u32[]{:S(2)}) copy-start(f32[2688,128]{1,0:T(8,128)} %pair.1) | copy-start | bytes 4128772
  135.6 3.1 %collective-permute-start.20 = (f32[1344,128]{1,0:T(8,128)S(1)}, f32[1344,128]{1,0:T(8,128)S(1)}, u32[]{:S(2)}, u32[]{:S(2)}) collective-permute-start(f32[1344,128]{1,0:T(8,128)S(1)} %slice_select_fusion), channel_id=1, source_target_pairs={{0,4},{4,0},{8,12},{12,8},{16,20},{20,16},{24,28},{28,24},{1,5},{5... | collective-permute-start | bytes 2064392 | tf_op jit(solution)/shard_map/ppermute | solution.py:288
  138.8 6.7 %collective-permute-start.21 = (f32[336,128]{1,0:T(8,128)S(1)}, f32[336,128]{1,0:T(8,128)S(1)}, u32[]{:S(2)}, u32[]{:S(2)}) collective-permute-start(f32[336,128]{1,0:T(8,128)S(1)} %get-tuple-element.40), channel_id=1, source_target_pairs={{0,8},{4,12},{8,0},{12,4},{16,24},{20,28},{24,16},{28,20},{1,9},{5... | collective-permute-start | bytes 516104 | tf_op jit(solution)/shard_map/ppermute | solution.py:288
  140.1 6.4 %collective-permute-start.27 = (f32[336,128]{1,0:T(8,128)S(1)}, f32[336,128]{1,0:T(8,128)S(1)}, u32[]{:S(2)}, u32[]{:S(2)}) collective-permute-start(f32[336,128]{1,0:T(8,128)S(1)} %get-tuple-element.41), channel_id=1, source_target_pairs={{0,16},{4,20},{8,24},{12,28},{16,0},{20,4},{24,8},{28,12},{1,17},{... | collective-permute-start | bytes 516104 | tf_op jit(solution)/shard_map/ppermute | solution.py:288
  146.5 4.6 %collective-permute-start.28 = (f32[168,128]{1,0:T(8,128)S(1)}, f32[168,128]{1,0:T(8,128)S(1)}, u32[]{:S(2)}, u32[]{:S(2)}) collective-permute-start(f32[168,128]{1,0:T(8,128)S(1)} %slice_select_fusion.3), channel_id=1, source_target_pairs={{0,8},{4,12},{8,0},{12,4},{16,24},{20,28},{24,16},{28,20},{1,9},{5... | collective-permute-start | bytes 258056 | tf_op jit(solution)/shard_map/ppermute | solution.py:288
  147.5 4.6 %collective-permute-start.22 = (f32[168,128]{1,0:T(8,128)S(1)}, f32[168,128]{1,0:T(8,128)S(1)}, u32[]{:S(2)}, u32[]{:S(2)}) collective-permute-start(f32[168,128]{1,0:T(8,128)S(1)} %slice_select_fusion.4), channel_id=1, source_target_pairs={{0,16},{4,20},{8,24},{12,28},{16,0},{20,4},{24,8},{28,12},{1,17},{... | collective-permute-start | bytes 258056 | tf_op jit(solution)/shard_map/ppermute | solution.py:288
  151.1 4.5 %collective-permute-start.29 = (f32[168,128]{1,0:T(8,128)S(1)}, f32[168,128]{1,0:T(8,128)S(1)}, u32[]{:S(2)}, u32[]{:S(2)}) collective-permute-start(f32[168,128]{1,0:T(8,128)S(1)} %select_add_fusion.3), channel_id=1, source_target_pairs={{0,1},{1,0},{2,3},{3,2},{4,5},{5,4},{6,7},{7,6},{8,9},{9,8},{10,11... | collective-permute-start | bytes 258056 | tf_op jit(solution)/shard_map/ppermute | solution.py:288
  152.0 4.7 %collective-permute-start.23 = (f32[168,128]{1,0:T(8,128)S(1)}, f32[168,128]{1,0:T(8,128)S(1)}, u32[]{:S(2)}, u32[]{:S(2)}) collective-permute-start(f32[168,128]{1,0:T(8,128)S(1)} %select_add_fusion.4), channel_id=1, source_target_pairs={{0,1},{1,0},{2,3},{3,2},{4,5},{5,4},{6,7},{7,6},{8,9},{9,8},{10,11... | collective-permute-start | bytes 258056 | tf_op jit(solution)/shard_map/ppermute | solution.py:288
  155.7 6.4 %collective-permute-start.30 = (f32[168,128]{1,0:T(8,128)S(1)}, f32[168,128]{1,0:T(8,128)S(1)}, u32[]{:S(2)}, u32[]{:S(2)}) collective-permute-start(f32[168,128]{1,0:T(8,128)S(1)} %add.66), channel_id=1, source_target_pairs={{0,2},{1,3},{2,0},{3,1},{4,6},{5,7},{6,4},{7,5},{8,10},{9,11},{10,... | collective-permute-start | bytes 258056 | tf_op jit(solution)/shard_map/ppermute | solution.py:288
  156.7 7.2 %collective-permute-start.24 = (f32[168,128]{1,0:T(8,128)S(1)}, f32[168,128]{1,0:T(8,128)S(1)}, u32[]{:S(2)}, u32[]{:S(2)}) collective-permute-start(f32[168,128]{1,0:T(8,128)S(1)} %add.62), channel_id=1, source_target_pairs={{0,2},{1,3},{2,0},{3,1},{4,6},{5,7},{6,4},{7,5},{8,10},{9,11},{10,... | collective-permute-start | bytes 258056 | tf_op jit(solution)/shard_map/ppermute | solution.py:288
  162.1 5.1 %collective-permute-start.31 = (f32[168,128]{1,0:T(8,128)S(1)}, f32[168,128]{1,0:T(8,128)S(1)}, u32[]{:S(2)}, u32[]{:S(2)}) collective-permute-start(f32[168,128]{1,0:T(8,128)S(1)} %add.67), channel_id=1, source_target_pairs={{0,8},{4,12},{8,0},{12,4},{16,24},{20,28},{24,16},{28,20},{1,9},{5... | collective-permute-start | bytes 258056 | tf_op jit(solution)/shard_map/ppermute | solution.py:288
  163.9 4.6 %collective-permute-start.25 = (f32[168,128]{1,0:T(8,128)S(1)}, f32[168,128]{1,0:T(8,128)S(1)}, u32[]{:S(2)}, u32[]{:S(2)}) collective-permute-start(f32[168,128]{1,0:T(8,128)S(1)} %add.63), channel_id=1, source_target_pairs={{0,16},{4,20},{8,24},{12,28},{16,0},{20,4},{24,8},{28,12},{1,17},{... | collective-permute-start | bytes 258056 | tf_op jit(solution)/shard_map/ppermute | solution.py:288
  167.2 5.5 %collective-permute-start.32 = (f32[336,128]{1,0:T(8,128)S(1)}, f32[336,128]{1,0:T(8,128)S(1)}, u32[]{:S(2)}, u32[]{:S(2)}) collective-permute-start(f32[336,128]{1,0:T(8,128)S(1)} %pad_maximum_fusion.3), channel_id=1, source_target_pairs={{0,16},{4,20},{8,24},{12,28},{16,0},{20,4},{24,8},{28,12},{1,17},{... | collective-permute-start | bytes 516104 | tf_op jit(solution)/shard_map/ppermute | solution.py:288
  168.5 5.5 %collective-permute-start.26 = (f32[336,128]{1,0:T(8,128)S(1)}, f32[336,128]{1,0:T(8,128)S(1)}, u32[]{:S(2)}, u32[]{:S(2)}) collective-permute-start(f32[336,128]{1,0:T(8,128)S(1)} %pad_maximum_fusion.2), channel_id=1, source_target_pairs={{0,8},{4,12},{8,0},{12,4},{16,24},{20,28},{24,16},{28,20},{1,9},{5... | collective-permute-start | bytes 516104 | tf_op jit(solution)/shard_map/ppermute | solution.py:288
  174.0 2.2 %collective-permute-start.33 = (f32[1344,128]{1,0:T(8,128)S(1)}, f32[1344,128]{1,0:T(8,128)S(1)}, u32[]{:S(2)}, u32[]{:S(2)}) collective-permute-start(f32[1344,128]{1,0:T(8,128)S(1)} %pad_maximum_fusion.1), channel_id=1, source_target_pairs={{0,4},{4,0},{8,12},{12,8},{16,20},{20,16},{24,28},{28,24},{1,5},{5... | collective-permute-start | bytes 2064392 | tf_op jit(solution)/shard_map/ppermute | solution.py:288
  (2 other events, 1.2 us)
